TPU v7x, 128 devices: a whole 4x4x4 slice. The times are simulated.
128 devices in a mesh: cls: 128 (over y, x, z, core).
Axes of the slice: x: 4, y: 4, z: 4, core: 2. Of those that a mesh axis runs over, the one named last changes fastest.
Arguments:
- features: bfloat16 [2048, 12544], P('cls'), may hold values from -6 to 6
- fc_weight: bfloat16 [12544, 512], replicated, may hold values from -0.0546875 to 0.0546875
- centers: bfloat16 [524288, 512], P('cls'), may hold values from -6 to 6
- labels: int32 [2048], replicated, may hold values from 0 to 524287
Outputs:
- loss: float32 [2048], P('cls')
- grad_centers: bfloat16 [524288, 512], P('cls')
- grad_fc: float32 [12544, 512], P('cls')
All inputs are finite; a program needn't handle non-finite values.
Results may differ from a plain program's by a relative error of at most 0.0078.
Values may be sent and summed in bfloat16 or wider, within the bound.
No kernel may reach another device: no remote copies, remote signals or barrier semaphores. Data moves between devices by JAX's collectives and lax.ppermute only.
A program may use at most 128 MiB of HBM per device.

v0:
```python
import math

import jax
import jax.numpy as jnp
from jax import lax
from jax.sharding import Mesh
from jax.sharding import PartitionSpec as P

CLS = ("cls_0", "cls_1", "cls_2", "cls_3")


logit_scale = 64.0
cos_margin = math.cos(0.5)
sin_margin = math.sin(0.5)
epsilon = 1e-06


def from_everyone(x, axis):
    copies = jnp.broadcast_to(x, (lax.axis_size(axis), *x.shape))
    return lax.all_to_all(copies, axis, split_axis=0, concat_axis=0, tiled=True)


def joined_along(tiles, dim):
    shape = list(tiles.shape[1:])
    shape[dim] *= tiles.shape[0]
    return jnp.moveaxis(tiles, 0, dim).reshape(shape)


def gathered_by_axis(x, axes, dim):
    far, near = axes
    tiles = from_everyone(from_everyone(x, far), near)
    return joined_along(tiles.swapaxes(0, 1).reshape(-1, *x.shape), dim)


def of_everyone(x, axis):
    return from_everyone(x, axis).sum(axis=0)


def by_axis(x, axes):
    far, near = axes
    return of_everyone(of_everyone(x, near), far)


def in_one(arrays, axis):
    ends = [0]
    for a in arrays:
        ends.append(ends[-1] + a.size)
    subtotal = by_axis(jnp.concatenate([a.ravel() for a in arrays]), axis)
    return tuple((subtotal[b:e].reshape(a.shape) for a, b, e in zip(arrays, ends, ends[1:])))


def cut_along(x, dim, peers):
    shape = x.shape
    tiles = x.reshape(*shape[:dim], peers, shape[dim] // peers, *shape[dim + 1 :])
    return jnp.moveaxis(tiles, dim, 0)


def summed_on_arrival(x, axis, dim):
    peers = lax.axis_size(axis)
    tiles = lax.all_to_all(cut_along(x, dim, peers), axis, 0, 0, tiled=True)
    return jnp.sum(tiles.astype(jnp.float32), axis=0)


def sum_by_axis(x, axes, dim):
    far, near = axes
    own = summed_on_arrival(cut_along(x, dim, lax.axis_size(far)), near, dim + 1)
    return jnp.sum(
        lax.all_to_all(own.astype(jnp.bfloat16), far, 0, 0, tiled=True).astype(jnp.float32), axis=0
    )


def inverse_norm(values):
    return lax.rsqrt(jnp.sum(values * values, axis=1, keepdims=True) + epsilon)


def margin_logits(emb_low, center_low, labels, offset):
    cosines = lax.dot_general(
        emb_low, center_low, (((1,), (1,)), ((), ())), preferred_element_type=jnp.float32
    )
    local_ids = labels - offset
    is_target = local_ids[:, None] == lax.broadcasted_iota(jnp.int32, (1, center_low.shape[0]), 1)
    target_cos = jnp.sum(jnp.where(is_target, cosines, 0.0), axis=1)
    target_sine = jnp.sqrt(1.0 - target_cos * target_cos)
    margined = target_cos * cos_margin - target_sine * sin_margin
    logits = logit_scale * jnp.where(is_target, margined[:, None], cosines)
    slope = cos_margin + sin_margin * target_cos / target_sine
    return (logits, is_target, slope)


def on_device(features, fc_weight, centers, labels):
    tok_rows = features.shape[0]
    class_rows = centers.shape[0]
    my_index = lax.axis_index(CLS)
    columns = lax.all_to_all(features, CLS, split_axis=1, concat_axis=0, tiled=True)
    embedded = jnp.dot(features, fc_weight, preferred_element_type=jnp.float32).astype(jnp.bfloat16)
    gathered = gathered_by_axis(embedded, (("cls_0", "cls_1", "cls_2"), "cls_3"), 0)
    all_float = gathered.astype(jnp.float32)
    emb_low = (all_float * inverse_norm(all_float)).astype(jnp.bfloat16)
    own_float = embedded.astype(jnp.float32)
    inv_emb = inverse_norm(own_float)
    emb_dir = own_float * inv_emb
    center_float = centers.astype(jnp.float32)
    inv_center = inverse_norm(center_float)
    center_dir = center_float * inv_center
    center_low = center_dir.astype(jnp.bfloat16)
    logits, is_target, slope = margin_logits(emb_low, center_low, labels, my_index * class_rows)
    target_logit = jnp.sum(jnp.where(is_target, logits, 0.0), axis=1)
    row_total, target_all = in_one(
        (jnp.sum(jnp.exp(logits - logit_scale), axis=1), target_logit),
        (("cls_0", "cls_1"), ("cls_2", "cls_3")),
    )
    log_total = logit_scale + jnp.log(row_total)
    loss = lax.dynamic_slice_in_dim(log_total - target_all, my_index * tok_rows, tok_rows)
    probs = jnp.exp(logits - log_total[:, None])
    grad_cos = (
        logit_scale
        * (probs - is_target.astype(jnp.float32))
        * jnp.where(is_target, slope[:, None], 1.0)
    ).astype(jnp.bfloat16)
    grad_unit = lax.dot_general(
        grad_cos, emb_low, (((0,), (0,)), ((), ())), preferred_element_type=jnp.float32
    )
    grad_centers = (
        (grad_unit - center_dir * jnp.sum(grad_unit * center_dir, axis=1, keepdims=True))
        * inv_center
    ).astype(jnp.bfloat16)
    grad_dir = sum_by_axis(
        jnp.dot(grad_cos, center_low, preferred_element_type=jnp.float32).astype(jnp.bfloat16),
        (("cls_0", "cls_1", "cls_2"), "cls_3"),
        0,
    )
    grad_emb = (
        (grad_dir - emb_dir * jnp.sum(grad_dir * emb_dir, axis=1, keepdims=True)) * inv_emb
    ).astype(jnp.bfloat16)
    all_grads = gathered_by_axis(grad_emb, (("cls_0", "cls_1", "cls_2"), "cls_3"), 0)
    grad_fc = lax.dot_general(
        columns, all_grads, (((0,), (0,)), ((), ())), preferred_element_type=jnp.float32
    )
    return (loss, grad_centers, grad_fc)


def solution(mesh):
    torus = Mesh(mesh.devices.reshape(4, 4, 4, 2), ("cls_0", "cls_1", "cls_2", "cls_3"))
    placed = (P(CLS, None), P(), P(CLS, None), P())
    return jax.shard_map(
        on_device,
        mesh=torus,
        in_specs=placed,
        out_specs=(P(CLS), P(CLS, None), P(CLS, None)),
        check_vma=False,
    )
```

profile of v0, /device:TPU:1, one launch (start us, length us, event | category | flops | bytes accessed | tf_op | source)
XLA Modules:
  0.0 228.6 jit_solution(8247104401457302656)
XLA Ops:
  0.6 7.2 %fusion.22 = (f32[16]{0:T(128)}, bf16[16,512]{1,0:T(8,128)(2,1)S(1)}) fusion(bf16[16,12544]{1,0:T(8,128)(2,1)} %param.4, bf16[12544,512]{1,0:T(8,128)(2,1)} %param.5), kind=kOutput, calls=%fused_computation.36 | convolution fusion | flops 205553648 | bytes 13262912 | tf_op jit(solution)/shard_map/dot_general | solution.py:95
  7.8 1.1 broadcast_in_dim.52
  8.9 12.0 %all-to-all-start = ((bf16[64,16,512]{2,1,0:T(8,128)(2,1)}), bf16[64,16,512]{2,1,0:T(8,128)(2,1)S(1)}, u32[]{:S(2)}, u32[]{:S(2)}) async-start(bf16[64,16,512]{2,1,0:T(8,128)(2,1)} %broadcast_in_dim.52), calls=%async_computation | async-start | bytes 2097152 | tf_op jit(solution)/shard_map/all_to_all | solution.py:20
  20.9 6.3 %copy.25 = bf16[4096,512]{0,1:T(8,128)(2,1)} copy(bf16[4096,512]{1,0:T(8,128)(2,1)} %param.6) | data formatting | bytes 8388608 | tf_op args[2]
  27.2 3.1 %fusion.7 = f32[4096]{0:T(1024)S(1)} fusion(bf16[4096,512]{0,1:T(8,128)(2,1)} %copy.25), kind=kLoop, calls=%fused_computation.15 | loop fusion | flops 6287360 | bytes 4210688 | tf_op jit(solution)/shard_map/reduce_sum | solution.py:73
  30.3 7.9 %all-to-all-done = bf16[64,16,512]{2,1,0:T(8,128)(2,1)S(1)} async-done(((bf16[64,16,512]{2,1,0:T(8,128)(2,1)}), bf16[64,16,512]{2,1,0:T(8,128)(2,1)S(1)}, u32[]{:S(2)}, u32[]{:S(2)}) %all-to-all-start) | async-done | bytes 1048608 | tf_op jit(solution)/shard_map/all_to_all | solution.py:20
  38.2 0.3 broadcast_in_dim.53
  38.5 7.4 %all_to_all.61 = bf16[2,64,16,512]{3,2,1,0:T(8,128)(2,1)S(1)} all-to-all(bf16[2,64,16,512]{3,2,1,0:T(8,128)(2,1)S(1)} %broadcast_in_dim.53), channel_id=1, replica_groups=mesh['cls_0'=4,'cls_1'=4,'cls_2'=4,'cls_3'=2] {'cls_3'}, dimensions={0} | all-to-all | bytes 4194304 | tf_op jit(solution)/shard_map/all_to_all | solution.py:20
  45.9 0.5 multiply_reduce_fusion
  46.5 0.1 rsqrt.32
  46.6 0.6 copy_convert_fusion
  47.2 0.3 fusion.8
  47.6 1.2 copy-done
  48.8 15.6 %select_reduce_fusion.1 = (f32[2048]{0:T(1024)S(1)}, f32[2048,4096]{1,0:T(8,128)}) fusion(s32[2048]{0:T(1024)S(1)} %broadcast_subtract_fusion, bf16[2048,512]{1,0:T(8,128)(2,1)S(1)} %fusion.8, bf16[4096,512]{0,1:T(8,128)(2,1)S(1)} %copy-done, f32[4096]{0:T(1024)S(1)} %add_rsqrt_fusion), kind=kOutput, calls=%fused_computation.4 | convolution fusion | flops 8621389824 | bytes 39878656 | tf_op jit(solution)/shard_map/dot_general | solution.py:77
  64.3 0.6 multiply_add_fusion
  65.0 18.9 %exponential_reduce_fusion = (f32[2048]{0:T(1024)S(1)}, f32[2048]{0:T(1024)S(1)}) fusion(f32[2048,4096]{1,0:T(8,128)} %get-tuple-element.25, f32[2048]{0:T(1024)S(1)} %get-tuple-element.23, s32[2048]{0:T(1024)S(1)} %broadcast_subtract_fusion), kind=kLoop, calls=%fused_computation.2 | loop fusion | flops 58716160 | bytes 33587200 | tf_op jit(solution)/shard_map/reduce_sum | solution.py:109
  83.8 0.1 broadcast_in_dim.56
  83.9 8.0 %all_to_all.62 = f32[8,1,4096]{2,1,0:T(1,128)S(1)} all-to-all(f32[8,1,4096]{2,1,0:T(1,128)S(1)} %broadcast_in_dim.56), channel_id=1, replica_groups=mesh['cls_0'=4,'cls_1'=4,'cls_2'=4,'cls_3'=2] {'cls_2','cls_3'}, dimensions={0} | all-to-all | bytes 262144 | tf_op jit(solution)/shard_map/all_to_all | solution.py:20
  91.9 0.1 reduce_sum.116
  92.0 0.2 broadcast_in_dim.57
  92.2 10.1 %all_to_all.63 = f32[16,1,4096]{2,1,0:T(1,128)S(1)} all-to-all(f32[16,1,4096]{2,1,0:T(1,128)S(1)} %broadcast_in_dim.57), channel_id=1, replica_groups=mesh['cls_0'=4,'cls_1'=4,'cls_2'=4,'cls_3'=2] {'cls_0','cls_1'}, dimensions={0} | all-to-all | bytes 524288 | tf_op jit(solution)/shard_map/all_to_all | solution.py:20
  102.4 0.2 reduce_sum.117
  102.5 0.6 fusion.23
  103.1 20.8 %multiply_convert_fusion = bf16[2048,4096]{1,0:T(8,128)(2,1)S(1)} fusion(f32[2048,4096]{1,0:T(8,128)} %get-tuple-element.25, f32[2048]{0:T(1024)} %get-tuple-element.22, f32[2048]{0:T(1024)S(1)} %get-tuple-element.20, f32[2048]{0:T(1024)S(1)} %get-tuple-element.23, s32[2048]{0:T(1024)S(1)} %broadcast_subtract_fusion), kind=kLoop, calls=%fused_computation | loop fusion | flops 83886080 | bytes 50364416 | tf_op jit(solution)/shard_map/convert_element_type | solution.py:119
  124.0 11.7 %fusion.13 = bf16[2048,512]{1,0:T(8,128)(2,1)} fusion(bf16[2048,4096]{1,0:T(8,128)(2,1)S(1)} %multiply_convert_fusion, bf16[4096,512]{0,1:T(8,128)(2,1)S(1)} %copy-done.1, f32[4096]{0:T(1024)} %copy-done.5), kind=kOutput, calls=%fused_computation.21 | convolution fusion | flops 8597274624 | bytes 23085056 | tf_op jit(solution)/shard_map/dot_general | solution.py:128
  135.7 1.8 copy.40
  137.5 0.0 copy-start.6
  137.5 7.3 %all_to_all.64 = bf16[2,64,16,512]{3,2,1,0:T(8,128)(2,1)S(1)} all-to-all(bf16[2,64,16,512]{3,2,1,0:T(8,128)(2,1)S(1)} %bitcast.29), channel_id=1, replica_groups=mesh['cls_0'=4,'cls_1'=4,'cls_2'=4,'cls_3'=2] {'cls_3'}, dimensions={0} | all-to-all | bytes 4194304 | tf_op jit(solution)/shard_map/all_to_all | solution.py:60
  144.8 1.7 reduce_sum.119
  146.5 4.7 %all-to-all-start.5 = ((bf16[64,16,512]{2,1,0:T(8,128)(2,1)}), bf16[64,16,512]{2,1,0:T(8,128)(2,1)S(1)}, u32[]{:S(2)}, u32[]{:S(2)}) async-start(bf16[64,16,512]{2,1,0:T(8,128)(2,1)} %reduce_sum.119), calls=%async_computation.5 | async-start | bytes 2097152 | tf_op jit(solution)/shard_map/all_to_all | solution.py:68
  151.2 1.9 all_to_all.48
  153.2 1.1 copy.30
  154.3 14.7 %all-to-all-done.5 = bf16[64,16,512]{2,1,0:T(8,128)(2,1)S(1)} async-done(((bf16[64,16,512]{2,1,0:T(8,128)(2,1)}), bf16[64,16,512]{2,1,0:T(8,128)(2,1)S(1)}, u32[]{:S(2)}, u32[]{:S(2)}) %all-to-all-start.5) | async-done | bytes 1048608 | tf_op jit(solution)/shard_map/all_to_all | solution.py:68
  169.0 0.2 convert_reduce_fusion
  169.2 0.2 fusion.18
  169.4 0.1 fusion.21
  169.5 1.2 broadcast_in_dim.60
  170.7 5.0 %all-to-all-start.6 = ((bf16[64,16,512]{2,1,0:T(8,128)(2,1)}), bf16[64,16,512]{2,1,0:T(8,128)(2,1)S(1)}, u32[]{:S(2)}, u32[]{:S(2)}) async-start(bf16[64,16,512]{2,1,0:T(8,128)(2,1)} %broadcast_in_dim.60), calls=%async_computation.6 | async-start | bytes 2097152 | tf_op jit(solution)/shard_map/all_to_all | solution.py:20
  175.7 16.3 %fusion.3 = (f32[4096]{0:T(1024)S(1)}, f32[4096,512]{0,1:T(8,128)}) fusion(bf16[4096,512]{0,1:T(8,128)(2,1)} %copy.25, f32[4096]{0:T(1024)S(1)} %copy-done.6, bf16[2048,4096]{1,0:T(8,128)(2,1)} %copy-done.2, bf16[2048,512]{1,0:T(8,128)(2,1)} %copy-done.4), kind=kOutput, calls=%fused_computation.11 | convolution fusion | flops 8598319104 | bytes 31490048 | tf_op jit(solution)/shard_map/dot_general | solution.py:120
  192.0 0.3 all-to-all-done.6
  192.3 0.3 broadcast_in_dim.61
  192.6 8.2 %all_to_all.65 = bf16[2,64,16,512]{3,2,1,0:T(8,128)(2,1)S(1)} all-to-all(bf16[2,64,16,512]{3,2,1,0:T(8,128)(2,1)S(1)} %broadcast_in_dim.61), channel_id=1, replica_groups=mesh['cls_0'=4,'cls_1'=4,'cls_2'=4,'cls_3'=2] {'cls_3'}, dimensions={0} | all-to-all | bytes 4194304 | tf_op jit(solution)/shard_map/all_to_all | solution.py:20
  200.7 7.6 %all-to-all-start.8 = ((bf16[16,128,98]{2,0,1:T(8,128)(2,1)}), bf16[16,128,98]{2,0,1:T(8,128)(2,1)S(1)}, u32[]{:S(2)}, u32[]{:S(2)}) async-start(bf16[16,128,98]{2,0,1:T(8,128)(2,1)} %copy.30), calls=%async_computation.8 | async-start | bytes 1048576 | tf_op jit(solution)/shard_map/all_to_all | solution.py:94
  208.3 8.2 %fusion.6 = bf16[4096,512]{0,1:T(8,128)(2,1)} fusion(f32[4096,512]{0,1:T(8,128)} %get-tuple-element.27, bf16[4096,512]{0,1:T(8,128)(2,1)} %copy.25, f32[4096]{0:T(1024)S(1)} %get-tuple-element.26, f32[4096]{0:T(1024)S(1)} %copy-done.6), kind=kLoop, calls=%fused_computation.14 | loop fusion | flops 12582912 | bytes 16809984 | tf_op jit(solution)/shard_map/convert_element_type | solution.py:126
  216.6 6.4 %copy.31 = bf16[4096,512]{1,0:T(8,128)(2,1)} copy(bf16[4096,512]{0,1:T(8,128)(2,1)} %fusion.6) | data formatting | bytes 8388608
  223.0 1.2 dynamic-slice_subtract_fusion
  224.2 1.6 copy.29
  225.8 2.7 %convolution_bitcast_fusion = f32[98,512]{1,0:T(8,128)} fusion(bf16[2048,512]{1,0:T(8,128)(2,1)} %bitcast.28, bf16[2048,98]{1,0:T(8,128)(2,1)S(1)} %bitcast.31), kind=kOutput, calls=%fused_computation.25 | convolution fusion | flops 205520896 | bytes 2699264 | tf_op jit(solution)/shard_map/dot_general | solution.py:136
  (22 shorter events, 0.1 us)
Async XLA Ops:
  7.8 19.4 %copy-start.7 = (s32[2048]{0:T(1024)S(1)}, s32[2048]{0:T(1024)}, u32[]{:S(2)}) copy-start(s32[2048]{0:T(1024)} %param.7) | copy-start | bytes 24580
  8.9 29.3 %all-to-all-start = ((bf16[64,16,512]{2,1,0:T(8,128)(2,1)}), bf16[64,16,512]{2,1,0:T(8,128)(2,1)S(1)}, u32[]{:S(2)}, u32[]{:S(2)}) async-start(bf16[64,16,512]{2,1,0:T(8,128)(2,1)} %broadcast_in_dim.52), calls=%async_computation | async-start | bytes 2097152 | tf_op jit(solution)/shard_map/all_to_all | solution.py:20
  30.3 17.2 %copy-start.5 = (f32[4096]{0:T(1024)}, f32[4096]{0:T(1024)S(1)}, u32[]{:S(2)}) copy-start(f32[4096]{0:T(1024)S(1)} %add_rsqrt_fusion) | copy-start | bytes 49156
  46.6 2.2 copy-start
  48.8 15.6 %copy-start.4 = (bf16[2048,512]{1,0:T(8,128)(2,1)}, bf16[2048,512]{1,0:T(8,128)(2,1)S(1)}, u32[]{:S(2)}) copy-start(bf16[2048,512]{1,0:T(8,128)(2,1)S(1)} %fusion.8) | copy-start | bytes 6291460
  103.1 20.8 %copy-start.1 = (bf16[4096,512]{0,1:T(8,128)(2,1)S(1)}, bf16[4096,512]{0,1:T(8,128)(2,1)}, u32[]{:S(2)}) copy-start(bf16[4096,512]{0,1:T(8,128)(2,1)} %copy.25) | copy-start | bytes 12582916
  124.0 11.7 %copy-start.2 = (bf16[2048,4096]{1,0:T(8,128)(2,1)}, bf16[2048,4096]{1,0:T(8,128)(2,1)S(1)}, u32[]{:S(2)}) copy-start(bf16[2048,4096]{1,0:T(8,128)(2,1)S(1)} %multiply_convert_fusion) | copy-start | bytes 50331652
  135.7 18.6 %copy-start.8 = (f32[16]{0:T(128)S(1)}, f32[16]{0:T(128)}, u32[]{:S(2)}) copy-start(f32[16]{0:T(128)} %get-tuple-element.28) | copy-start | bytes 196
  135.7 15.5 %copy-start.3 = (bf16[16,12544]{1,0:T(8,128)(2,1)S(1)}, bf16[16,12544]{1,0:T(8,128)(2,1)}, u32[]{:S(2)}) copy-start(bf16[16,12544]{1,0:T(8,128)(2,1)} %param.4) | copy-start | bytes 1204228
  137.5 38.2 %copy-start.6 = (f32[4096]{0:T(1024)S(1)}, f32[4096]{0:T(1024)}, u32[]{:S(2)}) copy-start(f32[4096]{0:T(1024)} %copy-done.5) | copy-start | bytes 49156
  146.5 22.5 %all-to-all-start.5 = ((bf16[64,16,512]{2,1,0:T(8,128)(2,1)}), bf16[64,16,512]{2,1,0:T(8,128)(2,1)S(1)}, u32[]{:S(2)}, u32[]{:S(2)}) async-start(bf16[64,16,512]{2,1,0:T(8,128)(2,1)} %reduce_sum.119), calls=%async_computation.5 | async-start | bytes 2097152 | tf_op jit(solution)/shard_map/all_to_all | solution.py:68
  170.7 21.6 %all-to-all-start.6 = ((bf16[64,16,512]{2,1,0:T(8,128)(2,1)}), bf16[64,16,512]{2,1,0:T(8,128)(2,1)S(1)}, u32[]{:S(2)}, u32[]{:S(2)}) async-start(bf16[64,16,512]{2,1,0:T(8,128)(2,1)} %broadcast_in_dim.60), calls=%async_computation.6 | async-start | bytes 2097152 | tf_op jit(solution)/shard_map/all_to_all | solution.py:20
  200.7 25.1 %all-to-all-start.8 = ((bf16[16,128,98]{2,0,1:T(8,128)(2,1)}), bf16[16,128,98]{2,0,1:T(8,128)(2,1)S(1)}, u32[]{:S(2)}, u32[]{:S(2)}) async-start(bf16[16,128,98]{2,0,1:T(8,128)(2,1)} %copy.30), calls=%async_computation.8 | async-start | bytes 1048576 | tf_op jit(solution)/shard_map/all_to_all | solution.py:94
where the time goes:
time: 230 us; the launch traced here: 229 us
  other arithmetic  57.3 us (25%)
  matrix products  53.5 us (23%)
  blocking collectives  41 us (18%)
  starting transfers between devices  29.2 us (13%)
  local copies, waits for them, and re-layouts  23.8 us (10%)
  waiting for transfers between devices  22.8 us (10%)
    all_to_all x4, blocking collectives, from_everyone(): return lax.all_to_all(copies, axis, split_axis=0, concat_axis=0, tiled=True)  33.7 us
    convert_element_type x1, other arithmetic, on_device(): grad_cos = (logit_scale * (probs - is_target.astype(jnp.float32)) * jnp.w...  20.8 us
    reduce_sum x1, other arithmetic, on_device(): jnp.sum(jnp.exp(logits - logit_scale), axis=1)  18.9 us
    all_to_all x2, starting transfers between devices, from_everyone(): return lax.all_to_all(copies, axis, split_axis=0, concat_axis=0, tiled=True)  17 us
    dot_general x1, matrix products, on_device(): lax.dot_general(grad_cos, emb_low, (((0,), (0,)), ((), ())), preferred_el...  16.3 us
    dot_general x1, matrix products, margin_logits(): lax.dot_general(emb_low, center_low, (((1,), (1,)), ((), ())), preferred_...  15.6 us
    all_to_all x1, waiting for transfers between devices, sum_by_axis(): lax.all_to_all(own.astype(jnp.bfloat16), far, 0, 0, tiled=True)  14.7 us
    unnamed x20, local copies, waits for them, and re-layouts  14 us
  transfers between devices with their start and end apart: 4, of which 3 were waited for; matrix products, arithmetic and copies ran while one was open for 19% of the time, Pallas kernels for 0%

commit v1 on v0

v1 whole, which is shorter than its diff:
```python
import functools
import math

import jax
import jax.numpy as jnp
from jax import lax
from jax.experimental import pallas as pl
from jax.experimental.pallas import tpu as pltpu
from jax.sharding import Mesh
from jax.sharding import PartitionSpec as P

CLS = ("cls_0", "cls_1", "cls_2", "cls_3")
CHIP = ("cls_0", "cls_1", "cls_2")
CORE = "cls_3"

logit_scale = 64.0
cos_margin = math.cos(0.5)
sin_margin = math.sin(0.5)
epsilon = 1e-06

f32 = jnp.float32
bf16 = jnp.bfloat16
MIB = 1024 * 1024


def swapped(x):
    return lax.ppermute(x, CORE, [(0, 1), (1, 0)])


def to_chips(x):
    return lax.all_to_all(x, CHIP, split_axis=0, concat_axis=0, tiled=True)


def from_chips(x):
    copies = jnp.broadcast_to(x, (lax.axis_size(CHIP), *x.shape))
    return lax.all_to_all(copies, CHIP, split_axis=0, concat_axis=0, tiled=True)


def inverse_norm(values, axis):
    return lax.rsqrt(jnp.sum(values * values, axis=axis, keepdims=True) + epsilon)


def margin(target_cos):
    target_sine = jnp.sqrt(1.0 - target_cos * target_cos)
    margined = target_cos * cos_margin - target_sine * sin_margin
    slope = cos_margin + sin_margin * target_cos / target_sine
    return margined, slope


def centers_kernel(base, steps, ids_ref, c_ref, *refs):
    if base:
        refs = refs[2:]
    low_ref, turned_ref, found_ref = refs[:3]
    i = pl.program_id(0)
    rows = c_ref.shape[0]
    block = c_ref[...].astype(f32)
    low = (block * inverse_norm(block, 1)).astype(bf16)
    low_ref[...] = low
    turned = low.T
    turned_ref[...] = turned
    ids = ids_ref[...] - (base + i) * rows
    hit = lax.broadcasted_iota(jnp.int32, (rows, ids.shape[1]), 0) == ids
    rows_here = jnp.dot(turned, jnp.where(hit, 1.0, 0.0).astype(bf16), preferred_element_type=f32)

    @pl.when(i == 0)
    def _():
        found_ref[...] = rows_here

    @pl.when(i > 0)
    def _():
        found_ref[...] += rows_here


def prepared_centers(centers, ids, old, half, halves, rows=512):
    count, depth = centers.shape
    steps = count // rows
    base = half * steps
    samples = ids.shape[1]
    whole = halves * count
    old = () if old is None else old
    return pl.pallas_call(
        functools.partial(centers_kernel, base, steps),
        grid=(steps,),
        in_specs=[
            pl.BlockSpec((1, samples), lambda i: (0, 0)),
            pl.BlockSpec((rows, depth), lambda i: (i, 0)),
        ]
        + [pl.BlockSpec(memory_space=pl.ANY)] * len(old),
        out_specs=[
            pl.BlockSpec((rows, depth), lambda i: (base + i, 0)),
            pl.BlockSpec((depth, rows), lambda i: (0, base + i)),
            pl.BlockSpec((depth, samples), lambda i: (0, 0)),
        ],
        out_shape=[
            jax.ShapeDtypeStruct((whole, depth), bf16),
            jax.ShapeDtypeStruct((depth, whole), bf16),
            jax.ShapeDtypeStruct((depth, samples), f32),
        ],
        input_output_aliases={2: 0, 3: 1} if old else {},
        compiler_params=pltpu.CompilerParams(vmem_limit_bytes=24 * MIB),
        cost_estimate=pl.CostEstimate(
            flops=2 * count * depth * samples, bytes_accessed=6 * count * depth, transcendentals=0
        ),
        name=f"centers_{half}",
    )(ids, centers, *old)


def logits_kernel(sub, x_ref, ids_ref, found_ref, low_ref, turned_ref, exp_ref, sums_ref, pull_ref, stat_ref,
                  emb_ref, turned_emb, total, row_sum):
    i = pl.program_id(0)
    rows = low_ref.shape[0]
    samples = x_ref.shape[0]

    @pl.when(i == 0)
    def _():
        x = x_ref[...].astype(f32)
        emb = (x * inverse_norm(x, 1)).astype(bf16)
        emb_ref[...] = emb
        turned_emb[...] = (emb * logit_scale).astype(bf16).T
        total[...] = jnp.zeros_like(total)
        row_sum[...] = jnp.zeros_like(row_sum)

    low = low_ref[...]
    turned = turned_ref[...]
    here = lax.broadcasted_iota(jnp.int32, (rows, sub), 0)
    parts = samples // sub
    logits = jnp.dot(low, turned_emb[:, :sub], preferred_element_type=f32)
    for s in range(parts):
        span = slice(s * sub, (s + 1) * sub)
        if s + 1 < parts:
            later = jnp.dot(low, turned_emb[:, (s + 1) * sub : (s + 2) * sub], preferred_element_type=f32)
        ids = ids_ref[:, span] - i * rows
        weight = jnp.where(here == ids, 0.0, jnp.exp(logits))
        row_sum[:, span] += jnp.sum(weight.reshape(rows // 8, 8, sub), axis=0)
        weight = weight.astype(bf16)
        exp_ref[:, span] = weight
        total[:, span] += jnp.dot(turned, weight, preferred_element_type=f32)
        if s + 1 < parts:
            logits = later

    @pl.when(i == pl.num_programs(0) - 1)
    def _():
        pull_ref[...] = total[...].astype(bf16).T
        found = found_ref[...]
        target_cos = jnp.sum(turned_emb[...].astype(f32) * found, axis=0, keepdims=True) * (1.0 / logit_scale)
        sums_ref[...] = jnp.sum(row_sum[...], axis=0, keepdims=True)
        stat_ref[...] = target_cos


def exponentials(x, ids, found, low, turned, rows=512, sub=256):
    samples, depth = x.shape
    count = low.shape[0]
    fixed = lambda i: (0, 0)
    return pl.pallas_call(
        functools.partial(logits_kernel, sub),
        grid=(count // rows,),
        in_specs=[
            pl.BlockSpec((samples, depth), fixed),
            pl.BlockSpec((1, samples), fixed),
            pl.BlockSpec((depth, samples), fixed),
            pl.BlockSpec((rows, depth), lambda i: (i, 0)),
            pl.BlockSpec((depth, rows), lambda i: (0, i)),
        ],
        out_specs=[
            pl.BlockSpec((rows, samples), lambda i: (i, 0)),
            pl.BlockSpec((1, samples), fixed),
            pl.BlockSpec((samples, depth), fixed),
            pl.BlockSpec((1, samples), fixed),
            pl.BlockSpec((samples, depth), fixed),
        ],
        out_shape=[
            jax.ShapeDtypeStruct((count, samples), bf16),
            jax.ShapeDtypeStruct((1, samples), f32),
            jax.ShapeDtypeStruct((samples, depth), bf16),
            jax.ShapeDtypeStruct((1, samples), f32),
            jax.ShapeDtypeStruct((samples, depth), bf16),
        ],
        scratch_shapes=[
            pltpu.VMEM((depth, samples), bf16),
            pltpu.VMEM((depth, samples), f32),
            pltpu.VMEM((8, samples), f32),
        ],
        compiler_params=pltpu.CompilerParams(vmem_limit_bytes=36 * MIB),
        cost_estimate=pl.CostEstimate(
            flops=4 * count * depth * samples, bytes_accessed=4 * count * depth, transcendentals=count * samples
        ),
        name="exponentials",
    )(x, ids, found, low, turned)


def push_kernel(base, final, ids_ref, patch_ref, emb_ref, exp_ref, *refs):
    i = pl.program_id(0)
    rows = exp_ref.shape[0]
    ids = ids_ref[...] - (base + i) * rows
    hit = lax.broadcasted_iota(jnp.int32, exp_ref.shape, 0) == ids
    weight = jnp.where(hit, patch_ref[...], exp_ref[...].astype(f32)).astype(bf16)
    push = jnp.dot(weight, emb_ref[...], preferred_element_type=f32)
    if final:
        c_ref, other_ref, out_ref = refs
        push = push + other_ref[...].astype(f32)
        block = c_ref[...].astype(f32)
        inv = inverse_norm(block, 1)
        unit = block * inv
        push = (push - unit * jnp.sum(push * unit, axis=1, keepdims=True)) * inv
        out_ref[...] = push.astype(bf16)
    else:
        (out_ref,) = refs
        out_ref[...] = push.astype(bf16)


def pushed(ids, patch, emb, exps, half, centers=None, other=None, rows=512):
    samples, depth = emb.shape
    count = exps.shape[0] // 2
    base = half * (count // rows)
    final = centers is not None
    fixed = lambda i: (0, 0)
    step = lambda i: (i, 0)
    extra = (centers, other) if final else ()
    return pl.pallas_call(
        functools.partial(push_kernel, base, final),
        grid=(count // rows,),
        in_specs=[
            pl.BlockSpec((1, samples), fixed),
            pl.BlockSpec((1, samples), fixed),
            pl.BlockSpec((samples, depth), fixed),
            pl.BlockSpec((rows, samples), lambda i: (base + i, 0)),
        ]
        + [pl.BlockSpec((rows, depth), step)] * len(extra),
        out_specs=pl.BlockSpec((rows, depth), step),
        out_shape=jax.ShapeDtypeStruct((count, depth), bf16),
        compiler_params=pltpu.CompilerParams(vmem_limit_bytes=24 * MIB),
        cost_estimate=pl.CostEstimate(
            flops=2 * count * depth * samples, bytes_accessed=2 * count * samples, transcendentals=0
        ),
        name=f"push_{half}",
    )(ids, patch, emb, exps, *extra)


def on_device(features, fc_weight, centers, labels):
    own, wide = features.shape
    class_rows, depth = centers.shape
    chips = lax.axis_size(CHIP)
    chip = lax.axis_index(CHIP)
    core = lax.axis_index(CORE)
    samples = chips * own

    other_centers = swapped(centers)
    embedded = jnp.dot(features, fc_weight, preferred_element_type=f32).astype(bf16)
    x = from_chips(embedded).reshape(samples, depth)

    by_core = labels.reshape(chips, 2, own)
    my_labels = jnp.where(core == 0, by_core[:, 0], by_core[:, 1]).reshape(1, samples)
    local = my_labels - chip * (2 * class_rows)
    inside = (local >= 0) & (local < 2 * class_rows)
    turned_ids = jnp.where(core == 0, local, (local + class_rows) % (2 * class_rows))
    ids = jnp.where(inside, turned_ids, -1)

    low, turned, found_a = prepared_centers(centers, ids, None, 0, 2)
    low, turned, found_b = prepared_centers(other_centers, ids, (low, turned), 1, 2)
    found = found_a + found_b

    split = features.reshape(own, chips, 2, wide // (2 * chips))
    mine = jnp.where(core == 0, split[:, :, 0], split[:, :, 1])
    theirs = jnp.where(core == 0, split[:, :, 1], split[:, :, 0])
    fcols = mine.shape[-1]
    pad = ((0, 0), (0, 0), (0, 128 - fcols))
    cargo = jnp.concatenate(
        [
            found.astype(bf16).T.reshape(chips, own, depth),
            jnp.pad(mine.swapaxes(0, 1), pad),
            jnp.pad(theirs.swapaxes(0, 1), pad),
        ],
        axis=2,
    )
    cargo = to_chips(cargo)

    exps, part_sums, pull, target_cos, emb_low = exponentials(x, ids, found, low, turned)
    is_here = ids >= 0
    margined, slope = margin(target_cos)
    target_exp = jnp.exp(logit_scale * margined)
    part_sums = part_sums + jnp.where(is_here, target_exp, 0.0)

    pulls = to_chips(pull.reshape(chips, own, depth))
    sums = jnp.sum(from_chips(part_sums), axis=0)

    patch = slope * (target_exp - sums)
    scaled = (emb_low.astype(f32) * (logit_scale / sums.reshape(samples, 1))).astype(bf16)
    other_push = swapped(pushed(ids, patch, scaled, exps, 1))
    grad_centers = pushed(ids, patch, scaled, exps, 0, centers, other_push)

    own_float = embedded.astype(f32)
    inv_emb = inverse_norm(own_float, 1)
    emb_dir = own_float * inv_emb
    own_target = jnp.sum(cargo[:, :, :depth].astype(f32), axis=0)
    own_cos = jnp.sum(emb_dir.astype(bf16).astype(f32) * own_target, axis=1, keepdims=True)
    own_margined, own_slope = margin(own_cos)
    own_logit = logit_scale * own_margined
    own_sums = lax.dynamic_slice_in_dim(sums.reshape(samples), chip * own, own).reshape(own, 1)
    loss = (jnp.log(own_sums) - own_logit).reshape(own)
    own_pull = jnp.sum(pulls.astype(f32), axis=0)
    at_target = logit_scale * own_slope * (jnp.exp(own_logit) / own_sums - 1.0)
    grad_dir = own_pull * (logit_scale / own_sums) + at_target * own_target
    grad_emb = (
        (grad_dir - emb_dir * jnp.sum(grad_dir * emb_dir, axis=1, keepdims=True)) * inv_emb
    ).astype(bf16)

    grads = from_chips(grad_emb).reshape(samples, depth)
    columns = cargo[:, :, depth:].reshape(samples, 256)
    both = lax.dot_general(columns, grads, (((0,), (0,)), ((), ())), preferred_element_type=f32)
    grad_fc = both[:fcols] + swapped(both[128 : 128 + fcols])
    return (loss, grad_centers, grad_fc)


def solution(mesh):
    torus = Mesh(mesh.devices.reshape(4, 4, 4, 2), CLS)
    placed = (P(CLS, None), P(), P(CLS, None), P())
    return jax.shard_map(
        on_device,
        mesh=torus,
        in_specs=placed,
        out_specs=(P(CLS), P(CLS, None), P(CLS, None)),
        check_vma=False,
    )
```

time: 230 us -> 213 us (0.926)
  Pallas kernels: 0 us -> 65.4 us
  other arithmetic: 57.3 us -> 10.3 us
  matrix products: 53.5 us -> 8.14 us
  blocking collectives: 41 us -> 0 us
  waiting for transfers between devices: 22.8 us -> 43 us
  starting transfers between devices: 29.2 us -> 49.3 us
  local copies, waits for them, and re-layouts: 23.8 us -> 34.6 us
    pallas_call x0 -> x5, Pallas kernels: none -> 65.4 us  [the longest x1 28 us: exponentials(): pl.pallas_call(functools.partial(logits_kernel, sub), grid=(count // rows...]
    dot_general x5 -> x2, matrix products: 53.5 us -> 8.14 us  [the longest x1 6.67 us: on_device(): jnp.dot(features, fc_weight, preferred_element_type=f32).astype(bf16)]
    all_to_all x5 -> x0, blocking collectives: 41 us -> none  [the longest x4 33.7 us: from_everyone(): return lax.all_to_all(copies, axis, split_axis=0, concat_axis=0, tiled=True)]
    convert_element_type x4 -> x1, other arithmetic: 30 us -> 0.29 us  [on_device(): (emb_low.astype(f32) * (logit_scale / sums.reshape(samples, 1))).astype(b...]
    reduce_sum x7 -> x4, other arithmetic: 24.6 us -> 4.13 us  [the longest x1 1.4 us: on_device(): own_pull = jnp.sum(pulls.astype(f32), axis=0)]
    all_to_all x4 -> x5, waiting for transfers between devices: 22.8 us -> 41.9 us  [the longest x2 21.6 us: to_chips(): return lax.all_to_all(x, CHIP, split_axis=0, concat_axis=0, tiled=True)]
    all_to_all x4 -> x5, starting transfers between devices: 29.2 us -> 42.4 us  [the longest x3 26.7 us: from_chips(): return lax.all_to_all(copies, CHIP, split_axis=0, concat_axis=0, tiled=True)]
    unnamed x20 -> x26, local copies, waits for them, and re-layouts: 14 us -> 24.5 us
  transfers between devices with their start and end apart: 4 -> 8, of which waited for: 3 -> 4; matrix products, arithmetic and copies ran while one was open for 19% -> 13% of each run, Pallas kernels for 0% -> 13%
where the time goes in v1:
time: 213 us; the launch traced here: 212 us
  Pallas kernels  65.4 us (31%)
  starting transfers between devices  49.3 us (23%)
  waiting for transfers between devices  43 us (20%)
  local copies, waits for them, and re-layouts  34.6 us (16%)
  other arithmetic  10.3 us (5%)
  matrix products  8.14 us (4%)
    pallas_call x1, Pallas kernels, exponentials(): pl.pallas_call(functools.partial(logits_kernel, sub), grid=(count // rows...  28 us
    all_to_all x3, starting transfers between devices, from_chips(): return lax.all_to_all(copies, CHIP, split_axis=0, concat_axis=0, tiled=True)  26.7 us
    unnamed x26, local copies, waits for them, and re-layouts  24.5 us
    all_to_all x2, waiting for transfers between devices, to_chips(): return lax.all_to_all(x, CHIP, split_axis=0, concat_axis=0, tiled=True)  21.6 us
    pallas_call x2, Pallas kernels, prepared_centers(): pl.pallas_call(functools.partial(centers_kernel, base, steps), grid=(step...  20.4 us
    all_to_all x3, waiting for transfers between devices, from_chips(): return lax.all_to_all(copies, CHIP, split_axis=0, concat_axis=0, tiled=True)  20.3 us
    pallas_call x2, Pallas kernels, pushed(): pl.pallas_call(functools.partial(push_kernel, base, final), grid=(count /...  17 us
    all_to_all x2, starting transfers between devices, to_chips(): return lax.all_to_all(x, CHIP, split_axis=0, concat_axis=0, tiled=True)  15.7 us
  transfers between devices with their start and end apart: 8, of which 4 were waited for; matrix products, arithmetic and copies ran while one was open for 13% of the time, Pallas kernels for 13%

profile of v1, /device:TPU:1, one launch (start us, length us, event | category | flops | bytes accessed | tf_op | source)
XLA Modules:
  0.0 211.6 jit_solution(16960669353312390246)
XLA Ops:
  0.6 1.5 collective-permute-start
  2.1 6.7 %fusion.14 = (f32[16]{0:T(128)S(1)}, bf16[16,512]{1,0:T(8,128)(2,1)S(1)}) fusion(bf16[16,12544]{1,0:T(8,128)(2,1)} %param.4, bf16[12544,512]{1,0:T(8,128)(2,1)} %param.5), kind=kOutput, calls=%fused_computation.29 | convolution fusion | flops 205553648 | bytes 13262912 | tf_op jit(solution)/shard_map/dot_general | solution.py:248
  8.8 1.2 broadcast_in_dim.20
  10.0 11.2 %all-to-all-start = ((bf16[64,16,512]{2,1,0:T(8,128)(2,1)}), bf16[64,16,512]{2,1,0:T(8,128)(2,1)S(1)}, u32[]{:S(2)}, u32[]{:S(2)}) async-start(bf16[64,16,512]{2,1,0:T(8,128)(2,1)} %broadcast_in_dim.20), calls=%async_computation | async-start | bytes 2097152 | tf_op jit(solution)/shard_map/all_to_all | solution.py:36
  21.3 2.8 %reshape.207 = bf16[16,64,2,98]{3,2,1,0:T(2,128)(2,1)} reshape(bf16[16,12544]{1,0:T(8,128)(2,1)S(1)} %copy-done.10) | data formatting | bytes 802816 | tf_op jit(solution)/shard_map/reshape | solution.py:262
  24.0 0.1 reshape.204
  24.2 0.1 fusion.16
  24.3 0.1 sub.63
  24.4 2.2 %copy-done.5 = bf16[4096,512]{1,0:T(8,128)(2,1)S(1)} copy-done((bf16[4096,512]{1,0:T(8,128)(2,1)S(1)}, bf16[4096,512]{1,0:T(8,128)(2,1)}, u32[]{:S(2)}) %copy-start.5) | copy-done | bytes 4194328
  26.6 9.7 %centers_0.1 = (bf16[8192,512]{1,0:T(8,128)(2,1)S(1)}, bf16[512,8192]{1,0:T(8,128)(2,1)S(1)}, f32[512,1024]{1,0:T(8,128)S(1)}) custom-call(s32[1,1024]{1,0:T(1,128)S(1)} %and_select_fusion.1.ids_ref, bf16[4096,512]{1,0:T(8,128)(2,1)S(1)} %copy-done.5), custom_call_target="tpu_custom_call" | custom-call | flops 4294967296 | bytes 12582912 | tf_op jit(solution)/shard_map/centers_0/pallas_call | solution.py:81
  36.3 10.7 %centers_1.1 = (bf16[8192,512]{1,0:T(8,128)(2,1)S(1)}, bf16[512,8192]{1,0:T(8,128)(2,1)S(1)}, f32[512,1024]{1,0:T(8,128)S(1)}) custom-call(s32[1,1024]{1,0:T(1,128)S(1)} %and_select_fusion.1.ids_ref, bf16[4096,512]{1,0:T(8,128)(2,1)} %collective-permute-done.c_ref, ...), custom_call_target="tpu_custom_call", output_to_operand_aliasing={{0}: (2, {}), {1}: (3, {})} | custom-call | flops 4294967296 | bytes 12582912 | tf_op jit(solution)/shard_map/centers_1/pallas_call | solution.py:81
  47.0 3.2 %copy-done.2 = bf16[8192,512]{1,0:T(8,128)(2,1)} copy-done((bf16[8192,512]{1,0:T(8,128)(2,1)}, bf16[8192,512]{1,0:T(8,128)(2,1)S(1)}, u32[]{:S(2)}) %copy-start.2) | copy-done | bytes 8388632
  50.2 3.2 %copy-done.4 = bf16[512,8192]{1,0:T(8,128)(2,1)} copy-done((bf16[512,8192]{1,0:T(8,128)(2,1)}, bf16[512,8192]{1,0:T(8,128)(2,1)S(1)}, u32[]{:S(2)}) %copy-start.4) | copy-done | bytes 8388632
  53.4 1.5 convert_bitcast_fusion
  54.9 3.4 %copy-done.3 = bf16[8192,512]{1,0:T(8,128)(2,1)S(1)} copy-done((bf16[8192,512]{1,0:T(8,128)(2,1)S(1)}, bf16[8192,512]{1,0:T(8,128)(2,1)}, u32[]{:S(2)}) %copy-start.3) | copy-done | bytes 8388632
  58.3 28.0 %exponentials.1 = (bf16[8192,1024]{1,0:T(8,128)(2,1)}, f32[1,1024]{1,0:T(1,128)S(1)}, bf16[1024,512]{1,0:T(8,128)(2,1)}, f32[1,1024]{1,0:T(1,128)S(1)}, bf16[1024,512]{1,0:T(8,128)(2,1)S(1)}) custom-call(bf16[1024,512]{1,0:T(8,128)(2,1)S(1)} %bitcast.19, s32[1,1024]{1,0:T(1,128)S(1)} %and_select_fusion.1.ids_ref, ...), custom_call_target="tpu_custom_call" | custom-call | flops 17179869184 | bytes 16777216 | tf_op jit(solution)/shard_map/exponentials/pallas_call | solution.py:154
  86.3 1.0 copy-done.7
  87.4 0.8 broadcast_in_dim.23
  88.2 10.2 %all-to-all-start.1 = ((f32[64,1,1024]{2,1,0:T(1,128)}), f32[64,1,1024]{2,1,0:T(1,128)}, u32[]{:S(2)}, u32[]{:S(2)}) async-start(f32[64,1,1024]{2,1,0:T(1,128)} %broadcast_in_dim.23), calls=%async_computation.1 | async-start | bytes 524288 | tf_op jit(solution)/shard_map/all_to_all | solution.py:36
  98.4 2.3 %fusion.19 = (bf16[16,64,1,98]{3,2,1,0:T(2,128)(2,1)S(1)}, bf16[16,64,1,98]{3,2,1,0:T(2,128)(2,1)S(1)}) fusion(bf16[16,64,2,98]{3,2,1,0:T(2,128)(2,1)} %reshape.207), kind=kLoop, calls=%fused_computation.55 | loop fusion | bytes 802816 | tf_op jit(solution)/shard_map/slice | solution.py:263
  100.7 1.3 select_bitcast_fusion.1
  102.0 0.5 copy.25
  102.5 5.0 %all-to-all-done.1 = f32[64,1,1024]{2,1,0:T(1,128)} async-done(((f32[64,1,1024]{2,1,0:T(1,128)}), f32[64,1,1024]{2,1,0:T(1,128)}, u32[]{:S(2)}, u32[]{:S(2)}) %all-to-all-start.1) | async-done | bytes 262176 | tf_op jit(solution)/shard_map/all_to_all | solution.py:36
  107.5 5.5 %all-to-all-start.3 = ((bf16[64,16,512]{2,1,0:T(8,128)(2,1)}), bf16[64,16,512]{2,1,0:T(8,128)(2,1)}, u32[]{:S(2)}, u32[]{:S(2)}) async-start(bf16[64,16,512]{2,1,0:T(8,128)(2,1)} %bitcast.9), calls=%async_computation.3 | async-start | bytes 2097152 | tf_op jit(solution)/shard_map/all_to_all | solution.py:31
  113.0 1.1 reduce_sum.56
  114.2 0.3 multiply_convert_fusion.emb_ref
  114.5 5.8 %copy-done = bf16[8192,1024]{1,0:T(8,128)(2,1)S(1)} copy-done((bf16[8192,1024]{1,0:T(8,128)(2,1)S(1)}, bf16[8192,1024]{1,0:T(8,128)(2,1)}, u32[]{:S(2)}) %copy-start) | copy-done | bytes 16777240
  120.3 6.8 %push_1.1 = bf16[4096,512]{1,0:T(8,128)(2,1)} custom-call(s32[1,1024]{1,0:T(1,128)S(1)} %and_select_fusion.1.ids_ref, f32[1,1024]{1,0:T(1,128)S(1)} %subtract_multiply_fusion.patch_ref, bf16[1024,512]{1,0:T(8,128)(2,1)S(1)} %multiply_convert_fusion.emb_ref, bf16[8192,1024]{1,0:T(8,128)(2,1)S(1)} %copy-done), custom_call_target="tpu_custom_call" | custom-call | flops 4294967296 | bytes 8388608 | tf_op jit(solution)/shard_map/push_1/pallas_call | solution.py:219
  127.1 2.1 collective-permute-start.1
  129.2 1.3 fusion.4
  130.5 10.2 %all-to-all-start.2 = ((bf16[64,16,768]{2,1,0:T(8,128)(2,1)}), bf16[64,16,768]{2,1,0:T(8,128)(2,1)}, u32[]{:S(2)}, u32[]{:S(2)}) async-start(bf16[64,16,768]{2,1,0:T(8,128)(2,1)} %fusion.4), calls=%async_computation.2 | async-start | bytes 3145728 | tf_op jit(solution)/shard_map/all_to_all | solution.py:31
  140.7 1.4 convert_reduce_fusion
  142.1 21.6 %all-to-all-done.2 = bf16[64,16,768]{2,1,0:T(8,128)(2,1)} async-done(((bf16[64,16,768]{2,1,0:T(8,128)(2,1)}), bf16[64,16,768]{2,1,0:T(8,128)(2,1)}, u32[]{:S(2)}, u32[]{:S(2)}) %all-to-all-start.2) | async-done | bytes 1572896 | tf_op jit(solution)/shard_map/all_to_all | solution.py:31
  163.8 1.4 convert_reduce_fusion.1
  165.2 0.2 multiply_reduce_fusion
  165.3 0.6 add_multiply_fusion
  165.9 0.2 fusion.10
  166.1 0.1 fusion.13
  166.2 1.1 broadcast_in_dim.24
  167.3 5.2 %all-to-all-start.4 = ((bf16[64,16,512]{2,1,0:T(8,128)(2,1)}), bf16[64,16,512]{2,1,0:T(8,128)(2,1)S(1)}, u32[]{:S(2)}, u32[]{:S(2)}) async-start(bf16[64,16,512]{2,1,0:T(8,128)(2,1)} %broadcast_in_dim.24), calls=%async_computation.4 | async-start | bytes 2097152 | tf_op jit(solution)/shard_map/all_to_all | solution.py:36
  172.5 1.1 slice.39
  173.6 15.3 %all-to-all-done.4 = bf16[64,16,512]{2,1,0:T(8,128)(2,1)S(1)} async-done(((bf16[64,16,512]{2,1,0:T(8,128)(2,1)}), bf16[64,16,512]{2,1,0:T(8,128)(2,1)S(1)}, u32[]{:S(2)}, u32[]{:S(2)}) %all-to-all-start.4) | async-done | bytes 1048608 | tf_op jit(solution)/shard_map/all_to_all | solution.py:36
  188.9 1.5 convolution_bitcast_fusion
  190.4 3.4 %collective-permute-start.2 = (f32[98,512]{1,0:T(8,128)S(1)}, f32[98,512]{1,0:T(8,128)S(1)}, u32[]{:S(2)}, u32[]{:S(2)}) collective-permute-start(f32[98,512]{1,0:T(8,128)S(1)} %slice.41), channel_id=1, source_target_pairs={{0,1},{1,0},{2,3},{3,2},{4,5},{5,4},{6,7},{7,6},{8,9},{9,8},{10,11... | collective-permute-start | bytes 602120 | tf_op jit(solution)/shard_map/ppermute | solution.py:27
  193.8 1.1 collective-permute-done.2
  194.9 0.7 slice_add_fusion
  195.6 5.8 %copy-done.1 = bf16[8192,1024]{1,0:T(8,128)(2,1)S(1)} copy-done((bf16[8192,1024]{1,0:T(8,128)(2,1)S(1)}, bf16[8192,1024]{1,0:T(8,128)(2,1)}, u32[]{:S(2)}) %copy-start.1) | copy-done | bytes 16777240
  201.4 10.2 %push_0.1 = bf16[4096,512]{1,0:T(8,128)(2,1)} custom-call(s32[1,1024]{1,0:T(1,128)S(1)} %and_select_fusion.1.ids_ref, f32[1,1024]{1,0:T(1,128)S(1)} %subtract_multiply_fusion.patch_ref, bf16[1024,512]{1,0:T(8,128)(2,1)S(1)} %multiply_convert_fusion.emb_ref, bf16[8192,1024]{1,0:T(8,128)(2,1)S(1)} %copy-done.1, bf16[4096,512]{1,0:T(8,128)(2,1)S(1)} %copy-done.6, ...), custom_call_target="tpu_custom_call" | custom-call | flops 4294967296 | bytes 8388608 | tf_op jit(solution)/shard_map/push_0/pallas_call | solution.py:219
  (29 shorter events, 0.2 us)
Async XLA Ops:
  0.6 35.6 %collective-permute-start = (bf16[4096,512]{1,0:T(8,128)(2,1)}, bf16[4096,512]{1,0:T(8,128)(2,1)}, u32[]{:S(2)}, u32[]{:S(2)}) collective-permute-start(bf16[4096,512]{1,0:T(8,128)(2,1)} %refs_0_.1), channel_id=1, source_target_pairs={{0,1},{1,0},{2,3},{3,2},{4,5},{5,4},{6,7},{7,6},{8,9},{9,8},{10,11... | collective-permute-start | bytes 12582920 | tf_op jit(solution)/shard_map/ppermute | solution.py:27
  8.8 12.5 %copy-start.10 = (bf16[16,12544]{1,0:T(8,128)(2,1)S(1)}, bf16[16,12544]{1,0:T(8,128)(2,1)}, u32[]{:S(2)}) copy-start(bf16[16,12544]{1,0:T(8,128)(2,1)} %param.4) | copy-start | bytes 1204228
  8.8 15.2 %copy-start.12 = (s32[2048]{0:T(1024)S(1)}, s32[2048]{0:T(1024)}, u32[]{:S(2)}) copy-start(s32[2048]{0:T(1024)} %param.7) | copy-start | bytes 24580
  10.0 45.0 %all-to-all-start = ((bf16[64,16,512]{2,1,0:T(8,128)(2,1)}), bf16[64,16,512]{2,1,0:T(8,128)(2,1)S(1)}, u32[]{:S(2)}, u32[]{:S(2)}) async-start(bf16[64,16,512]{2,1,0:T(8,128)(2,1)} %broadcast_in_dim.20), calls=%async_computation | async-start | bytes 2097152 | tf_op jit(solution)/shard_map/all_to_all | solution.py:36
  24.4 2.2 %copy-start.5 = (bf16[4096,512]{1,0:T(8,128)(2,1)S(1)}, bf16[4096,512]{1,0:T(8,128)(2,1)}, u32[]{:S(2)}) copy-start(bf16[4096,512]{1,0:T(8,128)(2,1)} %refs_0_.1) | copy-start | bytes 12582916
  47.0 3.2 %copy-start.2 = (bf16[8192,512]{1,0:T(8,128)(2,1)}, bf16[8192,512]{1,0:T(8,128)(2,1)S(1)}, u32[]{:S(2)}) copy-start(bf16[8192,512]{1,0:T(8,128)(2,1)S(1)} %get-tuple-element.18.low_ref) | copy-start | bytes 25165828
  50.2 3.2 %copy-start.4 = (bf16[512,8192]{1,0:T(8,128)(2,1)}, bf16[512,8192]{1,0:T(8,128)(2,1)S(1)}, u32[]{:S(2)}) copy-start(bf16[512,8192]{1,0:T(8,128)(2,1)S(1)} %get-tuple-element.19.turned_ref) | copy-start | bytes 25165828
  54.9 3.4 %copy-start.3 = (bf16[8192,512]{1,0:T(8,128)(2,1)S(1)}, bf16[8192,512]{1,0:T(8,128)(2,1)}, u32[]{:S(2)}) copy-start(bf16[8192,512]{1,0:T(8,128)(2,1)} %copy-done.2) | copy-start | bytes 25165828
  86.3 1.0 copy-start.7
  87.3 14.7 %copy-start.9 = (bf16[1024,512]{0,1:T(8,128)(2,1)S(1)}, bf16[1024,512]{0,1:T(8,128)(2,1)}, u32[]{:S(2)}) copy-start(bf16[1024,512]{0,1:T(8,128)(2,1)} %get-tuple-element.25) | copy-start | bytes 3145732
  88.2 19.3 %all-to-all-start.1 = ((f32[64,1,1024]{2,1,0:T(1,128)}), f32[64,1,1024]{2,1,0:T(1,128)}, u32[]{:S(2)}, u32[]{:S(2)}) async-start(f32[64,1,1024]{2,1,0:T(1,128)} %broadcast_in_dim.23), calls=%async_computation.1 | async-start | bytes 524288 | tf_op jit(solution)/shard_map/all_to_all | solution.py:36
  100.7 13.5 %copy-start.8 = (bf16[1024,512]{1,0:T(8,128)(2,1)S(1)}, bf16[1024,512]{1,0:T(8,128)(2,1)}, u32[]{:S(2)}) copy-start(bf16[1024,512]{1,0:T(8,128)(2,1)} %copy-done.7) | copy-start | bytes 3145732
  107.5 23.0 %all-to-all-start.3 = ((bf16[64,16,512]{2,1,0:T(8,128)(2,1)}), bf16[64,16,512]{2,1,0:T(8,128)(2,1)}, u32[]{:S(2)}, u32[]{:S(2)}) async-start(bf16[64,16,512]{2,1,0:T(8,128)(2,1)} %bitcast.9), calls=%async_computation.3 | async-start | bytes 2097152 | tf_op jit(solution)/shard_map/all_to_all | solution.py:31
  114.5 5.8 %copy-start = (bf16[8192,1024]{1,0:T(8,128)(2,1)S(1)}, bf16[8192,1024]{1,0:T(8,128)(2,1)}, u32[]{:S(2)}) copy-start(bf16[8192,1024]{1,0:T(8,128)(2,1)} %get-tuple-element.23.exp_ref) | copy-start | bytes 50331652
  120.3 8.9 %copy-start.11 = (bf16[64,16,98]{2,1,0:T(8,128)(2,1)S(1)}, bf16[64,16,98]{2,1,0:T(8,128)(2,1)}, u32[]{:S(2)}) copy-start(bf16[64,16,98]{2,1,0:T(8,128)(2,1)} %get-tuple-element.28) | copy-start | bytes 602116
  127.1 68.5 %collective-permute-start.1 = (bf16[4096,512]{1,0:T(8,128)(2,1)}, bf16[4096,512]{1,0:T(8,128)(2,1)}, u32[]{:S(2)}, u32[]{:S(2)}) collective-permute-start(bf16[4096,512]{1,0:T(8,128)(2,1)} %push_1.1), channel_id=1, source_target_pairs={{0,1},{1,0},{2,3},{3,2},{4,5},{5,4},{6,7},{7,6},{8,9},{9,8},{10,11... | collective-permute-start | bytes 12582920 | tf_op jit(solution)/shard_map/ppermute | solution.py:27
  130.5 33.2 %all-to-all-start.2 = ((bf16[64,16,768]{2,1,0:T(8,128)(2,1)}), bf16[64,16,768]{2,1,0:T(8,128)(2,1)}, u32[]{:S(2)}, u32[]{:S(2)}) async-start(bf16[64,16,768]{2,1,0:T(8,128)(2,1)} %fusion.4), calls=%async_computation.2 | async-start | bytes 3145728 | tf_op jit(solution)/shard_map/all_to_all | solution.py:31
  167.3 21.6 %all-to-all-start.4 = ((bf16[64,16,512]{2,1,0:T(8,128)(2,1)}), bf16[64,16,512]{2,1,0:T(8,128)(2,1)S(1)}, u32[]{:S(2)}, u32[]{:S(2)}) async-start(bf16[64,16,512]{2,1,0:T(8,128)(2,1)} %broadcast_in_dim.24), calls=%async_computation.4 | async-start | bytes 2097152 | tf_op jit(solution)/shard_map/all_to_all | solution.py:36
  188.9 6.7 %copy-start.6 = (bf16[4096,512]{1,0:T(8,128)(2,1)S(1)}, bf16[4096,512]{1,0:T(8,128)(2,1)}, u32[]{:S(2)}) copy-start(bf16[4096,512]{1,0:T(8,128)(2,1)} %refs_0_.1) | copy-start | bytes 12582916
  190.4 4.5 %collective-permute-start.2 = (f32[98,512]{1,0:T(8,128)S(1)}, f32[98,512]{1,0:T(8,128)S(1)}, u32[]{:S(2)}, u32[]{:S(2)}) collective-permute-start(f32[98,512]{1,0:T(8,128)S(1)} %slice.41), channel_id=1, source_target_pairs={{0,1},{1,0},{2,3},{3,2},{4,5},{5,4},{6,7},{7,6},{8,9},{9,8},{10,11... | collective-permute-start | bytes 602120 | tf_op jit(solution)/shard_map/ppermute | solution.py:27
  195.6 5.8 %copy-start.1 = (bf16[8192,1024]{1,0:T(8,128)(2,1)S(1)}, bf16[8192,1024]{1,0:T(8,128)(2,1)}, u32[]{:S(2)}) copy-start(bf16[8192,1024]{1,0:T(8,128)(2,1)} %get-tuple-element.23.exp_ref) | copy-start | bytes 50331652

commit v2 on v1

v2 whole, which is shorter than its diff:
```python
import functools
import math

import jax
import jax.numpy as jnp
from jax import lax
from jax.experimental import pallas as pl
from jax.experimental.pallas import tpu as pltpu
from jax.sharding import Mesh
from jax.sharding import PartitionSpec as P


CLS = ("cls_0", "cls_1", "cls_2", "cls_3")
CHIP = ("cls_0", "cls_1", "cls_2")
CORE = "cls_3"

logit_scale = 64.0
cos_margin = math.cos(0.5)
sin_margin = math.sin(0.5)
epsilon = 1e-06

f32 = jnp.float32
bf16 = jnp.bfloat16


def swapped(x):
    return lax.ppermute(x, CORE, [(0, 1), (1, 0)])


def to_chips(x):
    return lax.all_to_all(x, CHIP, split_axis=0, concat_axis=0, tiled=True)


def from_chips(x):
    copies = jnp.broadcast_to(x, (lax.axis_size(CHIP), *x.shape))
    return lax.all_to_all(copies, CHIP, split_axis=0, concat_axis=0, tiled=True)


def inverse_norm(values, axis):
    return lax.rsqrt(jnp.sum(values * values, axis=axis, keepdims=True) + epsilon)


def margin(target_cos):
    target_sine = jnp.sqrt(1.0 - target_cos * target_cos)
    margined = target_cos * cos_margin - target_sine * sin_margin
    slope = cos_margin + sin_margin * target_cos / target_sine
    return margined, slope


def targets_kernel(steps, ids_ref, own_ref, other_ref, found_ref, wide_ids, total):
    i = pl.program_id(0)
    rows = own_ref.shape[0]
    samples = found_ref.shape[0]

    @pl.when(i == 0)
    def _():
        wide_ids[...] = jnp.broadcast_to(ids_ref[...], (128, samples)).T
        total[...] = jnp.zeros_like(total)

    ids = jnp.concatenate([wide_ids[...] - i * rows] * (rows // 128), axis=1)
    hit = jnp.where(lax.broadcasted_iota(jnp.int32, (samples, rows), 1) == ids, 1.0, 0.0).astype(bf16)

    @pl.when(i < steps)
    def _():
        total[...] += jnp.dot(hit, own_ref[...], preferred_element_type=f32)

    @pl.when(i >= steps)
    def _():
        total[...] += jnp.dot(hit, other_ref[...], preferred_element_type=f32)

    @pl.when(i == 2 * steps - 1)
    def _():
        found_ref[...] = total[...].astype(bf16)


def halves(rows, depth, steps):
    return [
        pl.BlockSpec((rows, depth), lambda i: (jnp.minimum(i, steps - 1), 0)),
        pl.BlockSpec((rows, depth), lambda i: (jnp.maximum(i - steps, 0), 0)),
    ]


def target_rows(ids, own, other, rows=512):
    count, depth = own.shape
    samples = ids.shape[1]
    steps = count // rows
    fixed = lambda i: (0, 0)
    return pl.pallas_call(
        functools.partial(targets_kernel, steps),
        grid=(2 * steps,),
        in_specs=[pl.BlockSpec((1, samples), fixed)] + halves(rows, depth, steps),
        out_specs=pl.BlockSpec((samples, depth), fixed),
        out_shape=jax.ShapeDtypeStruct((samples, depth), bf16),
        scratch_shapes=[pltpu.VMEM((samples, 128), jnp.int32), pltpu.VMEM((samples, depth), f32)],
        cost_estimate=pl.CostEstimate(
            flops=4 * count * depth * samples, bytes_accessed=4 * count * depth, transcendentals=0
        ),
        name="targets",
    )(ids, own, other)


def row_of(values):
    part = values[:, :128]
    for k in range(1, values.shape[1] // 128):
        part = part + values[:, k * 128 : (k + 1) * 128]
    return jnp.sum(part.T, axis=0, keepdims=True)


def exp_kernel(steps, sub, ids_ref, x_ref, found_ref, own_ref, other_ref, exp_ref, low_ref, emb_ref, goal_ref,
               sums_ref, cos_ref, wide_ids, scaled, row_sum):
    i = pl.program_id(0)
    rows = own_ref.shape[0]
    samples = x_ref.shape[0]

    @pl.when(i == 0)
    def _():
        wide_ids[...] = jnp.broadcast_to(ids_ref[...], (128, samples)).T
        x = x_ref[...].astype(f32)
        emb = (x * inverse_norm(x, 1)).astype(bf16)
        emb_ref[...] = emb
        scaled[...] = (emb * logit_scale).astype(bf16)
        row_sum[...] = jnp.zeros_like(row_sum)

    block = jnp.where(i < steps, own_ref[...], other_ref[...]).astype(f32)
    low = (block * inverse_norm(block, 1)).astype(bf16)
    low_ref[...] = low
    columns = lax.broadcasted_iota(jnp.int32, (sub, rows), 1)
    parts = samples // sub

    def products(s):
        return lax.dot_general(
            scaled[s * sub : (s + 1) * sub, :], low, (((1,), (1,)), ((), ())), preferred_element_type=f32
        )

    logits = products(0)
    for s in range(parts):
        span = slice(s * sub, (s + 1) * sub)
        later = products(s + 1) if s + 1 < parts else None
        ids = jnp.concatenate([wide_ids[span, :] - i * rows] * (rows // 128), axis=1)
        weight = jnp.where(columns == ids, 0.0, jnp.exp(logits))
        part = weight[:, :128]
        for k in range(1, rows // 128):
            part = part + weight[:, k * 128 : (k + 1) * 128]
        row_sum[span, :] += part
        exp_ref[span, :] = weight.astype(bf16)
        logits = later

    @pl.when(i == 2 * steps - 1)
    def _():
        found = found_ref[...].astype(f32)
        goal = (found * inverse_norm(found, 1)).astype(bf16)
        goal_ref[...] = goal
        target_cos = row_of(goal.astype(f32) * scaled[...].astype(f32)) * (1.0 / logit_scale)
        cos_ref[...] = target_cos
        margined, _ = margin(target_cos)
        here = jnp.where(ids_ref[...] >= 0, jnp.exp(logit_scale * margined), 0.0)
        sums_ref[...] = row_of(row_sum[...]) + here


def exponentials(ids, x, found, own, other, rows=512, sub=256):
    samples, depth = x.shape
    count = own.shape[0]
    steps = count // rows
    fixed = lambda i: (0, 0)
    return pl.pallas_call(
        functools.partial(exp_kernel, steps, sub),
        grid=(2 * steps,),
        in_specs=[
            pl.BlockSpec((1, samples), fixed),
            pl.BlockSpec((samples, depth), fixed),
            pl.BlockSpec((samples, depth), fixed),
        ]
        + halves(rows, depth, steps),
        out_specs=[
            pl.BlockSpec((samples, rows), lambda i: (0, i)),
            pl.BlockSpec((rows, depth), lambda i: (i, 0)),
            pl.BlockSpec((samples, depth), fixed),
            pl.BlockSpec((samples, depth), fixed),
            pl.BlockSpec((1, samples), fixed),
            pl.BlockSpec((1, samples), fixed),
        ],
        out_shape=[
            jax.ShapeDtypeStruct((samples, 2 * count), bf16),
            jax.ShapeDtypeStruct((2 * count, depth), bf16),
            jax.ShapeDtypeStruct((samples, depth), bf16),
            jax.ShapeDtypeStruct((samples, depth), bf16),
            jax.ShapeDtypeStruct((1, samples), f32),
            jax.ShapeDtypeStruct((1, samples), f32),
        ],
        scratch_shapes=[
            pltpu.VMEM((samples, 128), jnp.int32),
            pltpu.VMEM((samples, depth), bf16),
            pltpu.VMEM((samples, 128), f32),
        ],
        cost_estimate=pl.CostEstimate(
            flops=4 * count * depth * samples,
            bytes_accessed=8 * count * depth,
            transcendentals=2 * count * samples,
        ),
        name="exponentials",
    )(ids, x, found, own, other)


def pull_kernel(exp_ref, low_ref, out_ref):
    i = pl.program_id(0)
    product = jnp.dot(exp_ref[...], low_ref[...], preferred_element_type=f32)

    @pl.when(i == 0)
    def _():
        out_ref[...] = product

    @pl.when(i > 0)
    def _():
        out_ref[...] += product


def pulled(exps, low, rows=1024):
    samples = exps.shape[0]
    count, depth = low.shape
    return pl.pallas_call(
        pull_kernel,
        grid=(count // rows,),
        in_specs=[
            pl.BlockSpec((samples, rows), lambda i: (0, i)),
            pl.BlockSpec((rows, depth), lambda i: (i, 0)),
        ],
        out_specs=pl.BlockSpec((samples, depth), lambda i: (0, 0)),
        out_shape=jax.ShapeDtypeStruct((samples, depth), f32),
        cost_estimate=pl.CostEstimate(
            flops=2 * count * depth * samples, bytes_accessed=2 * count * (depth + samples), transcendentals=0
        ),
        name="pull",
    )(exps, low)


def push_kernel(base, final, ids_ref, patch_ref, emb_ref, exp_ref, *refs):
    i = pl.program_id(0)
    samples, rows = exp_ref.shape
    if final:
        c_ref, other_ref, out_ref, wide_ids, wide_patch = refs
    else:
        out_ref, wide_ids, wide_patch = refs

    @pl.when(i == 0)
    def _():
        wide_ids[...] = jnp.broadcast_to(ids_ref[...], (128, samples)).T
        wide_patch[...] = jnp.broadcast_to(patch_ref[...], (128, samples)).T

    ids = jnp.concatenate([wide_ids[...] - (base + i) * rows] * (rows // 128), axis=1)
    patch = jnp.concatenate([wide_patch[...]] * (rows // 128), axis=1)
    hit = lax.broadcasted_iota(jnp.int32, exp_ref.shape, 1) == ids
    weight = jnp.where(hit, patch, exp_ref[...].astype(f32)).astype(bf16)
    push = lax.dot_general(weight, emb_ref[...], (((0,), (0,)), ((), ())), preferred_element_type=f32)
    if final:
        push = push + other_ref[...].astype(f32)
        block = c_ref[...].astype(f32)
        inv = inverse_norm(block, 1)
        unit = block * inv
        push = (push - unit * jnp.sum(push * unit, axis=1, keepdims=True)) * inv
    out_ref[...] = push.astype(bf16)


def pushed(ids, patch, emb, exps, half, centers=None, other=None, rows=512):
    samples, depth = emb.shape
    count = exps.shape[1] // 2
    base = half * (count // rows)
    final = centers is not None
    fixed = lambda i: (0, 0)
    step = lambda i: (i, 0)
    extra = (centers, other) if final else ()
    return pl.pallas_call(
        functools.partial(push_kernel, base, final),
        grid=(count // rows,),
        in_specs=[
            pl.BlockSpec((1, samples), fixed),
            pl.BlockSpec((1, samples), fixed),
            pl.BlockSpec((samples, depth), fixed),
            pl.BlockSpec((samples, rows), lambda i: (0, base + i)),
        ]
        + [pl.BlockSpec((rows, depth), step)] * len(extra),
        out_specs=pl.BlockSpec((rows, depth), step),
        out_shape=jax.ShapeDtypeStruct((count, depth), bf16),
        scratch_shapes=[pltpu.VMEM((samples, 128), jnp.int32), pltpu.VMEM((samples, 128), f32)],
        cost_estimate=pl.CostEstimate(
            flops=2 * count * depth * samples, bytes_accessed=2 * count * samples, transcendentals=0
        ),
    )(ids, patch, emb, exps, *extra)


def step(features, fc_weight, centers, labels):
    own, wide = features.shape
    class_rows, depth = centers.shape
    chips = lax.axis_size(CHIP)
    chip = lax.axis_index(CHIP)
    core = lax.axis_index(CORE)
    samples = chips * own

    other_centers = swapped(centers)
    embedded = jnp.dot(features, fc_weight, preferred_element_type=f32).astype(bf16)
    x = from_chips(embedded).reshape(samples, depth)

    by_core = labels.reshape(chips, 2, own)
    my_labels = jnp.where(core == 0, by_core[:, 0], by_core[:, 1]).reshape(1, samples)
    local = my_labels - chip * (2 * class_rows)
    inside = (local >= 0) & (local < 2 * class_rows)
    turned_ids = jnp.where(core == 0, local, (local + class_rows) % (2 * class_rows))
    ids = jnp.where(inside, turned_ids, -1)

    split = features.reshape(own, chips, 2, wide // (2 * chips))
    mine = jnp.where(core == 0, split[:, :, 0], split[:, :, 1])
    theirs = jnp.where(core == 0, split[:, :, 1], split[:, :, 0])
    fcols = mine.shape[-1]
    pad = ((0, 0), (0, 0), (0, 128 - fcols))
    cargo = jnp.concatenate([jnp.pad(mine.swapaxes(0, 1), pad), jnp.pad(theirs.swapaxes(0, 1), pad)], axis=2)

    found = target_rows(ids, centers, other_centers)
    exps, low, emb_low, goal, part_sums, target_cos = exponentials(ids, x, found, centers, other_centers)
    margined, slope = margin(target_cos)
    target_exp = jnp.exp(logit_scale * margined)
    goal_logit = jnp.where(ids >= 0, logit_scale * margined, 0.0).reshape(chips, 1, own)
    report = jnp.concatenate(
        [jnp.broadcast_to(part_sums, (chips, 1, samples)), jnp.pad(goal_logit, ((0, 0), (0, 0), (0, 128 - own)))],
        axis=2,
    )
    report = to_chips(report)
    pull = pulled(exps, low)
    report = jnp.sum(report, axis=0)
    sums = report[:, :samples]

    patch = slope * (target_exp - sums)
    scale = logit_scale / sums
    scale_column = scale.reshape(samples, 1)
    at_target = jnp.where(ids >= 0, scale * patch, 0.0).reshape(samples, 1)
    pull = (pull * scale_column + at_target * goal.astype(f32)).astype(bf16)
    scaled = (emb_low.astype(f32) * scale_column).astype(bf16)
    parcel = jnp.concatenate([pull.reshape(chips, own, depth), cargo], axis=2)
    parcel = to_chips(parcel)

    other_push = pushed(ids, patch, scaled, exps, 1)
    other_push = swapped(other_push)
    grad_centers = pushed(ids, patch, scaled, exps, 0, centers, other_push)

    own_float = embedded.astype(f32)
    inv_emb = inverse_norm(own_float, 1)
    emb_dir = own_float * inv_emb
    grad_dir = jnp.sum(parcel[:, :, :depth].astype(f32), axis=0)
    grad_emb = (
        (grad_dir - emb_dir * jnp.sum(grad_dir * emb_dir, axis=1, keepdims=True)) * inv_emb
    ).astype(bf16)
    grads = from_chips(grad_emb).reshape(samples, depth)

    columns = parcel[:, :, depth:].reshape(samples, 256)
    both = lax.dot_general(columns, grads, (((0,), (0,)), ((), ())), preferred_element_type=f32)
    theirs_fc = swapped(both[128 : 128 + fcols])
    grad_fc = both[:fcols] + theirs_fc
    own_sums = lax.dynamic_slice_in_dim(sums.reshape(samples), chip * own, own)
    loss = jnp.log(own_sums) - report[0, samples : samples + own]
    return (loss, grad_centers, grad_fc)


def solution(mesh):
    torus = Mesh(mesh.devices.reshape(4, 4, 4, 2), CLS)
    placed = (P(CLS, None), P(), P(CLS, None), P())
    return jax.shard_map(
        step,
        mesh=torus,
        in_specs=placed,
        out_specs=(P(CLS), P(CLS, None), P(CLS, None)),
        check_vma=False,
    )
```

time: 213 us -> 194 us (0.911)
  local copies, waits for them, and re-layouts: 34.6 us -> 6.8 us
  Pallas kernels: 65.4 us -> 83.5 us
  starting transfers between devices: 49.3 us -> 42 us
  waiting for transfers between devices: 43 us -> 40 us
    unnamed x26 -> x11, local copies, waits for them, and re-layouts: 24.5 us -> 1.6 us
    pallas_call x3, Pallas kernels: 48.4 us -> 59.1 us  [the longest x1 24.7 us: exponentials(): pl.pallas_call(functools.partial(exp_kernel, steps, sub), grid=(2 * steps...]
    all_to_all x3 -> x2, starting transfers between devices: 26.7 us -> 16.4 us  [from_chips(): return lax.all_to_all(copies, CHIP, split_axis=0, concat_axis=0, tiled=True)]
    pallas_call x2, Pallas kernels: 17 us -> 24.5 us  [pushed(): pl.pallas_call(functools.partial(push_kernel, base, final), grid=(count /...]
    all_to_all x2, starting transfers between devices: 15.7 us -> 19.8 us  [to_chips(): return lax.all_to_all(x, CHIP, split_axis=0, concat_axis=0, tiled=True)]
    all_to_all x3 -> x2, waiting for transfers between devices: 20.3 us -> 16.3 us  [from_chips(): return lax.all_to_all(copies, CHIP, split_axis=0, concat_axis=0, tiled=True)]
    reduce_sum x5 -> x3, other arithmetic: 4.31 us -> 0.56 us  [the longest x1 0.2 us: step(): report = jnp.sum(report, axis=0)]
    slice x3 -> x2, local copies, waits for them, and re-layouts: 3.35 us -> 0.05 us  [the longest x1 0.04 us: step(): columns = parcel[:, :, depth:].reshape(samples, 256)]
  transfers between devices with their start and end apart: 8 -> 7, of which waited for: 4 -> 3; matrix products, arithmetic and copies ran while one was open for 13% -> 10% of each run, Pallas kernels for 13% -> 18%
where the time goes in v2:
time: 194 us; the launch traced here: 192 us
  Pallas kernels  83.5 us (43%)
  starting transfers between devices  42 us (22%)
  waiting for transfers between devices  40 us (21%)
  other arithmetic  11.1 us (6%)
  matrix products  8.14 us (4%)
  local copies, waits for them, and re-layouts  6.8 us (4%)
    pallas_call x1, Pallas kernels, exponentials(): pl.pallas_call(functools.partial(exp_kernel, steps, sub), grid=(2 * steps...  24.7 us
    pallas_call x2, Pallas kernels, pushed(): pl.pallas_call(functools.partial(push_kernel, base, final), grid=(count /...  24.5 us
    all_to_all x2, waiting for transfers between devices, to_chips(): return lax.all_to_all(x, CHIP, split_axis=0, concat_axis=0, tiled=True)  23.1 us
    all_to_all x2, starting transfers between devices, to_chips(): return lax.all_to_all(x, CHIP, split_axis=0, concat_axis=0, tiled=True)  19.8 us
    pallas_call x1, Pallas kernels, target_rows(): pl.pallas_call(functools.partial(targets_kernel, steps), grid=(2 * steps,...  18.2 us
    all_to_all x2, starting transfers between devices, from_chips(): return lax.all_to_all(copies, CHIP, split_axis=0, concat_axis=0, tiled=True)  16.4 us
    all_to_all x2, waiting for transfers between devices, from_chips(): return lax.all_to_all(copies, CHIP, split_axis=0, concat_axis=0, tiled=True)  16.3 us
    pallas_call x1, Pallas kernels, pulled(): pl.pallas_call(pull_kernel, grid=(count // rows,), in_specs=[pl.BlockSpec...  16.3 us
  transfers between devices with their start and end apart: 7, of which 3 were waited for; matrix products, arithmetic and copies ran while one was open for 10% of the time, Pallas kernels for 18%

profile of v2, /device:TPU:1, one launch (start us, length us, event | category | flops | bytes accessed | tf_op | source)
XLA Modules:
  0.0 192.3 jit_solution(2140643095323214076)
XLA Ops:
  0.6 1.5 collective-permute-start
  2.1 6.7 %fusion.13 = (f32[16]{0:T(128)S(1)}, bf16[16,512]{1,0:T(8,128)(2,1)S(1)}) fusion(bf16[16,12544]{1,0:T(8,128)(2,1)} %param.4, bf16[12544,512]{1,0:T(8,128)(2,1)} %param.5), kind=kOutput, calls=%fused_computation.30 | convolution fusion | flops 205553648 | bytes 13262912 | tf_op jit(solution)/shard_map/dot_general | solution.py:299
  8.8 0.0 copy-start
  8.8 0.0 copy-start.4
  8.8 1.1 broadcast_in_dim.21
  9.9 11.2 %all-to-all-start = ((bf16[64,16,512]{2,1,0:T(8,128)(2,1)}), bf16[64,16,512]{2,1,0:T(8,128)(2,1)S(1)}, u32[]{:S(2)}, u32[]{:S(2)}) async-start(bf16[64,16,512]{2,1,0:T(8,128)(2,1)} %broadcast_in_dim.21), calls=%async_computation | async-start | bytes 2097152 | tf_op jit(solution)/shard_map/all_to_all | solution.py:36
  21.1 0.0 copy-done
  21.2 1.9 %reshape.152 = bf16[16,64,2,98]{3,2,1,0:T(2,128)(2,1)S(1)} reshape(bf16[16,12544]{1,0:T(8,128)(2,1)S(1)} %copy-done) | data formatting | bytes 802816 | tf_op jit(solution)/shard_map/reshape | solution.py:309
  23.1 0.0 copy-done.4
  23.1 0.1 reshape.148
  23.3 1.2 broadcast_select_fusion.1
  24.5 0.1 fusion.15
  24.6 0.1 sub.44
  24.7 0.6 and_select_fusion.1.ids_ref
  25.3 0.0 collective-permute-done.other_ref
  25.3 18.2 %targets.1.found_ref = bf16[1024,512]{1,0:T(8,128)(2,1)} custom-call(s32[1,1024]{1,0:T(1,128)} %and_select_fusion.1.ids_ref, bf16[4096,512]{1,0:T(8,128)(2,1)} %refs_0_.1, bf16[4096,512]{1,0:T(8,128)(2,1)} %collective-permute-done.other_ref), custom_call_target="tpu_custom_call" | custom-call | flops 8589934592 | bytes 8388608 | tf_op jit(solution)/shard_map/targets/pallas_call | solution.py:88
  43.5 0.0 all-to-all-done
  43.5 1.0 copy-done.1
  44.5 24.7 %exponentials.1 = (bf16[1024,8192]{1,0:T(8,128)(2,1)}, bf16[8192,512]{1,0:T(8,128)(2,1)}, bf16[1024,512]{1,0:T(8,128)(2,1)}, bf16[1024,512]{1,0:T(8,128)(2,1)}, f32[1,1024]{1,0:T(1,128)}, /*index=5*/f32[1,1024]{1,0:T(1,128)}) custom-call(s32[1,1024]{1,0:T(1,128)} %and_select_fusion.1.ids_ref, bf16[1024,512]{1,0:T(8,128)(2,1)} %bitcast.23, ...), custom_call_target="tpu_custom_call" | custom-call | flops 8589934592 | bytes 16777216 | tf_op jit(solution)/shard_map/exponentials/pallas_call | solution.py:165
  69.2 0.7 fusion.16
  69.9 0.1 reshape.150
  70.0 0.7 pad.17.clone
  70.7 0.9 pad_maximum_fusion
  71.6 10.0 %all-to-all-start.1 = ((f32[64,1,1152]{2,1,0:T(1,128)}), f32[64,1,1152]{2,1,0:T(1,128)S(1)}, u32[]{:S(2)}, u32[]{:S(2)}) async-start(f32[64,1,1152]{2,1,0:T(1,128)} %pad_maximum_fusion), calls=%async_computation.1 | async-start | bytes 589824 | tf_op jit(solution)/shard_map/all_to_all | solution.py:31
  81.6 16.3 %pull.1 = f32[1024,512]{1,0:T(8,128)} custom-call(bf16[1024,8192]{1,0:T(8,128)(2,1)} %get-tuple-element.12.exp_ref, bf16[8192,512]{1,0:T(8,128)(2,1)} %get-tuple-element.13.low_ref), custom_call_target="tpu_custom_call" | custom-call | flops 8589934592 | bytes 25165824 | tf_op jit(solution)/shard_map/pull/pallas_call | solution.py:220
  97.8 0.0 all-to-all-done.1
  97.8 0.2 reduce_sum.38
  98.0 0.7 compare_select_fusion.2
  98.7 3.5 %add_convert_fusion = (bf16[1024,512]{1,0:T(8,128)(2,1)S(1)}, bf16[1024,512]{1,0:T(8,128)(2,1)}) fusion(bf16[1024,512]{1,0:T(8,128)(2,1)} %get-tuple-element.14, f32[1024,512]{1,0:T(8,128)} %pull.1, f32[1024]{0:T(1024)S(1)} %bitcast.25, f32[1024]{0:T(1024)S(1)} %bitcast.26, bf16[1024,512]{1,0:T(8,128)(2,1)S(1)} %copy-done.2), kind=kLoop, calls=%fused_computation.7 | loop fusion | flops 4194304 | bytes 6299648 | tf_op jit(solution)/shard_map/convert_element_type | solution.py:334
  102.2 11.0 %shard_map.67 = bf16[4096,512]{1,0:T(8,128)(2,1)} custom-call(s32[1,1024]{1,0:T(1,128)} %and_select_fusion.1.ids_ref, f32[1,1024]{1,0:T(1,128)} %get-tuple-element.17.patch_ref, bf16[1024,512]{1,0:T(8,128)(2,1)} %get-tuple-element.22.emb_ref, bf16[1024,8192]{1,0:T(8,128)(2,1)} %get-tuple-element.12.exp_ref), custom_call_target="tpu_custom_call" | custom-call | flops 4294967296 | bytes 8388608 | tf_op jit(solution)/shard_map/pallas_call | solution.py:271
  113.2 0.9 collective-permute-start.1
  114.0 0.6 copy_bitcast_fusion
  114.7 1.4 fusion.4
  116.1 9.9 %all-to-all-start.2 = ((bf16[64,16,768]{2,1,0:T(8,128)(2,1)}), bf16[64,16,768]{2,1,0:T(8,128)(2,1)S(1)}, u32[]{:S(2)}, u32[]{:S(2)}) async-start(bf16[64,16,768]{2,1,0:T(8,128)(2,1)} %fusion.4), calls=%async_computation.2 | async-start | bytes 3145728 | tf_op jit(solution)/shard_map/all_to_all | solution.py:31
  126.0 23.1 %all-to-all-done.2 = bf16[64,16,768]{2,1,0:T(8,128)(2,1)S(1)} async-done(((bf16[64,16,768]{2,1,0:T(8,128)(2,1)}), bf16[64,16,768]{2,1,0:T(8,128)(2,1)S(1)}, u32[]{:S(2)}, u32[]{:S(2)}) %all-to-all-start.2) | async-done | bytes 1572896 | tf_op jit(solution)/shard_map/all_to_all | solution.py:31
  149.1 0.2 convert_reduce_fusion
  149.3 0.2 fusion.9
  149.5 0.1 fusion.12
  149.5 1.1 broadcast_in_dim.24
  150.7 5.2 %all-to-all-start.3 = ((bf16[64,16,512]{2,1,0:T(8,128)(2,1)}), bf16[64,16,512]{2,1,0:T(8,128)(2,1)S(1)}, u32[]{:S(2)}, u32[]{:S(2)}) async-start(bf16[64,16,512]{2,1,0:T(8,128)(2,1)} %broadcast_in_dim.24), calls=%async_computation.3 | async-start | bytes 2097152 | tf_op jit(solution)/shard_map/all_to_all | solution.py:36
  155.9 16.3 %all-to-all-done.3 = bf16[64,16,512]{2,1,0:T(8,128)(2,1)S(1)} async-done(((bf16[64,16,512]{2,1,0:T(8,128)(2,1)}), bf16[64,16,512]{2,1,0:T(8,128)(2,1)S(1)}, u32[]{:S(2)}, u32[]{:S(2)}) %all-to-all-start.3) | async-done | bytes 1048608 | tf_op jit(solution)/shard_map/all_to_all | solution.py:36
  172.2 1.5 convolution_bitcast_fusion
  173.7 3.4 %collective-permute-start.2 = (f32[98,512]{1,0:T(8,128)S(1)}, f32[98,512]{1,0:T(8,128)S(1)}, u32[]{:S(2)}, u32[]{:S(2)}) collective-permute-start(f32[98,512]{1,0:T(8,128)S(1)} %slice.51), channel_id=1, source_target_pairs={{0,1},{1,0},{2,3},{3,2},{4,5},{5,4},{6,7},{7,6},{8,9},{9,8},{10,11... | collective-permute-start | bytes 602120 | tf_op jit(solution)/shard_map/ppermute | solution.py:27
  177.1 0.6 fusion.18
  177.7 0.5 collective-permute-done.2
  178.2 0.7 slice_add_fusion
  178.9 0.0 collective-permute-done.1.refs_1_
  178.9 13.4 %shard_map.68 = bf16[4096,512]{1,0:T(8,128)(2,1)} custom-call(s32[1,1024]{1,0:T(1,128)} %and_select_fusion.1.ids_ref, f32[1,1024]{1,0:T(1,128)} %get-tuple-element.17.patch_ref, bf16[1024,512]{1,0:T(8,128)(2,1)} %get-tuple-element.22.emb_ref, bf16[1024,8192]{1,0:T(8,128)(2,1)} %get-tuple-element.12.exp_ref, bf16[4096,512]{1,0:T(8,128)(2,1)} %refs_0_.1, ...), custom_call_target="tpu_custom_call" | custom-call | flops 4294967296 | bytes 8388608 | tf_op jit(solution)/shard_map/pallas_call | solution.py:271
  (10 shorter events, 0.1 us)
Async XLA Ops:
  0.6 24.7 %collective-permute-start = (bf16[4096,512]{1,0:T(8,128)(2,1)}, bf16[4096,512]{1,0:T(8,128)(2,1)}, u32[]{:S(2)}, u32[]{:S(2)}) collective-permute-start(bf16[4096,512]{1,0:T(8,128)(2,1)} %refs_0_.1), channel_id=1, source_target_pairs={{0,1},{1,0},{2,3},{3,2},{4,5},{5,4},{6,7},{7,6},{8,9},{9,8},{10,11... | collective-permute-start | bytes 12582920 | tf_op jit(solution)/shard_map/ppermute | solution.py:27
  8.8 12.4 %copy-start = (bf16[16,12544]{1,0:T(8,128)(2,1)S(1)}, bf16[16,12544]{1,0:T(8,128)(2,1)}, u32[]{:S(2)}) copy-start(bf16[16,12544]{1,0:T(8,128)(2,1)} %param.4) | copy-start | bytes 1204228
  8.8 14.3 %copy-start.4 = (s32[2048]{0:T(1024)S(1)}, s32[2048]{0:T(1024)}, u32[]{:S(2)}) copy-start(s32[2048]{0:T(1024)} %param.7) | copy-start | bytes 24580
  9.9 33.6 %all-to-all-start = ((bf16[64,16,512]{2,1,0:T(8,128)(2,1)}), bf16[64,16,512]{2,1,0:T(8,128)(2,1)S(1)}, u32[]{:S(2)}, u32[]{:S(2)}) async-start(bf16[64,16,512]{2,1,0:T(8,128)(2,1)} %broadcast_in_dim.21), calls=%async_computation | async-start | bytes 2097152 | tf_op jit(solution)/shard_map/all_to_all | solution.py:36
  43.5 1.0 copy-start.1
  71.6 26.2 %all-to-all-start.1 = ((f32[64,1,1152]{2,1,0:T(1,128)}), f32[64,1,1152]{2,1,0:T(1,128)S(1)}, u32[]{:S(2)}, u32[]{:S(2)}) async-start(f32[64,1,1152]{2,1,0:T(1,128)} %pad_maximum_fusion), calls=%async_computation.1 | async-start | bytes 589824 | tf_op jit(solution)/shard_map/all_to_all | solution.py:31
  81.5 16.5 %copy-start.3 = (f32[1,1024]{1,0:T(1,128)S(1)}, f32[1,1024]{1,0:T(1,128)}, u32[]{:S(2)}) copy-start(f32[1,1024]{1,0:T(1,128)} %get-tuple-element.10) | copy-start | bytes 12292
  81.6 17.1 %copy-start.2 = (bf16[1024,512]{1,0:T(8,128)(2,1)S(1)}, bf16[1024,512]{1,0:T(8,128)(2,1)}, u32[]{:S(2)}) copy-start(bf16[1024,512]{1,0:T(8,128)(2,1)} %get-tuple-element.11) | copy-start | bytes 3145732
  113.2 65.7 %collective-permute-start.1 = (bf16[4096,512]{1,0:T(8,128)(2,1)}, bf16[4096,512]{1,0:T(8,128)(2,1)}, u32[]{:S(2)}, u32[]{:S(2)}) collective-permute-start(bf16[4096,512]{1,0:T(8,128)(2,1)} %shard_map.67), channel_id=1, source_target_pairs={{0,1},{1,0},{2,3},{3,2},{4,5},{5,4},{6,7},{7,6},{8,9},{9,8},{10,11... | collective-permute-start | bytes 12582920 | tf_op jit(solution)/shard_map/ppermute | solution.py:27
  116.1 33.0 %all-to-all-start.2 = ((bf16[64,16,768]{2,1,0:T(8,128)(2,1)}), bf16[64,16,768]{2,1,0:T(8,128)(2,1)S(1)}, u32[]{:S(2)}, u32[]{:S(2)}) async-start(bf16[64,16,768]{2,1,0:T(8,128)(2,1)} %fusion.4), calls=%async_computation.2 | async-start | bytes 3145728 | tf_op jit(solution)/shard_map/all_to_all | solution.py:31
  150.7 21.5 %all-to-all-start.3 = ((bf16[64,16,512]{2,1,0:T(8,128)(2,1)}), bf16[64,16,512]{2,1,0:T(8,128)(2,1)S(1)}, u32[]{:S(2)}, u32[]{:S(2)}) async-start(bf16[64,16,512]{2,1,0:T(8,128)(2,1)} %broadcast_in_dim.24), calls=%async_computation.3 | async-start | bytes 2097152 | tf_op jit(solution)/shard_map/all_to_all | solution.py:36
  173.7 4.5 %collective-permute-start.2 = (f32[98,512]{1,0:T(8,128)S(1)}, f32[98,512]{1,0:T(8,128)S(1)}, u32[]{:S(2)}, u32[]{:S(2)}) collective-permute-start(f32[98,512]{1,0:T(8,128)S(1)} %slice.51), channel_id=1, source_target_pairs={{0,1},{1,0},{2,3},{3,2},{4,5},{5,4},{6,7},{7,6},{8,9},{9,8},{10,11... | collective-permute-start | bytes 602120 | tf_op jit(solution)/shard_map/ppermute | solution.py:27

commit v3 on v2

--- a/solution.py
+++ b/solution.py
@@ -47,56 +47,66 @@
     return margined, slope
 
 
-def targets_kernel(steps, ids_ref, own_ref, other_ref, found_ref, wide_ids, total):
-    i = pl.program_id(0)
-    rows = own_ref.shape[0]
-    samples = found_ref.shape[0]
-
-    @pl.when(i == 0)
-    def _():
-        wide_ids[...] = jnp.broadcast_to(ids_ref[...], (128, samples)).T
-        total[...] = jnp.zeros_like(total)
-
-    ids = jnp.concatenate([wide_ids[...] - i * rows] * (rows // 128), axis=1)
-    hit = jnp.where(lax.broadcasted_iota(jnp.int32, (samples, rows), 1) == ids, 1.0, 0.0).astype(bf16)
-
-    @pl.when(i < steps)
-    def _():
-        total[...] += jnp.dot(hit, own_ref[...], preferred_element_type=f32)
-
-    @pl.when(i >= steps)
-    def _():
-        total[...] += jnp.dot(hit, other_ref[...], preferred_element_type=f32)
-
-    @pl.when(i == 2 * steps - 1)
-    def _():
-        found_ref[...] = total[...].astype(bf16)
-
-
-def halves(rows, depth, steps):
-    return [
-        pl.BlockSpec((rows, depth), lambda i: (jnp.minimum(i, steps - 1), 0)),
-        pl.BlockSpec((rows, depth), lambda i: (jnp.maximum(i - steps, 0), 0)),
+ANY = pl.BlockSpec(memory_space=pl.ANY)
+VMEM = pl.BlockSpec(memory_space=pltpu.VMEM)
+SMEM = pl.BlockSpec(memory_space=pltpu.SMEM)
+
+
+def targets_kernel(batch, ids_ref, busy_ref, own_ref, other_ref, goal_ref, centers, found, sems):
+    count, depth = own_ref.shape
+    copies = [
+        pltpu.make_async_copy(part, centers.at[pl.ds(k * count, count)], sems.at[k])
+        for k, part in enumerate((own_ref, other_ref))
     ]
-
-
-def target_rows(ids, own, other, rows=512):
+    for copy in copies:
+        copy.start()
+    found[...] = jnp.zeros_like(found)
+    for copy in copies:
+        copy.wait()
+    spot = lax.broadcasted_iota(jnp.int32, (16, depth), 0)
+
+    def group(g, carry):
+        @pl.when(busy_ref[g] >= 0)
+        def _():
+            def sample(b, carry):
+                at = g * batch + b
+                row = ids_ref[at]
+
+                @pl.when(row >= 0)
+                def _():
+                    near = centers[pl.ds(pl.multiple_of(row // 16 * 16, 16), 16), :].astype(f32)
+                    found[pl.ds(at, 1), :] = jnp.sum(jnp.where(spot == row % 16, near, 0.0), axis=0, keepdims=True)
+
+                return carry
+
+            lax.fori_loop(0, batch, sample, 0)
+
+        return carry
+
+    lax.fori_loop(0, busy_ref.shape[0], group, 0)
+    rows = found[...]
+    goal_ref[...] = (rows * inverse_norm(rows, 1)).astype(bf16)
+
+
+def target_directions(ids, batch, own, other):
     count, depth = own.shape
-    samples = ids.shape[1]
-    steps = count // rows
-    fixed = lambda i: (0, 0)
+    samples = ids.shape[0]
+    busy = jnp.max(ids.reshape(samples // batch, batch), axis=1)
     return pl.pallas_call(
-        functools.partial(targets_kernel, steps),
-        grid=(2 * steps,),
-        in_specs=[pl.BlockSpec((1, samples), fixed)] + halves(rows, depth, steps),
-        out_specs=pl.BlockSpec((samples, depth), fixed),
+        functools.partial(targets_kernel, batch),
+        in_specs=[SMEM, SMEM, ANY, ANY],
+        out_specs=VMEM,
         out_shape=jax.ShapeDtypeStruct((samples, depth), bf16),
-        scratch_shapes=[pltpu.VMEM((samples, 128), jnp.int32), pltpu.VMEM((samples, depth), f32)],
+        scratch_shapes=[
+            pltpu.VMEM((2 * count, depth), bf16),
+            pltpu.VMEM((samples, depth), f32),
+            pltpu.SemaphoreType.DMA((2,)),
+        ],
         cost_estimate=pl.CostEstimate(
-            flops=4 * count * depth * samples, bytes_accessed=4 * count * depth, transcendentals=0
+            flops=2 * count * depth * samples, bytes_accessed=4 * count * depth, transcendentals=0
         ),
         name="targets",
-    )(ids, own, other)
+    )(ids, busy, own, other)
 
 
 def row_of(values):
@@ -106,11 +116,12 @@
     return jnp.sum(part.T, axis=0, keepdims=True)
 
 
-def exp_kernel(steps, sub, ids_ref, x_ref, found_ref, own_ref, other_ref, exp_ref, low_ref, emb_ref, goal_ref,
-               sums_ref, cos_ref, wide_ids, scaled, row_sum):
+def exp_kernel(steps, early, lanes, ids_ref, x_ref, goal_ref, own_ref, other_ref, exp_ref, low_ref, pull_ref, emb_ref,
+               sums_ref, cos_ref, wide_ids, scaled, row_sum, total):
     i = pl.program_id(0)
     rows = own_ref.shape[0]
     samples = x_ref.shape[0]
+    sub = samples // lanes
 
     @pl.when(i == 0)
     def _():
@@ -120,60 +131,77 @@
         emb_ref[...] = emb
         scaled[...] = (emb * logit_scale).astype(bf16)
         row_sum[...] = jnp.zeros_like(row_sum)
-
-    block = jnp.where(i < steps, own_ref[...], other_ref[...]).astype(f32)
-    low = (block * inverse_norm(block, 1)).astype(bf16)
-    low_ref[...] = low
-    columns = lax.broadcasted_iota(jnp.int32, (sub, rows), 1)
-    parts = samples // sub
-
-    def products(s):
-        return lax.dot_general(
-            scaled[s * sub : (s + 1) * sub, :], low, (((1,), (1,)), ((), ())), preferred_element_type=f32
-        )
-
-    logits = products(0)
-    for s in range(parts):
-        span = slice(s * sub, (s + 1) * sub)
-        later = products(s + 1) if s + 1 < parts else None
-        ids = jnp.concatenate([wide_ids[span, :] - i * rows] * (rows // 128), axis=1)
-        weight = jnp.where(columns == ids, 0.0, jnp.exp(logits))
-        part = weight[:, :128]
-        for k in range(1, rows // 128):
-            part = part + weight[:, k * 128 : (k + 1) * 128]
-        row_sum[span, :] += part
-        exp_ref[span, :] = weight.astype(bf16)
-        logits = later
+        total[...] = jnp.zeros_like(total)
+
+    def chunk(with_pull):
+        block = jnp.where(i < steps, own_ref[...], other_ref[...]).astype(f32)
+        low_ref[...] = (block * inverse_norm(block, 1)).astype(bf16)
+        columns = lax.broadcasted_iota(jnp.int32, (sub, 128), 1)
+
+        def products(m):
+            return lax.dot_general(
+                scaled[m * sub : (m + 1) * sub, :],
+                low_ref[...],
+                (((1,), (1,)), ((), ())),
+                preferred_element_type=f32,
+            )
+
+        logits = products(0)
+        for m in range(lanes):
+            later = products(m + 1) if m + 1 < lanes else None
+            span = slice(m * sub, (m + 1) * sub)
+            ids = wide_ids[span, :] - i * rows
+            part = None
+            for t in range(rows // 128):
+                weight = jnp.exp(logits[:, t * 128 : (t + 1) * 128])
+                weight = jnp.where(columns + t * 128 == ids, 0.0, weight)
+                part = weight if part is None else part + weight
+                exp_ref[span, t * 128 : (t + 1) * 128] = weight.astype(bf16)
+            row_sum[span, :] += part
+            if with_pull:
+                total[span, :] += jnp.dot(exp_ref[span, :], low_ref[...], preferred_element_type=f32)
+            logits = later
+
+    @pl.when(i < early)
+    def _():
+        chunk(True)
+
+    @pl.when(i >= early)
+    def _():
+        chunk(False)
+
+    @pl.when(i == early)
+    def _():
+        pull_ref[...] = total[...]
 
     @pl.when(i == 2 * steps - 1)
     def _():
-        found = found_ref[...].astype(f32)
-        goal = (found * inverse_norm(found, 1)).astype(bf16)
-        goal_ref[...] = goal
-        target_cos = row_of(goal.astype(f32) * scaled[...].astype(f32)) * (1.0 / logit_scale)
+        target_cos = row_of(goal_ref[...].astype(f32) * scaled[...].astype(f32)) * (1.0 / logit_scale)
         cos_ref[...] = target_cos
         margined, _ = margin(target_cos)
         here = jnp.where(ids_ref[...] >= 0, jnp.exp(logit_scale * margined), 0.0)
         sums_ref[...] = row_of(row_sum[...]) + here
 
 
-def exponentials(ids, x, found, own, other, rows=512, sub=256):
+def exponentials(ids, x, goal, own, other, early, rows=1024, lanes=2):
     samples, depth = x.shape
     count = own.shape[0]
     steps = count // rows
+    late = 2 * steps - early
     fixed = lambda i: (0, 0)
     return pl.pallas_call(
-        functools.partial(exp_kernel, steps, sub),
+        functools.partial(exp_kernel, steps, early, lanes),
         grid=(2 * steps,),
         in_specs=[
             pl.BlockSpec((1, samples), fixed),
             pl.BlockSpec((samples, depth), fixed),
             pl.BlockSpec((samples, depth), fixed),
-        ]
-        + halves(rows, depth, steps),
+            pl.BlockSpec((rows, depth), lambda i: (jnp.minimum(i, steps - 1), 0)),
+            pl.BlockSpec((rows, depth), lambda i: (jnp.maximum(i - steps, 0), 0)),
+        ],
         out_specs=[
             pl.BlockSpec((samples, rows), lambda i: (0, i)),
-            pl.BlockSpec((rows, depth), lambda i: (i, 0)),
+            pl.BlockSpec((rows, depth), lambda i: (jnp.maximum(i - early, 0), 0)),
             pl.BlockSpec((samples, depth), fixed),
             pl.BlockSpec((samples, depth), fixed),
             pl.BlockSpec((1, samples), fixed),
@@ -181,8 +209,8 @@
         ],
         out_shape=[
             jax.ShapeDtypeStruct((samples, 2 * count), bf16),
-            jax.ShapeDtypeStruct((2 * count, depth), bf16),
-            jax.ShapeDtypeStruct((samples, depth), bf16),
+            jax.ShapeDtypeStruct((late * rows, depth), bf16),
+            jax.ShapeDtypeStruct((samples, depth), f32),
             jax.ShapeDtypeStruct((samples, depth), bf16),
             jax.ShapeDtypeStruct((1, samples), f32),
             jax.ShapeDtypeStruct((1, samples), f32),
@@ -191,6 +219,7 @@
             pltpu.VMEM((samples, 128), jnp.int32),
             pltpu.VMEM((samples, depth), bf16),
             pltpu.VMEM((samples, 128), f32),
+            pltpu.VMEM((samples, depth), f32),
         ],
         cost_estimate=pl.CostEstimate(
             flops=4 * count * depth * samples,
@@ -198,39 +227,55 @@
             transcendentals=2 * count * samples,
         ),
         name="exponentials",
-    )(ids, x, found, own, other)
-
-
-def pull_kernel(exp_ref, low_ref, out_ref):
-    i = pl.program_id(0)
-    product = jnp.dot(exp_ref[...], low_ref[...], preferred_element_type=f32)
-
-    @pl.when(i == 0)
-    def _():
-        out_ref[...] = product
-
-    @pl.when(i > 0)
-    def _():
-        out_ref[...] += product
-
-
-def pulled(exps, low, rows=1024):
+    )(ids, x, goal, own, other)
+
+
+def pull_kernel(early, rows, exp_ref, low_ref, start_ref, out_ref, exps, lows, exp_sems, low_sems, start_sem):
+    steps = low_ref.shape[0] // rows
+    start = pltpu.make_async_copy(start_ref, out_ref, start_sem)
+
+    def fetch(i, slot):
+        return (
+            pltpu.make_async_copy(
+                exp_ref.at[:, pl.ds((early + i) * rows, rows)], exps.at[slot], exp_sems.at[slot]
+            ),
+            pltpu.make_async_copy(low_ref.at[pl.ds(i * rows, rows)], lows.at[slot], low_sems.at[slot]),
+        )
+
+    for i in range(steps):
+        for copy in fetch(i, i):
+            copy.start()
+        if i == 0:
+            start.start()
+    for i in range(steps):
+        for copy in fetch(i, i):
+            copy.wait()
+        if i == 0:
+            start.wait()
+        out_ref[...] += jnp.dot(exps[i], lows[i], preferred_element_type=f32)
+
+
+def pulled(exps, low, start, early, rows=1024):
     samples = exps.shape[0]
     count, depth = low.shape
+    steps = count // rows
     return pl.pallas_call(
-        pull_kernel,
-        grid=(count // rows,),
-        in_specs=[
-            pl.BlockSpec((samples, rows), lambda i: (0, i)),
-            pl.BlockSpec((rows, depth), lambda i: (i, 0)),
-        ],
-        out_specs=pl.BlockSpec((samples, depth), lambda i: (0, 0)),
+        functools.partial(pull_kernel, early, rows),
+        in_specs=[ANY, ANY, ANY],
+        out_specs=VMEM,
         out_shape=jax.ShapeDtypeStruct((samples, depth), f32),
+        scratch_shapes=[
+            pltpu.VMEM((steps, samples, rows), bf16),
+            pltpu.VMEM((steps, rows, depth), bf16),
+            pltpu.SemaphoreType.DMA((steps,)),
+            pltpu.SemaphoreType.DMA((steps,)),
+            pltpu.SemaphoreType.DMA,
+        ],
         cost_estimate=pl.CostEstimate(
             flops=2 * count * depth * samples, bytes_accessed=2 * count * (depth + samples), transcendentals=0
         ),
         name="pull",
-    )(exps, low)
+    )(exps, low, start)
 
 
 def push_kernel(base, final, ids_ref, patch_ref, emb_ref, exp_ref, *refs):
@@ -313,8 +358,9 @@
     pad = ((0, 0), (0, 0), (0, 128 - fcols))
     cargo = jnp.concatenate([jnp.pad(mine.swapaxes(0, 1), pad), jnp.pad(theirs.swapaxes(0, 1), pad)], axis=2)
 
-    found = target_rows(ids, centers, other_centers)
-    exps, low, emb_low, goal, part_sums, target_cos = exponentials(ids, x, found, centers, other_centers)
+    goal = target_directions(ids.reshape(samples), own, centers, other_centers)
+    early = 6
+    exps, low, pull, emb_low, part_sums, target_cos = exponentials(ids, x, goal, centers, other_centers, early)
     margined, slope = margin(target_cos)
     target_exp = jnp.exp(logit_scale * margined)
     goal_logit = jnp.where(ids >= 0, logit_scale * margined, 0.0).reshape(chips, 1, own)
@@ -323,7 +369,7 @@
         axis=2,
     )
     report = to_chips(report)
-    pull = pulled(exps, low)
+    pull = pulled(exps, low, pull, early)
     report = jnp.sum(report, axis=0)
     sums = report[:, :samples]
 

time: 194 us -> 181 us (0.933)
  Pallas kernels: 83.5 us -> 69.1 us
  starting transfers between devices: 42 us -> 39 us
  waiting for transfers between devices: 40 us -> 42.5 us
    pallas_call x3, Pallas kernels: 59.1 us -> 44.6 us  [the longest x1 26.5 us: exponentials(): pl.pallas_call(functools.partial(exp_kernel, steps, early, lanes), grid=(...]
    all_to_all x2, starting transfers between devices: 19.8 us -> 15.1 us  [to_chips(): return lax.all_to_all(x, CHIP, split_axis=0, concat_axis=0, tiled=True)]
  transfers between devices with their start and end apart: 7 -> 7, of which waited for: 3 -> 5; matrix products, arithmetic and copies ran while one was open for 10% -> 12% of each run, Pallas kernels for 18% -> 10%
where the time goes in v3:
time: 181 us; the launch traced here: 180 us
  Pallas kernels  69.1 us (38%)
  waiting for transfers between devices  42.5 us (23%)
  starting transfers between devices  39 us (22%)
  other arithmetic  12.9 us (7%)
  matrix products  8.14 us (4%)
  local copies, waits for them, and re-layouts  7.47 us (4%)
    pallas_call x1, Pallas kernels, exponentials(): pl.pallas_call(functools.partial(exp_kernel, steps, early, lanes), grid=(...  26.5 us
    all_to_all x2, waiting for transfers between devices, to_chips(): return lax.all_to_all(x, CHIP, split_axis=0, concat_axis=0, tiled=True)  24.9 us
    pallas_call x2, Pallas kernels, pushed(): pl.pallas_call(functools.partial(push_kernel, base, final), grid=(count /...  24.5 us
    all_to_all x2, waiting for transfers between devices, from_chips(): return lax.all_to_all(copies, CHIP, split_axis=0, concat_axis=0, tiled=True)  17.1 us
    all_to_all x2, starting transfers between devices, from_chips(): return lax.all_to_all(copies, CHIP, split_axis=0, concat_axis=0, tiled=True)  16.4 us
    all_to_all x2, starting transfers between devices, to_chips(): return lax.all_to_all(x, CHIP, split_axis=0, concat_axis=0, tiled=True)  15.1 us
    pallas_call x1, Pallas kernels, target_directions(): pl.pallas_call(functools.partial(targets_kernel, batch), in_specs=[SMEM,...  11.7 us
    ppermute x3, starting transfers between devices, swapped(): return lax.ppermute(x, CORE, [(0, 1), (1, 0)])  7.48 us
  transfers between devices with their start and end apart: 7, of which 5 were waited for; matrix products, arithmetic and copies ran while one was open for 12% of the time, Pallas kernels for 10%

profile of v3, /device:TPU:1, one launch (start us, length us, event | category | flops | bytes accessed | tf_op | source)
XLA Modules:
  0.0 179.9 jit_solution(14441323842123721160)
XLA Ops:
  0.6 1.5 collective-permute-start
  2.1 6.7 %fusion.13 = (f32[16]{0:T(128)S(1)}, bf16[16,512]{1,0:T(8,128)(2,1)S(1)}) fusion(bf16[16,12544]{1,0:T(8,128)(2,1)} %param.4, bf16[12544,512]{1,0:T(8,128)(2,1)} %param.5), kind=kOutput, calls=%fused_computation.33 | convolution fusion | flops 205553648 | bytes 13262912 | tf_op jit(solution)/shard_map/dot_general | solution.py:344
  8.8 0.0 copy-start.4
  8.8 0.0 copy-start
  8.8 1.1 broadcast_in_dim.25
  9.9 11.2 %all-to-all-start = ((bf16[64,16,512]{2,1,0:T(8,128)(2,1)}), bf16[64,16,512]{2,1,0:T(8,128)(2,1)S(1)}, u32[]{:S(2)}, u32[]{:S(2)}) async-start(bf16[64,16,512]{2,1,0:T(8,128)(2,1)} %broadcast_in_dim.25), calls=%async_computation | async-start | bytes 2097152 | tf_op jit(solution)/shard_map/all_to_all | solution.py:36
  21.2 0.1 reshape.161
  21.3 0.5 broadcast.275
  21.8 0.8 fusion.27
  22.6 1.9 %reshape.165 = bf16[16,64,2,98]{3,2,1,0:T(2,128)(2,1)S(1)} reshape(bf16[16,12544]{1,0:T(8,128)(2,1)S(1)} %copy-done) | data formatting | bytes 802816 | tf_op jit(solution)/shard_map/reshape | solution.py:354
  24.6 0.1 sub.53
  24.6 0.1 sub.52
  24.7 0.6 fusion.17.busy_ref
  25.4 0.6 fusion.22.ids_ref
  26.0 0.6 and_select_fusion.1.ids_ref
  26.6 11.7 %targets.1.goal_ref = bf16[1024,512]{1,0:T(8,128)(2,1)} custom-call(s32[1024]{0:T(1024)} %fusion.22.ids_ref, s32[64]{0:T(128)} %fusion.17.busy_ref, bf16[4096,512]{1,0:T(8,128)(2,1)} %refs_0_.1, bf16[4096,512]{1,0:T(8,128)(2,1)} %collective-permute-done.other_ref), custom_call_target="tpu_custom_call" | custom-call | flops 4294967296 | bytes 8388608 | tf_op jit(solution)/shard_map/targets/pallas_call | solution.py:95
  38.3 0.7 all-to-all-done
  39.0 1.1 copy-done.1
  40.1 26.5 %exponentials.1 = (bf16[1024,8192]{1,0:T(8,128)(2,1)}, bf16[2048,512]{1,0:T(8,128)(2,1)}, f32[1024,512]{1,0:T(8,128)}, bf16[1024,512]{1,0:T(8,128)(2,1)}, f32[1,1024]{1,0:T(1,128)}, /*index=5*/f32[1,1024]{1,0:T(1,128)}) custom-call(s32[1,1024]{1,0:T(1,128)} %and_select_fusion.1.ids_ref, bf16[1024,512]{1,0:T(8,128)(2,1)} %bitcast.25, ...), custom_call_target="tpu_custom_call" | custom-call | flops 8589934592 | bytes 16777216 | tf_op jit(solution)/shard_map/exponentials/pallas_call | solution.py:192
  66.6 0.7 fusion.23
  67.3 0.1 reshape.163
  67.4 0.7 pad.17.clone
  68.1 0.9 pad_maximum_fusion
  69.0 8.1 %all-to-all-start.1 = ((f32[64,1,1152]{2,1,0:T(1,128)}), f32[64,1,1152]{2,1,0:T(1,128)S(1)}, u32[]{:S(2)}, u32[]{:S(2)}) async-start(f32[64,1,1152]{2,1,0:T(1,128)} %pad_maximum_fusion), calls=%async_computation.1 | async-start | bytes 589824 | tf_op jit(solution)/shard_map/all_to_all | solution.py:31
  77.1 1.2 broadcast_select_fusion.1
  78.4 6.4 %pull.1 = f32[1024,512]{1,0:T(8,128)} custom-call(bf16[1024,8192]{1,0:T(8,128)(2,1)} %get-tuple-element.12.exp_ref, bf16[2048,512]{1,0:T(8,128)(2,1)} %get-tuple-element.13.low_ref, f32[1024,512]{1,0:T(8,128)} %get-tuple-element.14.start_ref), custom_call_target="tpu_custom_call" | custom-call | flops 2147483648 | bytes 6291456 | tf_op jit(solution)/shard_map/pull/pallas_call | solution.py:262
  84.8 1.8 all-to-all-done.1
  86.5 0.2 reduce_sum.38
  86.8 0.7 compare_select_fusion.2
  87.4 3.4 %add_convert_fusion = (bf16[1024,512]{1,0:T(8,128)(2,1)S(1)}, bf16[1024,512]{1,0:T(8,128)(2,1)}) fusion(bf16[1024,512]{1,0:T(8,128)(2,1)S(1)} %copy-done.2, f32[1024,512]{1,0:T(8,128)} %pull.1, f32[1024]{0:T(1024)S(1)} %bitcast.29, f32[1024]{0:T(1024)S(1)} %bitcast.30, bf16[1024,512]{1,0:T(8,128)(2,1)} %get-tuple-element.11), kind=kLoop, calls=%fused_computation.7 | loop fusion | flops 4194304 | bytes 6299648 | tf_op jit(solution)/shard_map/convert_element_type | solution.py:380
  90.8 11.0 %shard_map.67 = bf16[4096,512]{1,0:T(8,128)(2,1)} custom-call(s32[1,1024]{1,0:T(1,128)} %and_select_fusion.1.ids_ref, f32[1,1024]{1,0:T(1,128)} %get-tuple-element.17.patch_ref, bf16[1024,512]{1,0:T(8,128)(2,1)} %get-tuple-element.24.emb_ref, bf16[1024,8192]{1,0:T(8,128)(2,1)} %get-tuple-element.12.exp_ref), custom_call_target="tpu_custom_call" | custom-call | flops 4294967296 | bytes 8388608 | tf_op jit(solution)/shard_map/pallas_call | solution.py:316
  101.8 2.6 %collective-permute-start.1 = (bf16[4096,512]{1,0:T(8,128)(2,1)}, bf16[4096,512]{1,0:T(8,128)(2,1)}, u32[]{:S(2)}, u32[]{:S(2)}) collective-permute-start(bf16[4096,512]{1,0:T(8,128)(2,1)} %shard_map.67), channel_id=1, source_target_pairs={{0,1},{1,0},{2,3},{3,2},{4,5},{5,4},{6,7},{7,6},{8,9},{9,8},{10,11... | collective-permute-start | bytes 12582920 | tf_op jit(solution)/shard_map/ppermute | solution.py:27
  104.5 0.6 copy_bitcast_fusion
  105.1 1.4 fusion.4
  106.5 7.0 %all-to-all-start.2 = ((bf16[64,16,768]{2,1,0:T(8,128)(2,1)}), bf16[64,16,768]{2,1,0:T(8,128)(2,1)S(1)}, u32[]{:S(2)}, u32[]{:S(2)}) async-start(bf16[64,16,768]{2,1,0:T(8,128)(2,1)} %fusion.4), calls=%async_computation.2 | async-start | bytes 3145728 | tf_op jit(solution)/shard_map/all_to_all | solution.py:31
  113.5 23.1 %all-to-all-done.2 = bf16[64,16,768]{2,1,0:T(8,128)(2,1)S(1)} async-done(((bf16[64,16,768]{2,1,0:T(8,128)(2,1)}), bf16[64,16,768]{2,1,0:T(8,128)(2,1)S(1)}, u32[]{:S(2)}, u32[]{:S(2)}) %all-to-all-start.2) | async-done | bytes 1572896 | tf_op jit(solution)/shard_map/all_to_all | solution.py:31
  136.6 0.2 convert_reduce_fusion
  136.8 0.2 fusion.9
  137.0 0.1 fusion.12
  137.1 1.1 broadcast_in_dim.30
  138.2 5.2 %all-to-all-start.3 = ((bf16[64,16,512]{2,1,0:T(8,128)(2,1)}), bf16[64,16,512]{2,1,0:T(8,128)(2,1)S(1)}, u32[]{:S(2)}, u32[]{:S(2)}) async-start(bf16[64,16,512]{2,1,0:T(8,128)(2,1)} %broadcast_in_dim.30), calls=%async_computation.3 | async-start | bytes 2097152 | tf_op jit(solution)/shard_map/all_to_all | solution.py:36
  143.4 16.3 %all-to-all-done.3 = bf16[64,16,512]{2,1,0:T(8,128)(2,1)S(1)} async-done(((bf16[64,16,512]{2,1,0:T(8,128)(2,1)}), bf16[64,16,512]{2,1,0:T(8,128)(2,1)S(1)}, u32[]{:S(2)}, u32[]{:S(2)}) %all-to-all-start.3) | async-done | bytes 1048608 | tf_op jit(solution)/shard_map/all_to_all | solution.py:36
  159.7 1.5 convolution_bitcast_fusion
  161.2 3.4 %collective-permute-start.2 = (f32[98,512]{1,0:T(8,128)S(1)}, f32[98,512]{1,0:T(8,128)S(1)}, u32[]{:S(2)}, u32[]{:S(2)}) collective-permute-start(f32[98,512]{1,0:T(8,128)S(1)} %slice.51), channel_id=1, source_target_pairs={{0,1},{1,0},{2,3},{3,2},{4,5},{5,4},{6,7},{7,6},{8,9},{9,8},{10,11... | collective-permute-start | bytes 602120 | tf_op jit(solution)/shard_map/ppermute | solution.py:27
  164.6 0.6 fusion.26
  165.2 0.5 collective-permute-done.2
  165.7 0.7 slice_add_fusion
  166.4 13.4 %shard_map.68 = bf16[4096,512]{1,0:T(8,128)(2,1)} custom-call(s32[1,1024]{1,0:T(1,128)} %and_select_fusion.1.ids_ref, f32[1,1024]{1,0:T(1,128)} %get-tuple-element.17.patch_ref, bf16[1024,512]{1,0:T(8,128)(2,1)} %get-tuple-element.24.emb_ref, bf16[1024,8192]{1,0:T(8,128)(2,1)} %get-tuple-element.12.exp_ref, bf16[4096,512]{1,0:T(8,128)(2,1)} %refs_0_.1, ...), custom_call_target="tpu_custom_call" | custom-call | flops 4294967296 | bytes 8388608 | tf_op jit(solution)/shard_map/pallas_call | solution.py:316
  (14 shorter events, 0.1 us)
Async XLA Ops:
  0.6 25.9 %collective-permute-start = (bf16[4096,512]{1,0:T(8,128)(2,1)}, bf16[4096,512]{1,0:T(8,128)(2,1)}, u32[]{:S(2)}, u32[]{:S(2)}) collective-permute-start(bf16[4096,512]{1,0:T(8,128)(2,1)} %refs_0_.1), channel_id=1, source_target_pairs={{0,1},{1,0},{2,3},{3,2},{4,5},{5,4},{6,7},{7,6},{8,9},{9,8},{10,11... | collective-permute-start | bytes 12582920 | tf_op jit(solution)/shard_map/ppermute | solution.py:27
  8.8 12.4 %copy-start.4 = (s32[2048]{0:T(1024)S(1)}, s32[2048]{0:T(1024)}, u32[]{:S(2)}) copy-start(s32[2048]{0:T(1024)} %param.7) | copy-start | bytes 24580
  8.8 13.8 %copy-start = (bf16[16,12544]{1,0:T(8,128)(2,1)S(1)}, bf16[16,12544]{1,0:T(8,128)(2,1)}, u32[]{:S(2)}) copy-start(bf16[16,12544]{1,0:T(8,128)(2,1)} %param.4) | copy-start | bytes 1204228
  9.9 29.1 %all-to-all-start = ((bf16[64,16,512]{2,1,0:T(8,128)(2,1)}), bf16[64,16,512]{2,1,0:T(8,128)(2,1)S(1)}, u32[]{:S(2)}, u32[]{:S(2)}) async-start(bf16[64,16,512]{2,1,0:T(8,128)(2,1)} %broadcast_in_dim.25), calls=%async_computation | async-start | bytes 2097152 | tf_op jit(solution)/shard_map/all_to_all | solution.py:36
  39.0 1.1 copy-start.1
  69.0 17.5 %all-to-all-start.1 = ((f32[64,1,1152]{2,1,0:T(1,128)}), f32[64,1,1152]{2,1,0:T(1,128)S(1)}, u32[]{:S(2)}, u32[]{:S(2)}) async-start(f32[64,1,1152]{2,1,0:T(1,128)} %pad_maximum_fusion), calls=%async_computation.1 | async-start | bytes 589824 | tf_op jit(solution)/shard_map/all_to_all | solution.py:31
  78.3 8.4 %copy-start.3 = (f32[1,1024]{1,0:T(1,128)S(1)}, f32[1,1024]{1,0:T(1,128)}, u32[]{:S(2)}) copy-start(f32[1,1024]{1,0:T(1,128)} %get-tuple-element.10) | copy-start | bytes 12292
  78.4 9.1 %copy-start.2 = (bf16[1024,512]{1,0:T(8,128)(2,1)S(1)}, bf16[1024,512]{1,0:T(8,128)(2,1)}, u32[]{:S(2)}) copy-start(bf16[1024,512]{1,0:T(8,128)(2,1)} %targets.1.goal_ref) | copy-start | bytes 3145732
  101.8 64.6 %collective-permute-start.1 = (bf16[4096,512]{1,0:T(8,128)(2,1)}, bf16[4096,512]{1,0:T(8,128)(2,1)}, u32[]{:S(2)}, u32[]{:S(2)}) collective-permute-start(bf16[4096,512]{1,0:T(8,128)(2,1)} %shard_map.67), channel_id=1, source_target_pairs={{0,1},{1,0},{2,3},{3,2},{4,5},{5,4},{6,7},{7,6},{8,9},{9,8},{10,11... | collective-permute-start | bytes 12582920 | tf_op jit(solution)/shard_map/ppermute | solution.py:27
  106.5 30.1 %all-to-all-start.2 = ((bf16[64,16,768]{2,1,0:T(8,128)(2,1)}), bf16[64,16,768]{2,1,0:T(8,128)(2,1)S(1)}, u32[]{:S(2)}, u32[]{:S(2)}) async-start(bf16[64,16,768]{2,1,0:T(8,128)(2,1)} %fusion.4), calls=%async_computation.2 | async-start | bytes 3145728 | tf_op jit(solution)/shard_map/all_to_all | solution.py:31
  138.2 21.5 %all-to-all-start.3 = ((bf16[64,16,512]{2,1,0:T(8,128)(2,1)}), bf16[64,16,512]{2,1,0:T(8,128)(2,1)S(1)}, u32[]{:S(2)}, u32[]{:S(2)}) async-start(bf16[64,16,512]{2,1,0:T(8,128)(2,1)} %broadcast_in_dim.30), calls=%async_computation.3 | async-start | bytes 2097152 | tf_op jit(solution)/shard_map/all_to_all | solution.py:36
  161.2 4.5 %collective-permute-start.2 = (f32[98,512]{1,0:T(8,128)S(1)}, f32[98,512]{1,0:T(8,128)S(1)}, u32[]{:S(2)}, u32[]{:S(2)}) collective-permute-start(f32[98,512]{1,0:T(8,128)S(1)} %slice.51), channel_id=1, source_target_pairs={{0,1},{1,0},{2,3},{3,2},{4,5},{5,4},{6,7},{7,6},{8,9},{9,8},{10,11... | collective-permute-start | bytes 602120 | tf_op jit(solution)/shard_map/ppermute | solution.py:27

commit v4 on v3

--- a/solution.py
+++ b/solution.py
@@ -50,6 +50,43 @@
 ANY = pl.BlockSpec(memory_space=pl.ANY)
 VMEM = pl.BlockSpec(memory_space=pltpu.VMEM)
 SMEM = pl.BlockSpec(memory_space=pltpu.SMEM)
+
+
+def embed_kernel(cuts, f_ref, w_ref, out_ref, copies_ref, weight, sems):
+    copies = [
+        pltpu.make_async_copy(w_ref.at[pl.ds(a, b - a)], weight.at[pl.ds(a, b - a)], sems.at[k])
+        for k, (a, b) in enumerate(zip(cuts, cuts[1:]))
+    ]
+    for copy in copies:
+        copy.start()
+    total = None
+    for copy, a, b in zip(copies, cuts, cuts[1:]):
+        copy.wait()
+        product = jnp.dot(f_ref[:, a:b], weight[a:b, :], preferred_element_type=f32)
+        total = product if total is None else total + product
+    rows = total.astype(bf16)
+    out_ref[...] = rows
+    for chip in range(copies_ref.shape[0]):
+        copies_ref[chip] = rows
+
+
+def embedded_rows(features, weight, chips, cuts):
+    own, wide = features.shape
+    depth = weight.shape[1]
+    return pl.pallas_call(
+        functools.partial(embed_kernel, cuts),
+        in_specs=[VMEM, ANY],
+        out_specs=[VMEM, VMEM],
+        out_shape=[
+            jax.ShapeDtypeStruct((own, depth), bf16),
+            jax.ShapeDtypeStruct((chips, own, depth), bf16),
+        ],
+        scratch_shapes=[pltpu.VMEM((wide, depth), bf16), pltpu.SemaphoreType.DMA((len(cuts) - 1,))],
+        cost_estimate=pl.CostEstimate(
+            flops=2 * own * wide * depth, bytes_accessed=2 * wide * depth, transcendentals=0
+        ),
+        name="embed",
+    )(features, weight)
 
 
 def targets_kernel(batch, ids_ref, busy_ref, own_ref, other_ref, goal_ref, centers, found, sems):
@@ -70,7 +107,7 @@
         def _():
             def sample(b, carry):
                 at = g * batch + b
-                row = ids_ref[at]
+                row = ids_ref[0, at]
 
                 @pl.when(row >= 0)
                 def _():
@@ -90,7 +127,7 @@
 
 def target_directions(ids, batch, own, other):
     count, depth = own.shape
-    samples = ids.shape[0]
+    samples = ids.shape[1]
     busy = jnp.max(ids.reshape(samples // batch, batch), axis=1)
     return pl.pallas_call(
         functools.partial(targets_kernel, batch),
@@ -117,7 +154,7 @@
 
 
 def exp_kernel(steps, early, lanes, ids_ref, x_ref, goal_ref, own_ref, other_ref, exp_ref, low_ref, pull_ref, emb_ref,
-               sums_ref, cos_ref, wide_ids, scaled, row_sum, total):
+               report_ref, cos_ref, wide_ids, scaled, row_sum, total):
     i = pl.program_id(0)
     rows = own_ref.shape[0]
     samples = x_ref.shape[0]
@@ -179,11 +216,20 @@
         target_cos = row_of(goal_ref[...].astype(f32) * scaled[...].astype(f32)) * (1.0 / logit_scale)
         cos_ref[...] = target_cos
         margined, _ = margin(target_cos)
-        here = jnp.where(ids_ref[...] >= 0, jnp.exp(logit_scale * margined), 0.0)
-        sums_ref[...] = row_of(row_sum[...]) + here
-
-
-def exponentials(ids, x, goal, own, other, early, rows=1024, lanes=2):
+        is_here = ids_ref[...] >= 0
+        logit = jnp.where(is_here, logit_scale * margined, 0.0)
+        sums = row_of(row_sum[...]) + jnp.where(is_here, jnp.exp(logit_scale * margined), 0.0)
+        chips = report_ref.shape[0]
+        own = samples // chips
+        lane = lax.broadcasted_iota(jnp.int32, (1, 128), 1)
+        for chip in range(chips):
+            k = chip * own // 128
+            theirs = (lane + k * 128) // own == chip
+            report_ref[chip, :, :samples] = sums
+            report_ref[chip, :, samples:] = jnp.where(theirs, logit[:, k * 128 : (k + 1) * 128], 0.0)
+
+
+def exponentials(ids, x, goal, own, other, chips, early, rows=1024, lanes=2):
     samples, depth = x.shape
     count = own.shape[0]
     steps = count // rows
@@ -204,7 +250,7 @@
             pl.BlockSpec((rows, depth), lambda i: (jnp.maximum(i - early, 0), 0)),
             pl.BlockSpec((samples, depth), fixed),
             pl.BlockSpec((samples, depth), fixed),
-            pl.BlockSpec((1, samples), fixed),
+            pl.BlockSpec((chips, 1, samples + 128), lambda i: (0, 0, 0)),
             pl.BlockSpec((1, samples), fixed),
         ],
         out_shape=[
@@ -212,7 +258,7 @@
             jax.ShapeDtypeStruct((late * rows, depth), bf16),
             jax.ShapeDtypeStruct((samples, depth), f32),
             jax.ShapeDtypeStruct((samples, depth), bf16),
-            jax.ShapeDtypeStruct((1, samples), f32),
+            jax.ShapeDtypeStruct((chips, 1, samples + 128), f32),
             jax.ShapeDtypeStruct((1, samples), f32),
         ],
         scratch_shapes=[
@@ -278,6 +324,65 @@
     )(exps, low, start)
 
 
+def settle_kernel(ids_ref, cos_ref, report_ref, pull_ref, goal_ref, emb_ref, cargo_ref, parcel_ref, scaled_ref,
+                  patch_ref, sums_ref, wide_scale, wide_target):
+    i = pl.program_id(0)
+    rows, depth = goal_ref.shape
+    samples = ids_ref.shape[1]
+
+    @pl.when(i == 0)
+    def _():
+        report = jnp.sum(report_ref[...], axis=0)
+        sums_ref[...] = report
+        sums = report[:, :samples]
+        margined, slope = margin(cos_ref[...])
+        patch = slope * (jnp.exp(logit_scale * margined) - sums)
+        patch_ref[...] = patch
+        scale = logit_scale / sums
+        at_target = jnp.where(ids_ref[...] >= 0, scale * patch, 0.0)
+        wide_scale[...] = jnp.broadcast_to(scale, (128, samples)).T
+        wide_target[...] = jnp.broadcast_to(at_target, (128, samples)).T
+
+    span = pl.ds(pl.multiple_of(i * rows, rows), rows)
+    scale = jnp.concatenate([wide_scale[span, :]] * (depth // 128), axis=1)
+    at_target = jnp.concatenate([wide_target[span, :]] * (depth // 128), axis=1)
+    parcel_ref[:, :depth] = (pull_ref[...] * scale + at_target * goal_ref[...].astype(f32)).astype(bf16)
+    parcel_ref[:, depth:] = cargo_ref[...]
+    scaled_ref[...] = (emb_ref[...].astype(f32) * scale).astype(bf16)
+
+
+def settled(ids, target_cos, report, pull, goal, emb, cargo, rows=512):
+    samples, depth = emb.shape
+    extra = cargo.shape[1]
+    fixed = lambda i: (0, 0)
+    step = lambda i: (i, 0)
+    row = pl.BlockSpec((1, samples), fixed)
+    return pl.pallas_call(
+        settle_kernel,
+        grid=(samples // rows,),
+        in_specs=[row, row, pl.BlockSpec(report.shape, lambda i: (0, 0, 0))]
+        + [pl.BlockSpec((rows, depth), step)] * 3
+        + [pl.BlockSpec((rows, extra), step)],
+        out_specs=[
+            pl.BlockSpec((rows, depth + extra), step),
+            pl.BlockSpec((rows, depth), step),
+            row,
+            pl.BlockSpec((1, report.shape[2]), fixed),
+        ],
+        out_shape=[
+            jax.ShapeDtypeStruct((samples, depth + extra), bf16),
+            jax.ShapeDtypeStruct((samples, depth), bf16),
+            jax.ShapeDtypeStruct((1, samples), f32),
+            jax.ShapeDtypeStruct((1, report.shape[2]), f32),
+        ],
+        scratch_shapes=[pltpu.VMEM((samples, 128), f32), pltpu.VMEM((samples, 128), f32)],
+        cost_estimate=pl.CostEstimate(
+            flops=8 * samples * depth, bytes_accessed=14 * samples * depth, transcendentals=0
+        ),
+        name="settle",
+    )(ids, target_cos, report, pull, goal, emb, cargo)
+
+
 def push_kernel(base, final, ids_ref, patch_ref, emb_ref, exp_ref, *refs):
     i = pl.program_id(0)
     samples, rows = exp_ref.shape
@@ -305,7 +410,7 @@
     out_ref[...] = push.astype(bf16)
 
 
-def pushed(ids, patch, emb, exps, half, centers=None, other=None, rows=512):
+def pushed(ids, patch, emb, exps, half, centers=None, other=None, rows=1024):
     samples, depth = emb.shape
     count = exps.shape[1] // 2
     base = half * (count // rows)
@@ -341,8 +446,9 @@
     samples = chips * own
 
     other_centers = swapped(centers)
-    embedded = jnp.dot(features, fc_weight, preferred_element_type=f32).astype(bf16)
-    x = from_chips(embedded).reshape(samples, depth)
+    cuts = tuple(range(0, wide, 1792)) + (wide,)
+    embedded, copies = embedded_rows(features, fc_weight, chips, cuts)
+    x = to_chips(copies).reshape(samples, depth)
 
     by_core = labels.reshape(chips, 2, own)
     my_labels = jnp.where(core == 0, by_core[:, 0], by_core[:, 1]).reshape(1, samples)
@@ -358,29 +464,15 @@
     pad = ((0, 0), (0, 0), (0, 128 - fcols))
     cargo = jnp.concatenate([jnp.pad(mine.swapaxes(0, 1), pad), jnp.pad(theirs.swapaxes(0, 1), pad)], axis=2)
 
-    goal = target_directions(ids.reshape(samples), own, centers, other_centers)
+    goal = target_directions(ids, own, centers, other_centers)
     early = 6
-    exps, low, pull, emb_low, part_sums, target_cos = exponentials(ids, x, goal, centers, other_centers, early)
-    margined, slope = margin(target_cos)
-    target_exp = jnp.exp(logit_scale * margined)
-    goal_logit = jnp.where(ids >= 0, logit_scale * margined, 0.0).reshape(chips, 1, own)
-    report = jnp.concatenate(
-        [jnp.broadcast_to(part_sums, (chips, 1, samples)), jnp.pad(goal_logit, ((0, 0), (0, 0), (0, 128 - own)))],
-        axis=2,
-    )
+    exps, low, pull, emb_low, report, target_cos = exponentials(ids, x, goal, centers, other_centers, chips, early)
     report = to_chips(report)
     pull = pulled(exps, low, pull, early)
-    report = jnp.sum(report, axis=0)
-    sums = report[:, :samples]
-
-    patch = slope * (target_exp - sums)
-    scale = logit_scale / sums
-    scale_column = scale.reshape(samples, 1)
-    at_target = jnp.where(ids >= 0, scale * patch, 0.0).reshape(samples, 1)
-    pull = (pull * scale_column + at_target * goal.astype(f32)).astype(bf16)
-    scaled = (emb_low.astype(f32) * scale_column).astype(bf16)
-    parcel = jnp.concatenate([pull.reshape(chips, own, depth), cargo], axis=2)
-    parcel = to_chips(parcel)
+    parcel, scaled, patch, report = settled(
+        ids, target_cos, report, pull, goal, emb_low, cargo.reshape(samples, 256)
+    )
+    parcel = to_chips(parcel.reshape(chips, own, depth + 256))
 
     other_push = pushed(ids, patch, scaled, exps, 1)
     other_push = swapped(other_push)
@@ -399,8 +491,9 @@
     both = lax.dot_general(columns, grads, (((0,), (0,)), ((), ())), preferred_element_type=f32)
     theirs_fc = swapped(both[128 : 128 + fcols])
     grad_fc = both[:fcols] + theirs_fc
-    own_sums = lax.dynamic_slice_in_dim(sums.reshape(samples), chip * own, own)
-    loss = jnp.log(own_sums) - report[0, samples : samples + own]
+    own_sums = lax.dynamic_slice_in_dim(report[0], chip * own, own)
+    own_logits = lax.dynamic_slice_in_dim(report[0], samples + chip * own % 128, own)
+    loss = jnp.log(own_sums) - own_logits
     return (loss, grad_centers, grad_fc)
 
 

time: 181 us -> 174 us (0.961)
  Pallas kernels: 69.1 us -> 77.3 us
  other arithmetic: 12.9 us -> 6.02 us
  matrix products: 8.14 us -> 1.47 us
    all_to_all x2 -> x3, starting transfers between devices: 15.1 us -> 26.7 us  [to_chips(): return lax.all_to_all(x, CHIP, split_axis=0, concat_axis=0, tiled=True)]
    pallas_call x0 -> x2, Pallas kernels: none -> 11.4 us  [the longest x1 7.22 us: embedded_rows(): pl.pallas_call(functools.partial(embed_kernel, cuts), in_specs=[VMEM, ANY...]
    all_to_all x2 -> x1, starting transfers between devices: 16.4 us -> 5.17 us  [from_chips(): return lax.all_to_all(copies, CHIP, split_axis=0, concat_axis=0, tiled=True)]
    dot_general x1 -> x0, matrix products: 6.67 us -> none  [step(): jnp.dot(features, fc_weight, preferred_element_type=f32).astype(bf16)]
    convert_element_type x1 -> x0, other arithmetic: 3.39 us -> none  [step(): pull = (pull * scale_column + at_target * goal.astype(f32)).astype(bf16)]
    pallas_call x2, Pallas kernels: 24.5 us -> 21.4 us  [pushed(): pl.pallas_call(functools.partial(push_kernel, base, final), grid=(count /...]
    select_n x3 -> x0, other arithmetic: 2.6 us -> none  [the longest x1 1.22 us: step(): mine = jnp.where(core == 0, split[:, :, 0], split[:, :, 1])]
    all_to_all x2 -> x1, waiting for transfers between devices: 17.1 us -> 16.3 us  [from_chips(): return lax.all_to_all(copies, CHIP, split_axis=0, concat_axis=0, tiled=True)]
  transfers between devices with their start and end apart: 7 -> 7, of which waited for: 5 -> 3; matrix products, arithmetic and copies ran while one was open for 12% -> 7% of each run, Pallas kernels for 10% -> 15%
where the time goes in v4:
time: 174 us; the launch traced here: 173 us
  Pallas kernels  77.3 us (44%)
  waiting for transfers between devices  41.7 us (24%)
  starting transfers between devices  39.4 us (23%)
  local copies, waits for them, and re-layouts  6.69 us (4%)
  other arithmetic  6.02 us (3%)
    all_to_all x3, starting transfers between devices, to_chips(): return lax.all_to_all(x, CHIP, split_axis=0, concat_axis=0, tiled=True)  26.7 us
    pallas_call x1, Pallas kernels, exponentials(): pl.pallas_call(functools.partial(exp_kernel, steps, early, lanes), grid=(...  26.6 us
    all_to_all x3, waiting for transfers between devices, to_chips(): return lax.all_to_all(x, CHIP, split_axis=0, concat_axis=0, tiled=True)  25.4 us
    pallas_call x2, Pallas kernels, pushed(): pl.pallas_call(functools.partial(push_kernel, base, final), grid=(count /...  21.4 us
    all_to_all x1, waiting for transfers between devices, from_chips(): return lax.all_to_all(copies, CHIP, split_axis=0, concat_axis=0, tiled=True)  16.3 us
    pallas_call x1, Pallas kernels, target_directions(): pl.pallas_call(functools.partial(targets_kernel, batch), in_specs=[SMEM,...  11.7 us
    ppermute x3, starting transfers between devices, swapped(): return lax.ppermute(x, CORE, [(0, 1), (1, 0)])  7.55 us
    pallas_call x1, Pallas kernels, embedded_rows(): pl.pallas_call(functools.partial(embed_kernel, cuts), in_specs=[VMEM, ANY...  7.22 us
  transfers between devices with their start and end apart: 7, of which 3 were waited for; matrix products, arithmetic and copies ran while one was open for 7% of the time, Pallas kernels for 15%

profile of v4, /device:TPU:1, one launch (start us, length us, event | category | flops | bytes accessed | tf_op | source)
XLA Modules:
  0.0 173.4 jit_solution(6222083510074367203)
XLA Ops:
  0.6 0.0 copy-start
  0.6 0.0 copy-start.4
  0.7 1.5 collective-permute-start
  2.1 7.2 %embed.1 = (bf16[16,512]{1,0:T(8,128)(2,1)}, bf16[64,16,512]{2,1,0:T(8,128)(2,1)}) custom-call(bf16[16,12544]{1,0:T(8,128)(2,1)} %f_ref.1, bf16[12544,512]{1,0:T(8,128)(2,1)} %w_ref.1), custom_call_target="tpu_custom_call" | custom-call | flops 205520896 | bytes 12845056 | tf_op jit(solution)/shard_map/embed/pallas_call | solution.py:76
  9.3 11.3 %all-to-all-start = ((bf16[64,16,512]{2,1,0:T(8,128)(2,1)}), bf16[64,16,512]{2,1,0:T(8,128)(2,1)S(1)}, u32[]{:S(2)}, u32[]{:S(2)}) async-start(bf16[64,16,512]{2,1,0:T(8,128)(2,1)} %get-tuple-element.15), calls=%async_computation | async-start | bytes 2097152 | tf_op jit(solution)/shard_map/all_to_all | solution.py:31
  20.6 0.0 copy-done
  20.6 1.9 %reshape.139 = bf16[16,64,2,98]{3,2,1,0:T(2,128)(2,1)S(1)} reshape(bf16[16,12544]{1,0:T(8,128)(2,1)S(1)} %copy-done) | data formatting | bytes 802816 | tf_op jit(solution)/shard_map/reshape | solution.py:460
  22.6 0.0 copy-done.4
  22.6 0.1 reshape.137
  22.7 0.5 broadcast.147
  23.3 0.8 fusion.19
  24.0 0.1 sub.32
  24.1 0.6 and_select_fusion.1.ids_ref
  24.7 0.6 fusion.15.busy_ref
  25.4 1.1 fusion.21
  26.5 0.6 select_bitcast_fusion.1
  27.1 0.0 collective-permute-done.other_ref
  27.1 11.7 %targets.1.goal_ref = bf16[1024,512]{1,0:T(8,128)(2,1)} custom-call(s32[1,1024]{1,0:T(1,128)} %and_select_fusion.1.ids_ref, s32[64]{0:T(128)} %fusion.15.busy_ref, bf16[4096,512]{1,0:T(8,128)(2,1)} %refs_0_.1, bf16[4096,512]{1,0:T(8,128)(2,1)} %collective-permute-done.other_ref), custom_call_target="tpu_custom_call" | custom-call | flops 4294967296 | bytes 8388608 | tf_op jit(solution)/shard_map/targets/pallas_call | solution.py:132
  38.7 0.0 all-to-all-done
  38.7 0.0 copy-start.2
  38.8 1.0 copy-done.2
  39.8 26.6 %exponentials.1 = (bf16[1024,8192]{1,0:T(8,128)(2,1)}, bf16[2048,512]{1,0:T(8,128)(2,1)}, f32[1024,512]{1,0:T(8,128)}, bf16[1024,512]{1,0:T(8,128)(2,1)}, f32[64,1,1152]{2,1,0:T(1,128)}, /*index=5*/f32[1,1024]{1,0:T(1,128)}) custom-call(s32[1,1024]{1,0:T(1,128)} %and_select_fusion.1.ids_ref, bf16[1024,512]{1,0:T(8,128)(2,1)} %bitcast.17, ...), custom_call_target="tpu_custom_call" | custom-call | flops 8589934592 | bytes 16777216 | tf_op jit(solution)/shard_map/exponentials/pallas_call | solution.py:238
  66.4 8.9 %all-to-all-start.1 = ((f32[64,1,1152]{2,1,0:T(1,128)}), f32[64,1,1152]{2,1,0:T(1,128)S(1)}, u32[]{:S(2)}, u32[]{:S(2)}) async-start(f32[64,1,1152]{2,1,0:T(1,128)} %get-tuple-element.17), calls=%async_computation.1 | async-start | bytes 589824 | tf_op jit(solution)/shard_map/all_to_all | solution.py:31
  75.2 0.9 fusion.3
  76.1 6.3 %pull.1.pull_ref = f32[1024,512]{1,0:T(8,128)} custom-call(bf16[1024,8192]{1,0:T(8,128)(2,1)} %get-tuple-element.18.exp_ref, bf16[2048,512]{1,0:T(8,128)(2,1)} %get-tuple-element.19.low_ref, f32[1024,512]{1,0:T(8,128)} %get-tuple-element.20.start_ref), custom_call_target="tpu_custom_call" | custom-call | flops 2147483648 | bytes 6291456 | tf_op jit(solution)/shard_map/pull/pallas_call | solution.py:308
  82.4 2.4 %all-to-all-done.1.report_ref = f32[64,1,1152]{2,1,0:T(1,128)S(1)} async-done(((f32[64,1,1152]{2,1,0:T(1,128)}), f32[64,1,1152]{2,1,0:T(1,128)S(1)}, u32[]{:S(2)}, u32[]{:S(2)}) %all-to-all-start.1) | async-done | bytes 294944 | tf_op jit(solution)/shard_map/all_to_all | solution.py:31
  84.8 0.0 copy-start.1
  84.8 0.7 copy-done.1
  85.5 4.1 %settle.1 = (bf16[1024,768]{1,0:T(8,128)(2,1)}, bf16[1024,512]{1,0:T(8,128)(2,1)}, f32[1,1024]{1,0:T(1,128)}, f32[1,1152]{1,0:T(1,128)}) custom-call(s32[1,1024]{1,0:T(1,128)} %and_select_fusion.1.ids_ref, f32[1,1024]{1,0:T(1,128)} %get-tuple-element.16.cos_ref, f32[64,1,1152]{2,1,0:T(1,128)} %copy-done.1, f32[1024,512]{1,0:T(8,128)} %pull.1.pull_ref, ...), custom_call_target="tpu_custom_call" | custom-call | flops 4194304 | bytes 7340032 | tf_op jit(solution)/shard_map/settle/pallas_call | solution.py:360
  89.7 9.3 %shard_map.67 = bf16[4096,512]{1,0:T(8,128)(2,1)} custom-call(s32[1,1024]{1,0:T(1,128)} %and_select_fusion.1.ids_ref, f32[1,1024]{1,0:T(1,128)} %get-tuple-element.23.patch_ref, bf16[1024,512]{1,0:T(8,128)(2,1)} %get-tuple-element.24.emb_ref, bf16[1024,8192]{1,0:T(8,128)(2,1)} %get-tuple-element.18.exp_ref), custom_call_target="tpu_custom_call" | custom-call | flops 4294967296 | bytes 8388608 | tf_op jit(solution)/shard_map/pallas_call | solution.py:421
  99.0 2.7 %collective-permute-start.1 = (bf16[4096,512]{1,0:T(8,128)(2,1)}, bf16[4096,512]{1,0:T(8,128)(2,1)}, u32[]{:S(2)}, u32[]{:S(2)}) collective-permute-start(bf16[4096,512]{1,0:T(8,128)(2,1)} %shard_map.67), channel_id=1, source_target_pairs={{0,1},{1,0},{2,3},{3,2},{4,5},{5,4},{6,7},{7,6},{8,9},{9,8},{10,11... | collective-permute-start | bytes 12582920 | tf_op jit(solution)/shard_map/ppermute | solution.py:27
  101.6 6.6 %all-to-all-start.2 = ((bf16[64,16,768]{2,1,0:T(8,128)(2,1)}), bf16[64,16,768]{2,1,0:T(8,128)(2,1)S(1)}, u32[]{:S(2)}, u32[]{:S(2)}) async-start(bf16[64,16,768]{2,1,0:T(8,128)(2,1)} %bitcast.8), calls=%async_computation.2 | async-start | bytes 3145728 | tf_op jit(solution)/shard_map/all_to_all | solution.py:31
  108.2 0.0 copy-done.3
  108.2 0.1 fusion.11
  108.3 23.0 %all-to-all-done.2 = bf16[64,16,768]{2,1,0:T(8,128)(2,1)S(1)} async-done(((bf16[64,16,768]{2,1,0:T(8,128)(2,1)}), bf16[64,16,768]{2,1,0:T(8,128)(2,1)S(1)}, u32[]{:S(2)}, u32[]{:S(2)}) %all-to-all-start.2) | async-done | bytes 1572896 | tf_op jit(solution)/shard_map/all_to_all | solution.py:31
  131.4 0.2 convert_reduce_fusion
  131.5 0.2 fusion.7
  131.7 0.1 fusion.10
  131.8 1.1 broadcast_in_dim.13
  132.9 5.2 %all-to-all-start.3 = ((bf16[64,16,512]{2,1,0:T(8,128)(2,1)}), bf16[64,16,512]{2,1,0:T(8,128)(2,1)S(1)}, u32[]{:S(2)}, u32[]{:S(2)}) async-start(bf16[64,16,512]{2,1,0:T(8,128)(2,1)} %broadcast_in_dim.13), calls=%async_computation.3 | async-start | bytes 2097152 | tf_op jit(solution)/shard_map/all_to_all | solution.py:36
  138.1 16.3 %all-to-all-done.3 = bf16[64,16,512]{2,1,0:T(8,128)(2,1)S(1)} async-done(((bf16[64,16,512]{2,1,0:T(8,128)(2,1)}), bf16[64,16,512]{2,1,0:T(8,128)(2,1)S(1)}, u32[]{:S(2)}, u32[]{:S(2)}) %all-to-all-start.3) | async-done | bytes 1048608 | tf_op jit(solution)/shard_map/all_to_all | solution.py:36
  154.4 1.5 convolution_bitcast_fusion
  155.9 3.4 %collective-permute-start.2 = (f32[98,512]{1,0:T(8,128)S(1)}, f32[98,512]{1,0:T(8,128)S(1)}, u32[]{:S(2)}, u32[]{:S(2)}) collective-permute-start(f32[98,512]{1,0:T(8,128)S(1)} %slice.41), channel_id=1, source_target_pairs={{0,1},{1,0},{2,3},{3,2},{4,5},{5,4},{6,7},{7,6},{8,9},{9,8},{10,11... | collective-permute-start | bytes 602120 | tf_op jit(solution)/shard_map/ppermute | solution.py:27
  159.3 1.3 subtract_bitcast_fusion
  160.6 0.0 collective-permute-done.2
  160.6 0.7 slice_add_fusion
  161.3 0.0 collective-permute-done.1.refs_1_
  161.3 12.1 %shard_map.68 = bf16[4096,512]{1,0:T(8,128)(2,1)} custom-call(s32[1,1024]{1,0:T(1,128)} %and_select_fusion.1.ids_ref, f32[1,1024]{1,0:T(1,128)} %get-tuple-element.23.patch_ref, bf16[1024,512]{1,0:T(8,128)(2,1)} %get-tuple-element.24.emb_ref, bf16[1024,8192]{1,0:T(8,128)(2,1)} %get-tuple-element.18.exp_ref, bf16[4096,512]{1,0:T(8,128)(2,1)} %refs_0_.1, ...), custom_call_target="tpu_custom_call" | custom-call | flops 4294967296 | bytes 8388608 | tf_op jit(solution)/shard_map/pallas_call | solution.py:421
  (4 shorter events, 0.1 us)
Async XLA Ops:
  0.6 20.0 %copy-start = (bf16[16,12544]{1,0:T(8,128)(2,1)S(1)}, bf16[16,12544]{1,0:T(8,128)(2,1)}, u32[]{:S(2)}) copy-start(bf16[16,12544]{1,0:T(8,128)(2,1)} %f_ref.1) | copy-start | bytes 1204228
  0.6 21.9 %copy-start.4 = (s32[2048]{0:T(1024)S(1)}, s32[2048]{0:T(1024)}, u32[]{:S(2)}) copy-start(s32[2048]{0:T(1024)} %param.7) | copy-start | bytes 24580
  0.7 26.4 %collective-permute-start = (bf16[4096,512]{1,0:T(8,128)(2,1)}, bf16[4096,512]{1,0:T(8,128)(2,1)}, u32[]{:S(2)}, u32[]{:S(2)}) collective-permute-start(bf16[4096,512]{1,0:T(8,128)(2,1)} %refs_0_.1), channel_id=1, source_target_pairs={{0,1},{1,0},{2,3},{3,2},{4,5},{5,4},{6,7},{7,6},{8,9},{9,8},{10,11... | collective-permute-start | bytes 12582920 | tf_op jit(solution)/shard_map/ppermute | solution.py:27
  9.3 29.4 %all-to-all-start = ((bf16[64,16,512]{2,1,0:T(8,128)(2,1)}), bf16[64,16,512]{2,1,0:T(8,128)(2,1)S(1)}, u32[]{:S(2)}, u32[]{:S(2)}) async-start(bf16[64,16,512]{2,1,0:T(8,128)(2,1)} %get-tuple-element.15), calls=%async_computation | async-start | bytes 2097152 | tf_op jit(solution)/shard_map/all_to_all | solution.py:31
  38.7 1.0 copy-start.2
  66.4 18.4 %all-to-all-start.1 = ((f32[64,1,1152]{2,1,0:T(1,128)}), f32[64,1,1152]{2,1,0:T(1,128)S(1)}, u32[]{:S(2)}, u32[]{:S(2)}) async-start(f32[64,1,1152]{2,1,0:T(1,128)} %get-tuple-element.17), calls=%async_computation.1 | async-start | bytes 589824 | tf_op jit(solution)/shard_map/all_to_all | solution.py:31
  84.8 0.7 copy-start.1
  89.7 18.5 %copy-start.3 = (bf16[16,512]{1,0:T(8,128)(2,1)S(1)}, bf16[16,512]{1,0:T(8,128)(2,1)}, u32[]{:S(2)}) copy-start(bf16[16,512]{1,0:T(8,128)(2,1)} %get-tuple-element.26) | copy-start | bytes 49156
  99.0 62.4 %collective-permute-start.1 = (bf16[4096,512]{1,0:T(8,128)(2,1)}, bf16[4096,512]{1,0:T(8,128)(2,1)}, u32[]{:S(2)}, u32[]{:S(2)}) collective-permute-start(bf16[4096,512]{1,0:T(8,128)(2,1)} %shard_map.67), channel_id=1, source_target_pairs={{0,1},{1,0},{2,3},{3,2},{4,5},{5,4},{6,7},{7,6},{8,9},{9,8},{10,11... | collective-permute-start | bytes 12582920 | tf_op jit(solution)/shard_map/ppermute | solution.py:27
  101.6 29.7 %all-to-all-start.2 = ((bf16[64,16,768]{2,1,0:T(8,128)(2,1)}), bf16[64,16,768]{2,1,0:T(8,128)(2,1)S(1)}, u32[]{:S(2)}, u32[]{:S(2)}) async-start(bf16[64,16,768]{2,1,0:T(8,128)(2,1)} %bitcast.8), calls=%async_computation.2 | async-start | bytes 3145728 | tf_op jit(solution)/shard_map/all_to_all | solution.py:31
  132.9 21.5 %all-to-all-start.3 = ((bf16[64,16,512]{2,1,0:T(8,128)(2,1)}), bf16[64,16,512]{2,1,0:T(8,128)(2,1)S(1)}, u32[]{:S(2)}, u32[]{:S(2)}) async-start(bf16[64,16,512]{2,1,0:T(8,128)(2,1)} %broadcast_in_dim.13), calls=%async_computation.3 | async-start | bytes 2097152 | tf_op jit(solution)/shard_map/all_to_all | solution.py:36
  155.9 4.7 %collective-permute-start.2 = (f32[98,512]{1,0:T(8,128)S(1)}, f32[98,512]{1,0:T(8,128)S(1)}, u32[]{:S(2)}, u32[]{:S(2)}) collective-permute-start(f32[98,512]{1,0:T(8,128)S(1)} %slice.41), channel_id=1, source_target_pairs={{0,1},{1,0},{2,3},{3,2},{4,5},{5,4},{6,7},{7,6},{8,9},{9,8},{10,11... | collective-permute-start | bytes 602120 | tf_op jit(solution)/shard_map/ppermute | solution.py:27

commit v5 on v4

--- a/solution.py
+++ b/solution.py
@@ -52,13 +52,25 @@
 SMEM = pl.BlockSpec(memory_space=pltpu.SMEM)
 
 
-def embed_kernel(cuts, f_ref, w_ref, out_ref, copies_ref, weight, sems):
+def embed_kernel(cuts, core_ref, f_ref, w_ref, out_ref, parcel_ref, weight, sems):
     copies = [
         pltpu.make_async_copy(w_ref.at[pl.ds(a, b - a)], weight.at[pl.ds(a, b - a)], sems.at[k])
         for k, (a, b) in enumerate(zip(cuts, cuts[1:]))
     ]
     for copy in copies:
         copy.start()
+    chips = parcel_ref.shape[0]
+    own, wide = f_ref.shape
+    depth = out_ref.shape[1]
+    fcols = wide // (2 * chips)
+    lower = core_ref[0] == 0
+    pad = jnp.zeros((own, 128 - fcols), bf16)
+    for chip in range(chips):
+        at = 2 * chip * fcols
+        first = jnp.concatenate([f_ref[:, at : at + fcols], pad], axis=1)
+        second = jnp.concatenate([f_ref[:, at + fcols : at + 2 * fcols], pad], axis=1)
+        parcel_ref[chip, :, depth : depth + 128] = jnp.where(lower, first, second)
+        parcel_ref[chip, :, depth + 128 :] = jnp.where(lower, second, first)
     total = None
     for copy, a, b in zip(copies, cuts, cuts[1:]):
         copy.wait()
@@ -66,27 +78,27 @@
         total = product if total is None else total + product
     rows = total.astype(bf16)
     out_ref[...] = rows
-    for chip in range(copies_ref.shape[0]):
-        copies_ref[chip] = rows
-
-
-def embedded_rows(features, weight, chips, cuts):
+    for chip in range(chips):
+        parcel_ref[chip, :, :depth] = rows
+
+
+def embedded_rows(core, features, weight, chips, cuts):
     own, wide = features.shape
     depth = weight.shape[1]
     return pl.pallas_call(
         functools.partial(embed_kernel, cuts),
-        in_specs=[VMEM, ANY],
+        in_specs=[SMEM, VMEM, ANY],
         out_specs=[VMEM, VMEM],
         out_shape=[
             jax.ShapeDtypeStruct((own, depth), bf16),
-            jax.ShapeDtypeStruct((chips, own, depth), bf16),
+            jax.ShapeDtypeStruct((chips, own, depth + 256), bf16),
         ],
         scratch_shapes=[pltpu.VMEM((wide, depth), bf16), pltpu.SemaphoreType.DMA((len(cuts) - 1,))],
         cost_estimate=pl.CostEstimate(
             flops=2 * own * wide * depth, bytes_accessed=2 * wide * depth, transcendentals=0
         ),
         name="embed",
-    )(features, weight)
+    )(core, features, weight)
 
 
 def targets_kernel(batch, ids_ref, busy_ref, own_ref, other_ref, goal_ref, centers, found, sems):
@@ -230,8 +242,8 @@
 
 
 def exponentials(ids, x, goal, own, other, chips, early, rows=1024, lanes=2):
-    samples, depth = x.shape
-    count = own.shape[0]
+    samples = x.shape[0]
+    count, depth = own.shape
     steps = count // rows
     late = 2 * steps - early
     fixed = lambda i: (0, 0)
@@ -324,7 +336,7 @@
     )(exps, low, start)
 
 
-def settle_kernel(ids_ref, cos_ref, report_ref, pull_ref, goal_ref, emb_ref, cargo_ref, parcel_ref, scaled_ref,
+def settle_kernel(ids_ref, cos_ref, report_ref, pull_ref, goal_ref, emb_ref, parcel_ref, scaled_ref,
                   patch_ref, sums_ref, wide_scale, wide_target):
     i = pl.program_id(0)
     rows, depth = goal_ref.shape
@@ -346,14 +358,12 @@
     span = pl.ds(pl.multiple_of(i * rows, rows), rows)
     scale = jnp.concatenate([wide_scale[span, :]] * (depth // 128), axis=1)
     at_target = jnp.concatenate([wide_target[span, :]] * (depth // 128), axis=1)
-    parcel_ref[:, :depth] = (pull_ref[...] * scale + at_target * goal_ref[...].astype(f32)).astype(bf16)
-    parcel_ref[:, depth:] = cargo_ref[...]
+    parcel_ref[...] = (pull_ref[...] * scale + at_target * goal_ref[...].astype(f32)).astype(bf16)
     scaled_ref[...] = (emb_ref[...].astype(f32) * scale).astype(bf16)
 
 
-def settled(ids, target_cos, report, pull, goal, emb, cargo, rows=512):
+def settled(ids, target_cos, report, pull, goal, emb, rows=512):
     samples, depth = emb.shape
-    extra = cargo.shape[1]
     fixed = lambda i: (0, 0)
     step = lambda i: (i, 0)
     row = pl.BlockSpec((1, samples), fixed)
@@ -361,16 +371,15 @@
         settle_kernel,
         grid=(samples // rows,),
         in_specs=[row, row, pl.BlockSpec(report.shape, lambda i: (0, 0, 0))]
-        + [pl.BlockSpec((rows, depth), step)] * 3
-        + [pl.BlockSpec((rows, extra), step)],
+        + [pl.BlockSpec((rows, depth), step)] * 3,
         out_specs=[
-            pl.BlockSpec((rows, depth + extra), step),
+            pl.BlockSpec((rows, depth), step),
             pl.BlockSpec((rows, depth), step),
             row,
             pl.BlockSpec((1, report.shape[2]), fixed),
         ],
         out_shape=[
-            jax.ShapeDtypeStruct((samples, depth + extra), bf16),
+            jax.ShapeDtypeStruct((samples, depth), bf16),
             jax.ShapeDtypeStruct((samples, depth), bf16),
             jax.ShapeDtypeStruct((1, samples), f32),
             jax.ShapeDtypeStruct((1, report.shape[2]), f32),
@@ -380,7 +389,7 @@
             flops=8 * samples * depth, bytes_accessed=14 * samples * depth, transcendentals=0
         ),
         name="settle",
-    )(ids, target_cos, report, pull, goal, emb, cargo)
+    )(ids, target_cos, report, pull, goal, emb)
 
 
 def push_kernel(base, final, ids_ref, patch_ref, emb_ref, exp_ref, *refs):
@@ -447,8 +456,8 @@
 
     other_centers = swapped(centers)
     cuts = tuple(range(0, wide, 1792)) + (wide,)
-    embedded, copies = embedded_rows(features, fc_weight, chips, cuts)
-    x = to_chips(copies).reshape(samples, depth)
+    embedded, parcel = embedded_rows(core.reshape(1), features, fc_weight, chips, cuts)
+    x = to_chips(parcel).reshape(samples, depth + 256)
 
     by_core = labels.reshape(chips, 2, own)
     my_labels = jnp.where(core == 0, by_core[:, 0], by_core[:, 1]).reshape(1, samples)
@@ -457,22 +466,13 @@
     turned_ids = jnp.where(core == 0, local, (local + class_rows) % (2 * class_rows))
     ids = jnp.where(inside, turned_ids, -1)
 
-    split = features.reshape(own, chips, 2, wide // (2 * chips))
-    mine = jnp.where(core == 0, split[:, :, 0], split[:, :, 1])
-    theirs = jnp.where(core == 0, split[:, :, 1], split[:, :, 0])
-    fcols = mine.shape[-1]
-    pad = ((0, 0), (0, 0), (0, 128 - fcols))
-    cargo = jnp.concatenate([jnp.pad(mine.swapaxes(0, 1), pad), jnp.pad(theirs.swapaxes(0, 1), pad)], axis=2)
-
     goal = target_directions(ids, own, centers, other_centers)
     early = 6
     exps, low, pull, emb_low, report, target_cos = exponentials(ids, x, goal, centers, other_centers, chips, early)
     report = to_chips(report)
     pull = pulled(exps, low, pull, early)
-    parcel, scaled, patch, report = settled(
-        ids, target_cos, report, pull, goal, emb_low, cargo.reshape(samples, 256)
-    )
-    parcel = to_chips(parcel.reshape(chips, own, depth + 256))
+    parcel, scaled, patch, report = settled(ids, target_cos, report, pull, goal, emb_low)
+    parcel = to_chips(parcel.reshape(chips, own, depth))
 
     other_push = pushed(ids, patch, scaled, exps, 1)
     other_push = swapped(other_push)
@@ -481,13 +481,14 @@
     own_float = embedded.astype(f32)
     inv_emb = inverse_norm(own_float, 1)
     emb_dir = own_float * inv_emb
-    grad_dir = jnp.sum(parcel[:, :, :depth].astype(f32), axis=0)
+    grad_dir = jnp.sum(parcel.astype(f32), axis=0)
     grad_emb = (
         (grad_dir - emb_dir * jnp.sum(grad_dir * emb_dir, axis=1, keepdims=True)) * inv_emb
     ).astype(bf16)
     grads = from_chips(grad_emb).reshape(samples, depth)
 
-    columns = parcel[:, :, depth:].reshape(samples, 256)
+    fcols = wide // (2 * chips)
+    columns = x[:, depth:]
     both = lax.dot_general(columns, grads, (((0,), (0,)), ((), ())), preferred_element_type=f32)
     theirs_fc = swapped(both[128 : 128 + fcols])
     grad_fc = both[:fcols] + theirs_fc

time: 174 us -> 169 us (0.971)
  blocking collectives: 0 us -> 21.5 us
  waiting for transfers between devices: 41.7 us -> 29.4 us
  starting transfers between devices: 39.4 us -> 30.1 us
  local copies, waits for them, and re-layouts: 6.69 us -> 2.73 us
    all_to_all x0 -> x1, blocking collectives: none -> 21.5 us  [from_chips(): return lax.all_to_all(copies, CHIP, split_axis=0, concat_axis=0, tiled=True)]
    all_to_all x1 -> x0, waiting for transfers between devices: 16.3 us -> none  [from_chips(): return lax.all_to_all(copies, CHIP, split_axis=0, concat_axis=0, tiled=True)]
    all_to_all x1 -> x0, starting transfers between devices: 5.17 us -> none  [from_chips(): return lax.all_to_all(copies, CHIP, split_axis=0, concat_axis=0, tiled=True)]
    all_to_all x3, starting transfers between devices: 26.7 us -> 22.2 us  [to_chips(): return lax.all_to_all(x, CHIP, split_axis=0, concat_axis=0, tiled=True)]
    all_to_all x3, waiting for transfers between devices: 25.4 us -> 29.4 us  [to_chips(): return lax.all_to_all(x, CHIP, split_axis=0, concat_axis=0, tiled=True)]
    reshape x1 -> x0, local copies, waits for them, and re-layouts: 1.94 us -> none  [step(): split = features.reshape(own, chips, 2, wide // (2 * chips))]
  transfers between devices with their start and end apart: 7 -> 6, of which waited for: 3 -> 3; matrix products, arithmetic and copies ran while one was open for 7% -> 4% of each run, Pallas kernels for 15% -> 15%
where the time goes in v5:
time: 169 us; the launch traced here: 168 us
  Pallas kernels  77.4 us (46%)
  starting transfers between devices  30.1 us (18%)
  waiting for transfers between devices  29.4 us (17%)
  blocking collectives  21.5 us (13%)
  other arithmetic  4.57 us (3%)
  local copies, waits for them, and re-layouts  2.73 us (2%)
    all_to_all x3, waiting for transfers between devices, to_chips(): return lax.all_to_all(x, CHIP, split_axis=0, concat_axis=0, tiled=True)  29.4 us
    pallas_call x1, Pallas kernels, exponentials(): pl.pallas_call(functools.partial(exp_kernel, steps, early, lanes), grid=(...  26.6 us
    all_to_all x3, starting transfers between devices, to_chips(): return lax.all_to_all(x, CHIP, split_axis=0, concat_axis=0, tiled=True)  22.2 us
    all_to_all x1, blocking collectives, from_chips(): return lax.all_to_all(copies, CHIP, split_axis=0, concat_axis=0, tiled=True)  21.5 us
    pallas_call x2, Pallas kernels, pushed(): pl.pallas_call(functools.partial(push_kernel, base, final), grid=(count /...  21.4 us
    pallas_call x1, Pallas kernels, target_directions(): pl.pallas_call(functools.partial(targets_kernel, batch), in_specs=[SMEM,...  11.8 us
    ppermute x3, starting transfers between devices, swapped(): return lax.ppermute(x, CORE, [(0, 1), (1, 0)])  7.83 us
    pallas_call x1, Pallas kernels, embedded_rows(): pl.pallas_call(functools.partial(embed_kernel, cuts), in_specs=[SMEM, VME...  7.57 us
  transfers between devices with their start and end apart: 6, of which 3 were waited for; matrix products, arithmetic and copies ran while one was open for 4% of the time, Pallas kernels for 15%

profile of v5, /device:TPU:1, one launch (start us, length us, event | category | flops | bytes accessed | tf_op | source)
XLA Modules:
  0.0 167.8 jit_solution(13463635325996501214)
XLA Ops:
  0.6 1.5 collective-permute-start
  2.1 7.6 %embed.1 = (bf16[16,512]{1,0:T(8,128)(2,1)}, bf16[64,16,768]{2,1,0:T(8,128)(2,1)}) custom-call(s32[1]{0:T(128)} %bitcast.core_ref, bf16[16,12544]{1,0:T(8,128)(2,1)} %f_ref.1, bf16[12544,512]{1,0:T(8,128)(2,1)} %w_ref.1), custom_call_target="tpu_custom_call" | custom-call | flops 205520896 | bytes 12845056 | tf_op jit(solution)/shard_map/embed/pallas_call | solution.py:88
  9.7 0.0 copy-start.3
  9.7 11.3 %all-to-all-start = ((bf16[64,16,768]{2,1,0:T(8,128)(2,1)}), bf16[64,16,768]{2,1,0:T(8,128)(2,1)S(1)}, u32[]{:S(2)}, u32[]{:S(2)}) async-start(bf16[64,16,768]{2,1,0:T(8,128)(2,1)} %get-tuple-element.15), calls=%async_computation | async-start | bytes 3145728 | tf_op jit(solution)/shard_map/all_to_all | solution.py:31
  21.0 0.0 copy-done.3
  21.0 0.1 reshape.131
  21.1 0.5 broadcast.134
  21.6 0.8 fusion.16
  22.4 0.1 sub.32
  22.5 0.6 fusion.12.busy_ref
  23.1 0.6 and_select_fusion.1.ids_ref
  23.7 0.0 collective-permute-done.other_ref
  23.7 11.8 %targets.1.goal_ref = bf16[1024,512]{1,0:T(8,128)(2,1)} custom-call(s32[1,1024]{1,0:T(1,128)} %and_select_fusion.1.ids_ref, s32[64]{0:T(128)} %fusion.12.busy_ref, bf16[4096,512]{1,0:T(8,128)(2,1)} %refs_0_.1, bf16[4096,512]{1,0:T(8,128)(2,1)} %collective-permute-done.other_ref), custom_call_target="tpu_custom_call" | custom-call | flops 4294967296 | bytes 8388608 | tf_op jit(solution)/shard_map/targets/pallas_call | solution.py:144
  35.5 8.6 %all-to-all-done = bf16[64,16,768]{2,1,0:T(8,128)(2,1)S(1)} async-done(((bf16[64,16,768]{2,1,0:T(8,128)(2,1)}), bf16[64,16,768]{2,1,0:T(8,128)(2,1)S(1)}, u32[]{:S(2)}, u32[]{:S(2)}) %all-to-all-start) | async-done | bytes 1572896 | tf_op jit(solution)/shard_map/all_to_all | solution.py:31
  44.1 0.0 copy-start
  44.1 1.1 copy-done
  45.2 26.6 %exponentials.1 = (bf16[1024,8192]{1,0:T(8,128)(2,1)}, bf16[2048,512]{1,0:T(8,128)(2,1)}, f32[1024,512]{1,0:T(8,128)}, bf16[1024,512]{1,0:T(8,128)(2,1)}, f32[64,1,1152]{2,1,0:T(1,128)}, /*index=5*/f32[1,1024]{1,0:T(1,128)}) custom-call(s32[1,1024]{1,0:T(1,128)} %and_select_fusion.1.ids_ref, bf16[1024,768]{1,0:T(8,128)(2,1)} %bitcast.8, ...), custom_call_target="tpu_custom_call" | custom-call | flops 8589934592 | bytes 16777216 | tf_op jit(solution)/shard_map/exponentials/pallas_call | solution.py:250
  71.8 5.3 %all-to-all-start.1 = ((f32[64,1,1152]{2,1,0:T(1,128)}), f32[64,1,1152]{2,1,0:T(1,128)S(1)}, u32[]{:S(2)}, u32[]{:S(2)}) async-start(f32[64,1,1152]{2,1,0:T(1,128)} %get-tuple-element.17), calls=%async_computation.1 | async-start | bytes 589824 | tf_op jit(solution)/shard_map/all_to_all | solution.py:31
  77.1 6.3 %pull.1.pull_ref = f32[1024,512]{1,0:T(8,128)} custom-call(bf16[1024,8192]{1,0:T(8,128)(2,1)} %get-tuple-element.18.exp_ref, bf16[2048,512]{1,0:T(8,128)(2,1)} %get-tuple-element.19.low_ref, f32[1024,512]{1,0:T(8,128)} %get-tuple-element.20.start_ref), custom_call_target="tpu_custom_call" | custom-call | flops 2147483648 | bytes 6291456 | tf_op jit(solution)/shard_map/pull/pallas_call | solution.py:320
  83.5 3.1 %all-to-all-done.1.report_ref = f32[64,1,1152]{2,1,0:T(1,128)S(1)} async-done(((f32[64,1,1152]{2,1,0:T(1,128)}), f32[64,1,1152]{2,1,0:T(1,128)S(1)}, u32[]{:S(2)}, u32[]{:S(2)}) %all-to-all-start.1) | async-done | bytes 294944 | tf_op jit(solution)/shard_map/all_to_all | solution.py:31
  86.6 0.0 copy-start.1
  86.6 0.7 copy-done.1
  87.3 3.8 %settle.1 = (bf16[1024,512]{1,0:T(8,128)(2,1)}, bf16[1024,512]{1,0:T(8,128)(2,1)}, f32[1,1024]{1,0:T(1,128)}, f32[1,1152]{1,0:T(1,128)}) custom-call(s32[1,1024]{1,0:T(1,128)} %and_select_fusion.1.ids_ref, f32[1,1024]{1,0:T(1,128)} %get-tuple-element.16.cos_ref, f32[64,1,1152]{2,1,0:T(1,128)} %copy-done.1, f32[1024,512]{1,0:T(8,128)} %pull.1.pull_ref, ...), custom_call_target="tpu_custom_call" | custom-call | flops 4194304 | bytes 7340032 | tf_op jit(solution)/shard_map/settle/pallas_call | solution.py:370
  91.1 9.3 %shard_map.67 = bf16[4096,512]{1,0:T(8,128)(2,1)} custom-call(s32[1,1024]{1,0:T(1,128)} %and_select_fusion.1.ids_ref, f32[1,1024]{1,0:T(1,128)} %get-tuple-element.23.patch_ref, bf16[1024,512]{1,0:T(8,128)(2,1)} %get-tuple-element.24.emb_ref, bf16[1024,8192]{1,0:T(8,128)(2,1)} %get-tuple-element.18.exp_ref), custom_call_target="tpu_custom_call" | custom-call | flops 4294967296 | bytes 8388608 | tf_op jit(solution)/shard_map/pallas_call | solution.py:430
  100.3 0.0 copy-start.2
  100.3 3.3 %collective-permute-start.1 = (bf16[4096,512]{1,0:T(8,128)(2,1)}, bf16[4096,512]{1,0:T(8,128)(2,1)}, u32[]{:S(2)}, u32[]{:S(2)}) collective-permute-start(bf16[4096,512]{1,0:T(8,128)(2,1)} %shard_map.67), channel_id=1, source_target_pairs={{0,1},{1,0},{2,3},{3,2},{4,5},{5,4},{6,7},{7,6},{8,9},{9,8},{10,11... | collective-permute-start | bytes 12582920 | tf_op jit(solution)/shard_map/ppermute | solution.py:27
  103.7 5.7 %all-to-all-start.2 = ((bf16[64,16,512]{2,1,0:T(8,128)(2,1)}), bf16[64,16,512]{2,1,0:T(8,128)(2,1)S(1)}, u32[]{:S(2)}, u32[]{:S(2)}) async-start(bf16[64,16,512]{2,1,0:T(8,128)(2,1)} %bitcast.4), calls=%async_computation.2 | async-start | bytes 2097152 | tf_op jit(solution)/shard_map/all_to_all | solution.py:31
  109.3 0.0 copy-done.2
  109.3 0.1 fusion.8
  109.5 17.7 %all-to-all-done.2 = bf16[64,16,512]{2,1,0:T(8,128)(2,1)S(1)} async-done(((bf16[64,16,512]{2,1,0:T(8,128)(2,1)}), bf16[64,16,512]{2,1,0:T(8,128)(2,1)S(1)}, u32[]{:S(2)}, u32[]{:S(2)}) %all-to-all-start.2) | async-done | bytes 1048608 | tf_op jit(solution)/shard_map/all_to_all | solution.py:31
  127.1 0.2 convert_reduce_fusion
  127.3 0.2 fusion.4
  127.5 0.1 fusion.7
  127.6 0.1 broadcast_in_dim.13
  127.7 21.5 %all_to_all.20 = bf16[64,16,512]{2,1,0:T(8,128)(2,1)S(1)} all-to-all(bf16[64,16,512]{2,1,0:T(8,128)(2,1)S(1)} %broadcast_in_dim.13), channel_id=1, replica_groups=mesh['cls_0'=4,'cls_1'=4,'cls_2'=4,'cls_3'=2] {'cls_0','cls_1','cls_2'}, dimensions={0} | all-to-all | bytes 2097152 | tf_op jit(solution)/shard_map/all_to_all | solution.py:36
  149.2 1.5 fusion
  150.7 3.0 %collective-permute-start.2 = (f32[98,512]{1,0:T(8,128)S(1)}, f32[98,512]{1,0:T(8,128)S(1)}, u32[]{:S(2)}, u32[]{:S(2)}) collective-permute-start(f32[98,512]{1,0:T(8,128)S(1)} %slice.24), channel_id=1, source_target_pairs={{0,1},{1,0},{2,3},{3,2},{4,5},{5,4},{6,7},{7,6},{8,9},{9,8},{10,11... | collective-permute-start | bytes 602120 | tf_op jit(solution)/shard_map/ppermute | solution.py:27
  153.7 1.3 subtract_bitcast_fusion
  155.0 0.0 collective-permute-done.2
  155.0 0.7 slice_add_fusion
  155.7 0.0 collective-permute-done.1.refs_1_
  155.7 12.1 %shard_map.68 = bf16[4096,512]{1,0:T(8,128)(2,1)} custom-call(s32[1,1024]{1,0:T(1,128)} %and_select_fusion.1.ids_ref, f32[1,1024]{1,0:T(1,128)} %get-tuple-element.23.patch_ref, bf16[1024,512]{1,0:T(8,128)(2,1)} %get-tuple-element.24.emb_ref, bf16[1024,8192]{1,0:T(8,128)(2,1)} %get-tuple-element.18.exp_ref, bf16[4096,512]{1,0:T(8,128)(2,1)} %refs_0_.1, ...), custom_call_target="tpu_custom_call" | custom-call | flops 4294967296 | bytes 8388608 | tf_op jit(solution)/shard_map/pallas_call | solution.py:430
  (2 shorter events, 0.0 us)
Async XLA Ops:
  0.6 23.1 %collective-permute-start = (bf16[4096,512]{1,0:T(8,128)(2,1)}, bf16[4096,512]{1,0:T(8,128)(2,1)}, u32[]{:S(2)}, u32[]{:S(2)}) collective-permute-start(bf16[4096,512]{1,0:T(8,128)(2,1)} %refs_0_.1), channel_id=1, source_target_pairs={{0,1},{1,0},{2,3},{3,2},{4,5},{5,4},{6,7},{7,6},{8,9},{9,8},{10,11... | collective-permute-start | bytes 12582920 | tf_op jit(solution)/shard_map/ppermute | solution.py:27
  9.7 11.3 %copy-start.3 = (s32[2048]{0:T(1024)S(1)}, s32[2048]{0:T(1024)}, u32[]{:S(2)}) copy-start(s32[2048]{0:T(1024)} %param.7) | copy-start | bytes 24580
  9.7 34.4 %all-to-all-start = ((bf16[64,16,768]{2,1,0:T(8,128)(2,1)}), bf16[64,16,768]{2,1,0:T(8,128)(2,1)S(1)}, u32[]{:S(2)}, u32[]{:S(2)}) async-start(bf16[64,16,768]{2,1,0:T(8,128)(2,1)} %get-tuple-element.15), calls=%async_computation | async-start | bytes 3145728 | tf_op jit(solution)/shard_map/all_to_all | solution.py:31
  44.1 1.1 copy-start
  71.8 14.7 %all-to-all-start.1 = ((f32[64,1,1152]{2,1,0:T(1,128)}), f32[64,1,1152]{2,1,0:T(1,128)S(1)}, u32[]{:S(2)}, u32[]{:S(2)}) async-start(f32[64,1,1152]{2,1,0:T(1,128)} %get-tuple-element.17), calls=%async_computation.1 | async-start | bytes 589824 | tf_op jit(solution)/shard_map/all_to_all | solution.py:31
  86.6 0.7 copy-start.1
  100.3 9.0 %copy-start.2 = (bf16[16,512]{1,0:T(8,128)(2,1)S(1)}, bf16[16,512]{1,0:T(8,128)(2,1)}, u32[]{:S(2)}) copy-start(bf16[16,512]{1,0:T(8,128)(2,1)} %get-tuple-element.26) | copy-start | bytes 49156
  100.3 55.4 %collective-permute-start.1 = (bf16[4096,512]{1,0:T(8,128)(2,1)}, bf16[4096,512]{1,0:T(8,128)(2,1)}, u32[]{:S(2)}, u32[]{:S(2)}) collective-permute-start(bf16[4096,512]{1,0:T(8,128)(2,1)} %shard_map.67), channel_id=1, source_target_pairs={{0,1},{1,0},{2,3},{3,2},{4,5},{5,4},{6,7},{7,6},{8,9},{9,8},{10,11... | collective-permute-start | bytes 12582920 | tf_op jit(solution)/shard_map/ppermute | solution.py:27
  103.7 23.5 %all-to-all-start.2 = ((bf16[64,16,512]{2,1,0:T(8,128)(2,1)}), bf16[64,16,512]{2,1,0:T(8,128)(2,1)S(1)}, u32[]{:S(2)}, u32[]{:S(2)}) async-start(bf16[64,16,512]{2,1,0:T(8,128)(2,1)} %bitcast.4), calls=%async_computation.2 | async-start | bytes 2097152 | tf_op jit(solution)/shard_map/all_to_all | solution.py:31
  150.7 4.3 %collective-permute-start.2 = (f32[98,512]{1,0:T(8,128)S(1)}, f32[98,512]{1,0:T(8,128)S(1)}, u32[]{:S(2)}, u32[]{:S(2)}) collective-permute-start(f32[98,512]{1,0:T(8,128)S(1)} %slice.24), channel_id=1, source_target_pairs={{0,1},{1,0},{2,3},{3,2},{4,5},{5,4},{6,7},{7,6},{8,9},{9,8},{10,11... | collective-permute-start | bytes 602120 | tf_op jit(solution)/shard_map/ppermute | solution.py:27

commit v6 on v5

--- a/solution.py
+++ b/solution.py
@@ -101,17 +101,30 @@
     )(core, features, weight)
 
 
-def targets_kernel(batch, ids_ref, busy_ref, own_ref, other_ref, goal_ref, centers, found, sems):
+def centers_kernel(batch, rows, ids_ref, busy_ref, own_ref, other_ref, low_ref, goal_ref, centers, found, in_sems,
+                   out_sems):
     count, depth = own_ref.shape
-    copies = [
-        pltpu.make_async_copy(part, centers.at[pl.ds(k * count, count)], sems.at[k])
-        for k, part in enumerate((own_ref, other_ref))
-    ]
-    for copy in copies:
-        copy.start()
+    steps = 2 * count // rows
+
+    def arrival(i):
+        source = own_ref if i * rows < count else other_ref
+        return pltpu.make_async_copy(
+            source.at[pl.ds(i * rows % count, rows)], centers.at[pl.ds(i * rows, rows)], in_sems.at[i]
+        )
+
+    def departure(i):
+        span = pl.ds(i * rows, rows)
+        return pltpu.make_async_copy(centers.at[span], low_ref.at[span], out_sems.at[i])
+
+    for i in range(steps):
+        arrival(i).start()
     found[...] = jnp.zeros_like(found)
-    for copy in copies:
-        copy.wait()
+    for i in range(steps):
+        arrival(i).wait()
+        block = centers[i * rows : (i + 1) * rows, :].astype(f32)
+        centers[i * rows : (i + 1) * rows, :] = (block * inverse_norm(block, 1)).astype(bf16)
+        if i > 0:
+            departure(i - 1).start()
     spot = lax.broadcasted_iota(jnp.int32, (16, depth), 0)
 
     def group(g, carry):
@@ -133,26 +146,33 @@
         return carry
 
     lax.fori_loop(0, busy_ref.shape[0], group, 0)
-    rows = found[...]
-    goal_ref[...] = (rows * inverse_norm(rows, 1)).astype(bf16)
-
-
-def target_directions(ids, batch, own, other):
+    departure(steps - 1).start()
+    goal_ref[...] = found[...].astype(bf16)
+    for i in range(steps):
+        departure(i).wait()
+
+
+def center_directions(ids, batch, own, other, rows=1024):
     count, depth = own.shape
     samples = ids.shape[1]
+    steps = 2 * count // rows
     busy = jnp.max(ids.reshape(samples // batch, batch), axis=1)
     return pl.pallas_call(
-        functools.partial(targets_kernel, batch),
+        functools.partial(centers_kernel, batch, rows),
         in_specs=[SMEM, SMEM, ANY, ANY],
-        out_specs=VMEM,
-        out_shape=jax.ShapeDtypeStruct((samples, depth), bf16),
+        out_specs=[ANY, VMEM],
+        out_shape=[
+            jax.ShapeDtypeStruct((2 * count, depth), bf16),
+            jax.ShapeDtypeStruct((samples, depth), bf16),
+        ],
         scratch_shapes=[
             pltpu.VMEM((2 * count, depth), bf16),
             pltpu.VMEM((samples, depth), f32),
-            pltpu.SemaphoreType.DMA((2,)),
+            pltpu.SemaphoreType.DMA((steps,)),
+            pltpu.SemaphoreType.DMA((steps,)),
         ],
         cost_estimate=pl.CostEstimate(
-            flops=2 * count * depth * samples, bytes_accessed=4 * count * depth, transcendentals=0
+            flops=2 * count * depth * samples, bytes_accessed=8 * count * depth, transcendentals=0
         ),
         name="targets",
     )(ids, busy, own, other)
@@ -165,10 +185,10 @@
     return jnp.sum(part.T, axis=0, keepdims=True)
 
 
-def exp_kernel(steps, early, lanes, ids_ref, x_ref, goal_ref, own_ref, other_ref, exp_ref, low_ref, pull_ref, emb_ref,
+def exp_kernel(early, lanes, ids_ref, x_ref, goal_ref, low_ref, exp_ref, pull_ref, emb_ref,
                report_ref, cos_ref, wide_ids, scaled, row_sum, total):
     i = pl.program_id(0)
-    rows = own_ref.shape[0]
+    rows = low_ref.shape[0]
     samples = x_ref.shape[0]
     sub = samples // lanes
 
@@ -183,8 +203,6 @@
         total[...] = jnp.zeros_like(total)
 
     def chunk(with_pull):
-        block = jnp.where(i < steps, own_ref[...], other_ref[...]).astype(f32)
-        low_ref[...] = (block * inverse_norm(block, 1)).astype(bf16)
         columns = lax.broadcasted_iota(jnp.int32, (sub, 128), 1)
 
         def products(m):
@@ -223,7 +241,7 @@
     def _():
         pull_ref[...] = total[...]
 
-    @pl.when(i == 2 * steps - 1)
+    @pl.when(i == pl.num_programs(0) - 1)
     def _():
         target_cos = row_of(goal_ref[...].astype(f32) * scaled[...].astype(f32)) * (1.0 / logit_scale)
         cos_ref[...] = target_cos
@@ -241,33 +259,28 @@
             report_ref[chip, :, samples:] = jnp.where(theirs, logit[:, k * 128 : (k + 1) * 128], 0.0)
 
 
-def exponentials(ids, x, goal, own, other, chips, early, rows=1024, lanes=2):
+def exponentials(ids, x, goal, low, chips, early, rows=1024, lanes=2):
     samples = x.shape[0]
-    count, depth = own.shape
-    steps = count // rows
-    late = 2 * steps - early
+    count, depth = low.shape
     fixed = lambda i: (0, 0)
     return pl.pallas_call(
-        functools.partial(exp_kernel, steps, early, lanes),
-        grid=(2 * steps,),
+        functools.partial(exp_kernel, early, lanes),
+        grid=(count // rows,),
         in_specs=[
             pl.BlockSpec((1, samples), fixed),
             pl.BlockSpec((samples, depth), fixed),
             pl.BlockSpec((samples, depth), fixed),
-            pl.BlockSpec((rows, depth), lambda i: (jnp.minimum(i, steps - 1), 0)),
-            pl.BlockSpec((rows, depth), lambda i: (jnp.maximum(i - steps, 0), 0)),
+            pl.BlockSpec((rows, depth), lambda i: (i, 0)),
         ],
         out_specs=[
             pl.BlockSpec((samples, rows), lambda i: (0, i)),
-            pl.BlockSpec((rows, depth), lambda i: (jnp.maximum(i - early, 0), 0)),
             pl.BlockSpec((samples, depth), fixed),
             pl.BlockSpec((samples, depth), fixed),
             pl.BlockSpec((chips, 1, samples + 128), lambda i: (0, 0, 0)),
             pl.BlockSpec((1, samples), fixed),
         ],
         out_shape=[
-            jax.ShapeDtypeStruct((samples, 2 * count), bf16),
-            jax.ShapeDtypeStruct((late * rows, depth), bf16),
+            jax.ShapeDtypeStruct((samples, count), bf16),
             jax.ShapeDtypeStruct((samples, depth), f32),
             jax.ShapeDtypeStruct((samples, depth), bf16),
             jax.ShapeDtypeStruct((chips, 1, samples + 128), f32),
@@ -280,16 +293,16 @@
             pltpu.VMEM((samples, depth), f32),
         ],
         cost_estimate=pl.CostEstimate(
-            flops=4 * count * depth * samples,
-            bytes_accessed=8 * count * depth,
-            transcendentals=2 * count * samples,
+            flops=2 * count * depth * samples,
+            bytes_accessed=4 * count * depth,
+            transcendentals=count * samples,
         ),
         name="exponentials",
-    )(ids, x, goal, own, other)
+    )(ids, x, goal, low)
 
 
 def pull_kernel(early, rows, exp_ref, low_ref, start_ref, out_ref, exps, lows, exp_sems, low_sems, start_sem):
-    steps = low_ref.shape[0] // rows
+    steps = low_ref.shape[0] // rows - early
     start = pltpu.make_async_copy(start_ref, out_ref, start_sem)
 
     def fetch(i, slot):
@@ -297,7 +310,7 @@
             pltpu.make_async_copy(
                 exp_ref.at[:, pl.ds((early + i) * rows, rows)], exps.at[slot], exp_sems.at[slot]
             ),
-            pltpu.make_async_copy(low_ref.at[pl.ds(i * rows, rows)], lows.at[slot], low_sems.at[slot]),
+            pltpu.make_async_copy(low_ref.at[pl.ds((early + i) * rows, rows)], lows.at[slot], low_sems.at[slot]),
         )
 
     for i in range(steps):
@@ -316,7 +329,7 @@
 def pulled(exps, low, start, early, rows=1024):
     samples = exps.shape[0]
     count, depth = low.shape
-    steps = count // rows
+    steps = count // rows - early
     return pl.pallas_call(
         functools.partial(pull_kernel, early, rows),
         in_specs=[ANY, ANY, ANY],
@@ -330,7 +343,9 @@
             pltpu.SemaphoreType.DMA,
         ],
         cost_estimate=pl.CostEstimate(
-            flops=2 * count * depth * samples, bytes_accessed=2 * count * (depth + samples), transcendentals=0
+            flops=2 * steps * rows * depth * samples,
+            bytes_accessed=2 * steps * rows * (depth + samples),
+            transcendentals=0,
         ),
         name="pull",
     )(exps, low, start)
@@ -466,9 +481,9 @@
     turned_ids = jnp.where(core == 0, local, (local + class_rows) % (2 * class_rows))
     ids = jnp.where(inside, turned_ids, -1)
 
-    goal = target_directions(ids, own, centers, other_centers)
+    low, goal = center_directions(ids, own, centers, other_centers)
     early = 6
-    exps, low, pull, emb_low, report, target_cos = exponentials(ids, x, goal, centers, other_centers, chips, early)
+    exps, pull, emb_low, report, target_cos = exponentials(ids, x, goal, low, chips, early)
     report = to_chips(report)
     pull = pulled(exps, low, pull, early)
     parcel, scaled, patch, report = settled(ids, target_cos, report, pull, goal, emb_low)

time: 169 us -> 167 us (0.988)
  waiting for transfers between devices: 29.4 us -> 27 us
    all_to_all x3, waiting for transfers between devices: 29.4 us -> 27 us  [to_chips(): return lax.all_to_all(x, CHIP, split_axis=0, concat_axis=0, tiled=True)]
  transfers between devices with their start and end apart: 6 -> 6, of which waited for: 3 -> 3; matrix products, arithmetic and copies ran while one was open for 4% -> 4% of each run, Pallas kernels for 15% -> 17%
where the time goes in v6:
time: 167 us; the launch traced here: 166 us
  Pallas kernels  78 us (47%)
  starting transfers between devices  29.9 us (18%)
  waiting for transfers between devices  27 us (16%)
  blocking collectives  21.6 us (13%)
  other arithmetic  4.55 us (3%)
  local copies, waits for them, and re-layouts  2.72 us (2%)
    all_to_all x3, waiting for transfers between devices, to_chips(): return lax.all_to_all(x, CHIP, split_axis=0, concat_axis=0, tiled=True)  27 us
    pallas_call x1, Pallas kernels, exponentials(): pl.pallas_call(functools.partial(exp_kernel, early, lanes), grid=(count /...  24.6 us
    all_to_all x3, starting transfers between devices, to_chips(): return lax.all_to_all(x, CHIP, split_axis=0, concat_axis=0, tiled=True)  22.1 us
    all_to_all x1, blocking collectives, from_chips(): return lax.all_to_all(copies, CHIP, split_axis=0, concat_axis=0, tiled=True)  21.6 us
    pallas_call x2, Pallas kernels, pushed(): pl.pallas_call(functools.partial(push_kernel, base, final), grid=(count /...  21.4 us
    pallas_call x1, Pallas kernels, center_directions(): pl.pallas_call(functools.partial(centers_kernel, batch, rows), in_specs=[...  14.3 us
    ppermute x3, starting transfers between devices, swapped(): return lax.ppermute(x, CORE, [(0, 1), (1, 0)])  7.8 us
    pallas_call x1, Pallas kernels, embedded_rows(): pl.pallas_call(functools.partial(embed_kernel, cuts), in_specs=[SMEM, VME...  7.58 us
  transfers between devices with their start and end apart: 6, of which 3 were waited for; matrix products, arithmetic and copies ran while one was open for 4% of the time, Pallas kernels for 17%

profile of v6, /device:TPU:1, one launch (start us, length us, event | category | flops | bytes accessed | tf_op | source)
XLA Modules:
  0.0 166.0 jit_solution(455699377436300885)
XLA Ops:
  0.6 1.5 collective-permute-start
  2.1 0.0 copy-start.3
  2.1 7.6 %embed.1 = (bf16[16,512]{1,0:T(8,128)(2,1)}, bf16[64,16,768]{2,1,0:T(8,128)(2,1)}) custom-call(s32[1]{0:T(128)} %bitcast.core_ref, bf16[16,12544]{1,0:T(8,128)(2,1)} %f_ref.1, bf16[12544,512]{1,0:T(8,128)(2,1)} %w_ref.1), custom_call_target="tpu_custom_call" | custom-call | flops 205520896 | bytes 12845056 | tf_op jit(solution)/shard_map/embed/pallas_call | solution.py:88
  9.7 11.3 %all-to-all-start = ((bf16[64,16,768]{2,1,0:T(8,128)(2,1)}), bf16[64,16,768]{2,1,0:T(8,128)(2,1)S(1)}, u32[]{:S(2)}, u32[]{:S(2)}) async-start(bf16[64,16,768]{2,1,0:T(8,128)(2,1)} %get-tuple-element.16), calls=%async_computation | async-start | bytes 3145728 | tf_op jit(solution)/shard_map/all_to_all | solution.py:31
  21.0 0.0 copy-done.3
  21.0 0.1 reshape.131
  21.1 0.5 broadcast.134
  21.6 0.8 fusion.16
  22.4 0.1 sub.32
  22.5 0.6 fusion.12.busy_ref
  23.1 0.6 and_select_fusion.1.ids_ref
  23.7 0.0 collective-permute-done.other_ref
  23.7 14.3 %targets.1 = (bf16[8192,512]{1,0:T(8,128)(2,1)}, bf16[1024,512]{1,0:T(8,128)(2,1)}) custom-call(s32[1,1024]{1,0:T(1,128)} %and_select_fusion.1.ids_ref, s32[64]{0:T(128)} %fusion.12.busy_ref, bf16[4096,512]{1,0:T(8,128)(2,1)} %refs_0_.1, bf16[4096,512]{1,0:T(8,128)(2,1)} %collective-permute-done.other_ref), custom_call_target="tpu_custom_call" | custom-call | flops 4294967296 | bytes 16777216 | tf_op jit(solution)/shard_map/targets/pallas_call | solution.py:160
  38.1 6.0 %all-to-all-done = bf16[64,16,768]{2,1,0:T(8,128)(2,1)S(1)} async-done(((bf16[64,16,768]{2,1,0:T(8,128)(2,1)}), bf16[64,16,768]{2,1,0:T(8,128)(2,1)S(1)}, u32[]{:S(2)}, u32[]{:S(2)}) %all-to-all-start) | async-done | bytes 1572896 | tf_op jit(solution)/shard_map/all_to_all | solution.py:31
  44.1 0.0 copy-start
  44.1 1.1 copy-done
  45.2 24.6 %exponentials.1 = (bf16[1024,8192]{1,0:T(8,128)(2,1)}, f32[1024,512]{1,0:T(8,128)}, bf16[1024,512]{1,0:T(8,128)(2,1)}, f32[64,1,1152]{2,1,0:T(1,128)}, f32[1,1024]{1,0:T(1,128)}) custom-call(s32[1,1024]{1,0:T(1,128)} %and_select_fusion.1.ids_ref, bf16[1024,768]{1,0:T(8,128)(2,1)} %bitcast.8, bf16[1024,512]{1,0:T(8,128)(2,1)} %get-tuple-element.17.goal_ref, ...), custom_call_target="tpu_custom_call" | custom-call | flops 8589934592 | bytes 16777216 | tf_op jit(solution)/shard_map/exponentials/pallas_call | solution.py:266
  69.9 5.1 %all-to-all-start.1 = ((f32[64,1,1152]{2,1,0:T(1,128)}), f32[64,1,1152]{2,1,0:T(1,128)S(1)}, u32[]{:S(2)}, u32[]{:S(2)}) async-start(f32[64,1,1152]{2,1,0:T(1,128)} %get-tuple-element.20), calls=%async_computation.1 | async-start | bytes 589824 | tf_op jit(solution)/shard_map/all_to_all | solution.py:31
  75.0 6.3 %pull.1.pull_ref = f32[1024,512]{1,0:T(8,128)} custom-call(bf16[1024,8192]{1,0:T(8,128)(2,1)} %get-tuple-element.21.exp_ref, bf16[8192,512]{1,0:T(8,128)(2,1)} %get-tuple-element.18.low_ref, f32[1024,512]{1,0:T(8,128)} %get-tuple-element.22.start_ref), custom_call_target="tpu_custom_call" | custom-call | flops 2147483648 | bytes 6291456 | tf_op jit(solution)/shard_map/pull/pallas_call | solution.py:333
  81.3 3.3 %all-to-all-done.1.report_ref = f32[64,1,1152]{2,1,0:T(1,128)S(1)} async-done(((f32[64,1,1152]{2,1,0:T(1,128)}), f32[64,1,1152]{2,1,0:T(1,128)S(1)}, u32[]{:S(2)}, u32[]{:S(2)}) %all-to-all-start.1) | async-done | bytes 294944 | tf_op jit(solution)/shard_map/all_to_all | solution.py:31
  84.6 0.0 copy-start.1
  84.6 0.7 copy-done.1
  85.3 3.8 %settle.1 = (bf16[1024,512]{1,0:T(8,128)(2,1)}, bf16[1024,512]{1,0:T(8,128)(2,1)}, f32[1,1024]{1,0:T(1,128)}, f32[1,1152]{1,0:T(1,128)}) custom-call(s32[1,1024]{1,0:T(1,128)} %and_select_fusion.1.ids_ref, f32[1,1024]{1,0:T(1,128)} %get-tuple-element.19.cos_ref, f32[64,1,1152]{2,1,0:T(1,128)} %copy-done.1, f32[1024,512]{1,0:T(8,128)} %pull.1.pull_ref, ...), custom_call_target="tpu_custom_call" | custom-call | flops 4194304 | bytes 7340032 | tf_op jit(solution)/shard_map/settle/pallas_call | solution.py:385
  89.1 0.0 copy-start.2
  89.1 9.3 %shard_map.67 = bf16[4096,512]{1,0:T(8,128)(2,1)} custom-call(s32[1,1024]{1,0:T(1,128)} %and_select_fusion.1.ids_ref, f32[1,1024]{1,0:T(1,128)} %get-tuple-element.25.patch_ref, bf16[1024,512]{1,0:T(8,128)(2,1)} %get-tuple-element.26.emb_ref, bf16[1024,8192]{1,0:T(8,128)(2,1)} %get-tuple-element.21.exp_ref), custom_call_target="tpu_custom_call" | custom-call | flops 4294967296 | bytes 8388608 | tf_op jit(solution)/shard_map/pallas_call | solution.py:445
  98.4 3.3 %collective-permute-start.1 = (bf16[4096,512]{1,0:T(8,128)(2,1)}, bf16[4096,512]{1,0:T(8,128)(2,1)}, u32[]{:S(2)}, u32[]{:S(2)}) collective-permute-start(bf16[4096,512]{1,0:T(8,128)(2,1)} %shard_map.67), channel_id=1, source_target_pairs={{0,1},{1,0},{2,3},{3,2},{4,5},{5,4},{6,7},{7,6},{8,9},{9,8},{10,11... | collective-permute-start | bytes 12582920 | tf_op jit(solution)/shard_map/ppermute | solution.py:27
  101.7 5.7 %all-to-all-start.2 = ((bf16[64,16,512]{2,1,0:T(8,128)(2,1)}), bf16[64,16,512]{2,1,0:T(8,128)(2,1)S(1)}, u32[]{:S(2)}, u32[]{:S(2)}) async-start(bf16[64,16,512]{2,1,0:T(8,128)(2,1)} %bitcast.4), calls=%async_computation.2 | async-start | bytes 2097152 | tf_op jit(solution)/shard_map/all_to_all | solution.py:31
  107.4 0.0 copy-done.2
  107.4 0.1 fusion.8
  107.5 17.8 %all-to-all-done.2 = bf16[64,16,512]{2,1,0:T(8,128)(2,1)S(1)} async-done(((bf16[64,16,512]{2,1,0:T(8,128)(2,1)}), bf16[64,16,512]{2,1,0:T(8,128)(2,1)S(1)}, u32[]{:S(2)}, u32[]{:S(2)}) %all-to-all-start.2) | async-done | bytes 1048608 | tf_op jit(solution)/shard_map/all_to_all | solution.py:31
  125.2 0.2 convert_reduce_fusion
  125.4 0.2 fusion.4
  125.6 0.1 fusion.7
  125.7 0.1 broadcast_in_dim.13
  125.8 21.6 %all_to_all.20 = bf16[64,16,512]{2,1,0:T(8,128)(2,1)S(1)} all-to-all(bf16[64,16,512]{2,1,0:T(8,128)(2,1)S(1)} %broadcast_in_dim.13), channel_id=1, replica_groups=mesh['cls_0'=4,'cls_1'=4,'cls_2'=4,'cls_3'=2] {'cls_0','cls_1','cls_2'}, dimensions={0} | all-to-all | bytes 2097152 | tf_op jit(solution)/shard_map/all_to_all | solution.py:36
  147.4 1.5 fusion
  148.9 3.0 %collective-permute-start.2 = (f32[98,512]{1,0:T(8,128)S(1)}, f32[98,512]{1,0:T(8,128)S(1)}, u32[]{:S(2)}, u32[]{:S(2)}) collective-permute-start(f32[98,512]{1,0:T(8,128)S(1)} %slice.24), channel_id=1, source_target_pairs={{0,1},{1,0},{2,3},{3,2},{4,5},{5,4},{6,7},{7,6},{8,9},{9,8},{10,11... | collective-permute-start | bytes 602120 | tf_op jit(solution)/shard_map/ppermute | solution.py:27
  151.9 1.3 subtract_bitcast_fusion
  153.2 0.0 collective-permute-done.2
  153.2 0.7 slice_add_fusion
  153.9 0.0 collective-permute-done.1.refs_1_
  153.9 12.1 %shard_map.68 = bf16[4096,512]{1,0:T(8,128)(2,1)} custom-call(s32[1,1024]{1,0:T(1,128)} %and_select_fusion.1.ids_ref, f32[1,1024]{1,0:T(1,128)} %get-tuple-element.25.patch_ref, bf16[1024,512]{1,0:T(8,128)(2,1)} %get-tuple-element.26.emb_ref, bf16[1024,8192]{1,0:T(8,128)(2,1)} %get-tuple-element.21.exp_ref, bf16[4096,512]{1,0:T(8,128)(2,1)} %refs_0_.1, ...), custom_call_target="tpu_custom_call" | custom-call | flops 4294967296 | bytes 8388608 | tf_op jit(solution)/shard_map/pallas_call | solution.py:445
  (2 shorter events, 0.0 us)
Async XLA Ops:
  0.6 23.1 %collective-permute-start = (bf16[4096,512]{1,0:T(8,128)(2,1)}, bf16[4096,512]{1,0:T(8,128)(2,1)}, u32[]{:S(2)}, u32[]{:S(2)}) collective-permute-start(bf16[4096,512]{1,0:T(8,128)(2,1)} %refs_0_.1), channel_id=1, source_target_pairs={{0,1},{1,0},{2,3},{3,2},{4,5},{5,4},{6,7},{7,6},{8,9},{9,8},{10,11... | collective-permute-start | bytes 12582920 | tf_op jit(solution)/shard_map/ppermute | solution.py:27
  2.1 18.9 %copy-start.3 = (s32[2048]{0:T(1024)S(1)}, s32[2048]{0:T(1024)}, u32[]{:S(2)}) copy-start(s32[2048]{0:T(1024)} %param.7) | copy-start | bytes 24580
  9.7 34.4 %all-to-all-start = ((bf16[64,16,768]{2,1,0:T(8,128)(2,1)}), bf16[64,16,768]{2,1,0:T(8,128)(2,1)S(1)}, u32[]{:S(2)}, u32[]{:S(2)}) async-start(bf16[64,16,768]{2,1,0:T(8,128)(2,1)} %get-tuple-element.16), calls=%async_computation | async-start | bytes 3145728 | tf_op jit(solution)/shard_map/all_to_all | solution.py:31
  44.1 1.1 copy-start
  69.9 14.7 %all-to-all-start.1 = ((f32[64,1,1152]{2,1,0:T(1,128)}), f32[64,1,1152]{2,1,0:T(1,128)S(1)}, u32[]{:S(2)}, u32[]{:S(2)}) async-start(f32[64,1,1152]{2,1,0:T(1,128)} %get-tuple-element.20), calls=%async_computation.1 | async-start | bytes 589824 | tf_op jit(solution)/shard_map/all_to_all | solution.py:31
  84.6 0.7 copy-start.1
  89.1 18.3 %copy-start.2 = (bf16[16,512]{1,0:T(8,128)(2,1)S(1)}, bf16[16,512]{1,0:T(8,128)(2,1)}, u32[]{:S(2)}) copy-start(bf16[16,512]{1,0:T(8,128)(2,1)} %get-tuple-element.28) | copy-start | bytes 49156
  98.4 55.5 %collective-permute-start.1 = (bf16[4096,512]{1,0:T(8,128)(2,1)}, bf16[4096,512]{1,0:T(8,128)(2,1)}, u32[]{:S(2)}, u32[]{:S(2)}) collective-permute-start(bf16[4096,512]{1,0:T(8,128)(2,1)} %shard_map.67), channel_id=1, source_target_pairs={{0,1},{1,0},{2,3},{3,2},{4,5},{5,4},{6,7},{7,6},{8,9},{9,8},{10,11... | collective-permute-start | bytes 12582920 | tf_op jit(solution)/shard_map/ppermute | solution.py:27
  101.7 23.6 %all-to-all-start.2 = ((bf16[64,16,512]{2,1,0:T(8,128)(2,1)}), bf16[64,16,512]{2,1,0:T(8,128)(2,1)S(1)}, u32[]{:S(2)}, u32[]{:S(2)}) async-start(bf16[64,16,512]{2,1,0:T(8,128)(2,1)} %bitcast.4), calls=%async_computation.2 | async-start | bytes 2097152 | tf_op jit(solution)/shard_map/all_to_all | solution.py:31
  148.9 4.3 %collective-permute-start.2 = (f32[98,512]{1,0:T(8,128)S(1)}, f32[98,512]{1,0:T(8,128)S(1)}, u32[]{:S(2)}, u32[]{:S(2)}) collective-permute-start(f32[98,512]{1,0:T(8,128)S(1)} %slice.24), channel_id=1, source_target_pairs={{0,1},{1,0},{2,3},{3,2},{4,5},{5,4},{6,7},{7,6},{8,9},{9,8},{10,11... | collective-permute-start | bytes 602120 | tf_op jit(solution)/shard_map/ppermute | solution.py:27

commit v7 on v6

--- a/solution.py
+++ b/solution.py
@@ -78,8 +78,10 @@
         total = product if total is None else total + product
     rows = total.astype(bf16)
     out_ref[...] = rows
+    rows = rows.astype(f32)
+    low = (rows * inverse_norm(rows, 1)).astype(bf16)
     for chip in range(chips):
-        parcel_ref[chip, :, :depth] = rows
+        parcel_ref[chip, :, :depth] = low
 
 
 def embedded_rows(core, features, weight, chips, cuts):
@@ -185,7 +187,7 @@
     return jnp.sum(part.T, axis=0, keepdims=True)
 
 
-def exp_kernel(early, lanes, ids_ref, x_ref, goal_ref, low_ref, exp_ref, pull_ref, emb_ref,
+def exp_kernel(early, lanes, ids_ref, x_ref, goal_ref, low_ref, exp_ref, pull_ref,
                report_ref, cos_ref, wide_ids, scaled, row_sum, total):
     i = pl.program_id(0)
     rows = low_ref.shape[0]
@@ -195,10 +197,7 @@
     @pl.when(i == 0)
     def _():
         wide_ids[...] = jnp.broadcast_to(ids_ref[...], (128, samples)).T
-        x = x_ref[...].astype(f32)
-        emb = (x * inverse_norm(x, 1)).astype(bf16)
-        emb_ref[...] = emb
-        scaled[...] = (emb * logit_scale).astype(bf16)
+        scaled[...] = (x_ref[...].astype(f32) * logit_scale).astype(bf16)
         row_sum[...] = jnp.zeros_like(row_sum)
         total[...] = jnp.zeros_like(total)
 
@@ -275,14 +274,12 @@
         out_specs=[
             pl.BlockSpec((samples, rows), lambda i: (0, i)),
             pl.BlockSpec((samples, depth), fixed),
-            pl.BlockSpec((samples, depth), fixed),
             pl.BlockSpec((chips, 1, samples + 128), lambda i: (0, 0, 0)),
             pl.BlockSpec((1, samples), fixed),
         ],
         out_shape=[
             jax.ShapeDtypeStruct((samples, count), bf16),
             jax.ShapeDtypeStruct((samples, depth), f32),
-            jax.ShapeDtypeStruct((samples, depth), bf16),
             jax.ShapeDtypeStruct((chips, 1, samples + 128), f32),
             jax.ShapeDtypeStruct((1, samples), f32),
         ],
@@ -378,7 +375,7 @@
 
 
 def settled(ids, target_cos, report, pull, goal, emb, rows=512):
-    samples, depth = emb.shape
+    samples, depth = goal.shape
     fixed = lambda i: (0, 0)
     step = lambda i: (i, 0)
     row = pl.BlockSpec((1, samples), fixed)
@@ -394,17 +391,18 @@
             pl.BlockSpec((1, report.shape[2]), fixed),
         ],
         out_shape=[
-            jax.ShapeDtypeStruct((samples, depth), bf16),
-            jax.ShapeDtypeStruct((samples, depth), bf16),
-            jax.ShapeDtypeStruct((1, samples), f32),
-            jax.ShapeDtypeStruct((1, report.shape[2]), f32),
+            pltpu.HBM((samples, depth), bf16),
+            pltpu.HBM((samples, depth), bf16),
+            pltpu.HBM((1, samples), f32),
+            pltpu.HBM((1, report.shape[2]), f32),
         ],
         scratch_shapes=[pltpu.VMEM((samples, 128), f32), pltpu.VMEM((samples, 128), f32)],
+        compiler_params=pltpu.CompilerParams(vmem_limit_bytes=24 * 1024 * 1024),
         cost_estimate=pl.CostEstimate(
             flops=8 * samples * depth, bytes_accessed=14 * samples * depth, transcendentals=0
         ),
         name="settle",
-    )(ids, target_cos, report, pull, goal, emb)
+    )(ids, target_cos, report, pltpu.with_memory_space_constraint(pull, pltpu.HBM), goal, emb)
 
 
 def push_kernel(base, final, ids_ref, patch_ref, emb_ref, exp_ref, *refs):
@@ -483,10 +481,10 @@
 
     low, goal = center_directions(ids, own, centers, other_centers)
     early = 6
-    exps, pull, emb_low, report, target_cos = exponentials(ids, x, goal, low, chips, early)
+    exps, pull, report, target_cos = exponentials(ids, x, goal, low, chips, early)
     report = to_chips(report)
     pull = pulled(exps, low, pull, early)
-    parcel, scaled, patch, report = settled(ids, target_cos, report, pull, goal, emb_low)
+    parcel, scaled, patch, report = settled(ids, target_cos, report, pull, goal, x)
     parcel = to_chips(parcel.reshape(chips, own, depth))
 
     other_push = pushed(ids, patch, scaled, exps, 1)
@@ -503,10 +501,13 @@
     grads = from_chips(grad_emb).reshape(samples, depth)
 
     fcols = wide // (2 * chips)
-    columns = x[:, depth:]
-    both = lax.dot_general(columns, grads, (((0,), (0,)), ((), ())), preferred_element_type=f32)
-    theirs_fc = swapped(both[128 : 128 + fcols])
-    grad_fc = both[:fcols] + theirs_fc
+    columns, their_columns = x[:, depth : depth + 128], x[:, depth + 128 :]
+    turned = (((0,), (0,)), ((), ()))
+    theirs_fc = lax.dot_general(their_columns, grads, turned, preferred_element_type=f32)[:fcols]
+    theirs_fc = swapped(theirs_fc)
+    own_fc = lax.dot_general(columns, grads, turned, preferred_element_type=f32)[:fcols]
+    own_fc, theirs_fc = lax.optimization_barrier((own_fc, theirs_fc))
+    grad_fc = own_fc + theirs_fc
     own_sums = lax.dynamic_slice_in_dim(report[0], chip * own, own)
     own_logits = lax.dynamic_slice_in_dim(report[0], samples + chip * own % 128, own)
     loss = jnp.log(own_sums) - own_logits

time: 167 us -> 165 us (0.988)
  blocking collectives: 21.6 us -> 0 us
  waiting for transfers between devices: 27 us -> 43 us
  starting transfers between devices: 29.9 us -> 35.1 us
    all_to_all x1 -> x0, blocking collectives: 21.6 us -> none  [from_chips(): return lax.all_to_all(copies, CHIP, split_axis=0, concat_axis=0, tiled=True)]
    all_to_all x0 -> x1, waiting for transfers between devices: none -> 15.5 us  [from_chips(): return lax.all_to_all(copies, CHIP, split_axis=0, concat_axis=0, tiled=True)]
    all_to_all x0 -> x1, starting transfers between devices: none -> 4.99 us  [from_chips(): return lax.all_to_all(copies, CHIP, split_axis=0, concat_axis=0, tiled=True)]
  transfers between devices with their start and end apart: 6 -> 7, of which waited for: 3 -> 5; matrix products, arithmetic and copies ran while one was open for 4% -> 4% of each run, Pallas kernels for 17% -> 17%
where the time goes in v7:
time: 165 us; the launch traced here: 164 us
  Pallas kernels  77.4 us (47%)
  waiting for transfers between devices  43 us (26%)
  starting transfers between devices  35.1 us (21%)
  other arithmetic  4.48 us (3%)
  local copies, waits for them, and re-layouts  3.04 us (2%)
    all_to_all x3, waiting for transfers between devices, to_chips(): return lax.all_to_all(x, CHIP, split_axis=0, concat_axis=0, tiled=True)  26.7 us
    pallas_call x1, Pallas kernels, exponentials(): pl.pallas_call(functools.partial(exp_kernel, early, lanes), grid=(count /...  24.3 us
    all_to_all x3, starting transfers between devices, to_chips(): return lax.all_to_all(x, CHIP, split_axis=0, concat_axis=0, tiled=True)  22.3 us
    pallas_call x2, Pallas kernels, pushed(): pl.pallas_call(functools.partial(push_kernel, base, final), grid=(count /...  21.4 us
    all_to_all x1, waiting for transfers between devices, from_chips(): return lax.all_to_all(copies, CHIP, split_axis=0, concat_axis=0, tiled=True)  15.5 us
    pallas_call x1, Pallas kernels, center_directions(): pl.pallas_call(functools.partial(centers_kernel, batch, rows), in_specs=[...  14.4 us
    ppermute x3, starting transfers between devices, swapped(): return lax.ppermute(x, CORE, [(0, 1), (1, 0)])  7.83 us
    pallas_call x1, Pallas kernels, embedded_rows(): pl.pallas_call(functools.partial(embed_kernel, cuts), in_specs=[SMEM, VME...  7.65 us
  transfers between devices with their start and end apart: 7, of which 5 were waited for; matrix products, arithmetic and copies ran while one was open for 4% of the time, Pallas kernels for 17%

profile of v7, /device:TPU:1, one launch (start us, length us, event | category | flops | bytes accessed | tf_op | source)
XLA Modules:
  0.0 164.5 jit_solution(1371572395389470680)
XLA Ops:
  0.6 1.5 collective-permute-start
  2.1 7.7 %embed.1 = (bf16[16,512]{1,0:T(8,128)(2,1)}, bf16[64,16,768]{2,1,0:T(8,128)(2,1)}) custom-call(s32[1]{0:T(128)} %bitcast.core_ref, bf16[16,12544]{1,0:T(8,128)(2,1)} %f_ref.1, bf16[12544,512]{1,0:T(8,128)(2,1)} %w_ref.1), custom_call_target="tpu_custom_call" | custom-call | flops 205520896 | bytes 12845056 | tf_op jit(solution)/shard_map/embed/pallas_call | solution.py:90
  9.8 0.0 copy-start.6
  9.8 11.3 %all-to-all-start = ((bf16[64,16,768]{2,1,0:T(8,128)(2,1)}), bf16[64,16,768]{2,1,0:T(8,128)(2,1)S(1)}, u32[]{:S(2)}, u32[]{:S(2)}) async-start(bf16[64,16,768]{2,1,0:T(8,128)(2,1)} %get-tuple-element.17), calls=%async_computation | async-start | bytes 3145728 | tf_op jit(solution)/shard_map/all_to_all | solution.py:31
  21.0 0.0 copy-done.6
  21.1 0.1 reshape.131
  21.2 0.5 broadcast.134
  21.7 0.8 fusion.18
  22.5 0.1 sub.32
  22.6 0.6 fusion.14.busy_ref
  23.2 0.6 and_select_fusion.1.ids_ref
  23.8 0.0 collective-permute-done.other_ref
  23.8 14.4 %targets.1 = (bf16[8192,512]{1,0:T(8,128)(2,1)}, bf16[1024,512]{1,0:T(8,128)(2,1)}) custom-call(s32[1,1024]{1,0:T(1,128)} %and_select_fusion.1.ids_ref, s32[64]{0:T(128)} %fusion.14.busy_ref, bf16[4096,512]{1,0:T(8,128)(2,1)} %refs_0_.1, bf16[4096,512]{1,0:T(8,128)(2,1)} %collective-permute-done.other_ref), custom_call_target="tpu_custom_call" | custom-call | flops 4294967296 | bytes 16777216 | tf_op jit(solution)/shard_map/targets/pallas_call | solution.py:162
  38.2 6.0 %all-to-all-done = bf16[64,16,768]{2,1,0:T(8,128)(2,1)S(1)} async-done(((bf16[64,16,768]{2,1,0:T(8,128)(2,1)}), bf16[64,16,768]{2,1,0:T(8,128)(2,1)S(1)}, u32[]{:S(2)}, u32[]{:S(2)}) %all-to-all-start) | async-done | bytes 1572896 | tf_op jit(solution)/shard_map/all_to_all | solution.py:31
  44.2 1.1 copy-done
  45.3 24.3 %exponentials.1 = (bf16[1024,8192]{1,0:T(8,128)(2,1)}, f32[1024,512]{1,0:T(8,128)}, f32[64,1,1152]{2,1,0:T(1,128)}, f32[1,1024]{1,0:T(1,128)}) custom-call(s32[1,1024]{1,0:T(1,128)} %and_select_fusion.1.ids_ref, bf16[1024,768]{1,0:T(8,128)(2,1)} %bitcast.9, bf16[1024,512]{1,0:T(8,128)(2,1)} %get-tuple-element.18.goal_ref, ...), custom_call_target="tpu_custom_call" | custom-call | flops 8589934592 | bytes 16777216 | tf_op jit(solution)/shard_map/exponentials/pallas_call | solution.py:265
  69.6 5.1 %all-to-all-start.1 = ((f32[64,1,1152]{2,1,0:T(1,128)}), f32[64,1,1152]{2,1,0:T(1,128)S(1)}, u32[]{:S(2)}, u32[]{:S(2)}) async-start(f32[64,1,1152]{2,1,0:T(1,128)} %get-tuple-element.21), calls=%async_computation.1 | async-start | bytes 589824 | tf_op jit(solution)/shard_map/all_to_all | solution.py:31
  74.8 0.0 copy-start.1
  74.8 0.0 copy-start.2
  74.8 0.0 copy-start.3
  74.8 0.0 copy-start.4
  74.8 6.5 %pull.1.pull_ref = f32[1024,512]{1,0:T(8,128)} custom-call(bf16[1024,8192]{1,0:T(8,128)(2,1)} %get-tuple-element.22.exp_ref, bf16[8192,512]{1,0:T(8,128)(2,1)} %get-tuple-element.19.low_ref, f32[1024,512]{1,0:T(8,128)} %get-tuple-element.23.start_ref), custom_call_target="tpu_custom_call" | custom-call | flops 2147483648 | bytes 6291456 | tf_op jit(solution)/shard_map/pull/pallas_call | solution.py:330
  81.3 3.1 %all-to-all-done.1.report_ref = f32[64,1,1152]{2,1,0:T(1,128)S(1)} async-done(((f32[64,1,1152]{2,1,0:T(1,128)}), f32[64,1,1152]{2,1,0:T(1,128)S(1)}, u32[]{:S(2)}, u32[]{:S(2)}) %all-to-all-start.1) | async-done | bytes 294944 | tf_op jit(solution)/shard_map/all_to_all | solution.py:31
  84.3 0.0 copy-done.1
  84.3 0.0 copy-done.2
  84.3 0.0 copy-done.3
  84.4 0.0 copy-done.4
  84.4 3.3 %settle.1 = (bf16[1024,512]{1,0:T(8,128)(2,1)}, bf16[1024,512]{1,0:T(8,128)(2,1)}, f32[1,1024]{1,0:T(1,128)}, f32[1,1152]{1,0:T(1,128)}) custom-call(s32[1,1024]{1,0:T(1,128)S(1)} %copy-done.3, f32[1,1024]{1,0:T(1,128)S(1)} %copy-done.4, f32[64,1,1152]{2,1,0:T(1,128)S(1)} %all-to-all-done.1.report_ref, f32[1024,512]{1,0:T(8,128)} %pull.1.pull_ref, ...), custom_call_target="tpu_custom_call" | custom-call | flops 4194304 | bytes 7340032 | tf_op jit(solution)/shard_map/settle/pallas_call | solution.py:382
  87.6 9.3 %shard_map.67 = bf16[4096,512]{1,0:T(8,128)(2,1)} custom-call(s32[1,1024]{1,0:T(1,128)} %and_select_fusion.1.ids_ref, f32[1,1024]{1,0:T(1,128)} %get-tuple-element.25.patch_ref, bf16[1024,512]{1,0:T(8,128)(2,1)} %get-tuple-element.26.emb_ref, bf16[1024,8192]{1,0:T(8,128)(2,1)} %get-tuple-element.22.exp_ref), custom_call_target="tpu_custom_call" | custom-call | flops 4294967296 | bytes 8388608 | tf_op jit(solution)/shard_map/pallas_call | solution.py:443
  96.9 3.3 %collective-permute-start.1 = (bf16[4096,512]{1,0:T(8,128)(2,1)}, bf16[4096,512]{1,0:T(8,128)(2,1)}, u32[]{:S(2)}, u32[]{:S(2)}) collective-permute-start(bf16[4096,512]{1,0:T(8,128)(2,1)} %shard_map.67), channel_id=1, source_target_pairs={{0,1},{1,0},{2,3},{3,2},{4,5},{5,4},{6,7},{7,6},{8,9},{9,8},{10,11... | collective-permute-start | bytes 12582920 | tf_op jit(solution)/shard_map/ppermute | solution.py:27
  100.2 5.9 %all-to-all-start.2 = ((bf16[64,16,512]{2,1,0:T(8,128)(2,1)}), bf16[64,16,512]{2,1,0:T(8,128)(2,1)S(1)}, u32[]{:S(2)}, u32[]{:S(2)}) async-start(bf16[64,16,512]{2,1,0:T(8,128)(2,1)} %bitcast.15), calls=%async_computation.2 | async-start | bytes 2097152 | tf_op jit(solution)/shard_map/all_to_all | solution.py:31
  106.1 0.0 copy-done.5
  106.1 0.1 fusion.10
  106.2 17.7 %all-to-all-done.2 = bf16[64,16,512]{2,1,0:T(8,128)(2,1)S(1)} async-done(((bf16[64,16,512]{2,1,0:T(8,128)(2,1)}), bf16[64,16,512]{2,1,0:T(8,128)(2,1)S(1)}, u32[]{:S(2)}, u32[]{:S(2)}) %all-to-all-start.2) | async-done | bytes 1048608 | tf_op jit(solution)/shard_map/all_to_all | solution.py:31
  123.9 0.2 convert_reduce_fusion
  124.1 0.2 fusion.6
  124.3 0.1 fusion.9
  124.3 1.1 broadcast_in_dim.13
  125.5 5.0 %all-to-all-start.3 = ((bf16[64,16,512]{2,1,0:T(8,128)(2,1)}), bf16[64,16,512]{2,1,0:T(8,128)(2,1)S(1)}, u32[]{:S(2)}, u32[]{:S(2)}) async-start(bf16[64,16,512]{2,1,0:T(8,128)(2,1)} %broadcast_in_dim.13), calls=%async_computation.3 | async-start | bytes 2097152 | tf_op jit(solution)/shard_map/all_to_all | solution.py:36
  130.5 1.2 subtract_bitcast_fusion
  131.7 15.5 %all-to-all-done.3 = bf16[64,16,512]{2,1,0:T(8,128)(2,1)S(1)} async-done(((bf16[64,16,512]{2,1,0:T(8,128)(2,1)}), bf16[64,16,512]{2,1,0:T(8,128)(2,1)S(1)}, u32[]{:S(2)}, u32[]{:S(2)}) %all-to-all-start.3) | async-done | bytes 1048608 | tf_op jit(solution)/shard_map/all_to_all | solution.py:36
  147.2 0.3 fusion
  147.5 3.1 %collective-permute-start.2 = (f32[98,512]{1,0:T(8,128)S(1)}, f32[98,512]{1,0:T(8,128)S(1)}, u32[]{:S(2)}, u32[]{:S(2)}) collective-permute-start(f32[98,512]{1,0:T(8,128)S(1)} %fusion), channel_id=1, source_target_pairs={{0,1},{1,0},{2,3},{3,2},{4,5},{5,4},{6,7},{7,6},{8,9},{9,8},{10,11... | collective-permute-start | bytes 602120 | tf_op jit(solution)/shard_map/ppermute | solution.py:27
  150.6 0.3 fusion.2
  150.9 0.8 collective-permute-done.2
  151.6 0.7 add.77
  152.4 0.0 collective-permute-done.1.refs_1_
  152.4 12.1 %shard_map.68 = bf16[4096,512]{1,0:T(8,128)(2,1)} custom-call(s32[1,1024]{1,0:T(1,128)} %and_select_fusion.1.ids_ref, f32[1,1024]{1,0:T(1,128)} %get-tuple-element.25.patch_ref, bf16[1024,512]{1,0:T(8,128)(2,1)} %get-tuple-element.26.emb_ref, bf16[1024,8192]{1,0:T(8,128)(2,1)} %get-tuple-element.22.exp_ref, bf16[4096,512]{1,0:T(8,128)(2,1)} %refs_0_.1, ...), custom_call_target="tpu_custom_call" | custom-call | flops 4294967296 | bytes 8388608 | tf_op jit(solution)/shard_map/pallas_call | solution.py:443
  (3 shorter events, 0.0 us)
Async XLA Ops:
  0.6 23.2 %collective-permute-start = (bf16[4096,512]{1,0:T(8,128)(2,1)}, bf16[4096,512]{1,0:T(8,128)(2,1)}, u32[]{:S(2)}, u32[]{:S(2)}) collective-permute-start(bf16[4096,512]{1,0:T(8,128)(2,1)} %refs_0_.1), channel_id=1, source_target_pairs={{0,1},{1,0},{2,3},{3,2},{4,5},{5,4},{6,7},{7,6},{8,9},{9,8},{10,11... | collective-permute-start | bytes 12582920 | tf_op jit(solution)/shard_map/ppermute | solution.py:27
  9.8 11.3 %copy-start.6 = (s32[2048]{0:T(1024)S(1)}, s32[2048]{0:T(1024)}, u32[]{:S(2)}) copy-start(s32[2048]{0:T(1024)} %param.7) | copy-start | bytes 24580
  9.8 34.4 %all-to-all-start = ((bf16[64,16,768]{2,1,0:T(8,128)(2,1)}), bf16[64,16,768]{2,1,0:T(8,128)(2,1)S(1)}, u32[]{:S(2)}, u32[]{:S(2)}) async-start(bf16[64,16,768]{2,1,0:T(8,128)(2,1)} %get-tuple-element.17), calls=%async_computation | async-start | bytes 3145728 | tf_op jit(solution)/shard_map/all_to_all | solution.py:31
  44.2 1.1 copy-start
  69.6 14.7 %all-to-all-start.1 = ((f32[64,1,1152]{2,1,0:T(1,128)}), f32[64,1,1152]{2,1,0:T(1,128)S(1)}, u32[]{:S(2)}, u32[]{:S(2)}) async-start(f32[64,1,1152]{2,1,0:T(1,128)} %get-tuple-element.21), calls=%async_computation.1 | async-start | bytes 589824 | tf_op jit(solution)/shard_map/all_to_all | solution.py:31
  74.8 9.6 %copy-start.1 = (bf16[64,16,768]{2,1,0:T(8,128)(2,1)S(1)}, bf16[64,16,768]{2,1,0:T(8,128)(2,1)}, u32[]{:S(2)}) copy-start(bf16[64,16,768]{2,1,0:T(8,128)(2,1)} %copy-done) | copy-start | bytes 4718596
  74.8 9.6 %copy-start.2 = (bf16[1024,512]{1,0:T(8,128)(2,1)S(1)}, bf16[1024,512]{1,0:T(8,128)(2,1)}, u32[]{:S(2)}) copy-start(bf16[1024,512]{1,0:T(8,128)(2,1)} %get-tuple-element.18.goal_ref) | copy-start | bytes 3145732
  74.8 9.6 %copy-start.3 = (s32[1,1024]{1,0:T(1,128)S(1)}, s32[1,1024]{1,0:T(1,128)}, u32[]{:S(2)}) copy-start(s32[1,1024]{1,0:T(1,128)} %and_select_fusion.1.ids_ref) | copy-start | bytes 12292
  74.8 9.6 %copy-start.4 = (f32[1,1024]{1,0:T(1,128)S(1)}, f32[1,1024]{1,0:T(1,128)}, u32[]{:S(2)}) copy-start(f32[1,1024]{1,0:T(1,128)} %get-tuple-element.20.cos_ref) | copy-start | bytes 12292
  96.9 9.2 %copy-start.5 = (bf16[16,512]{1,0:T(8,128)(2,1)S(1)}, bf16[16,512]{1,0:T(8,128)(2,1)}, u32[]{:S(2)}) copy-start(bf16[16,512]{1,0:T(8,128)(2,1)} %get-tuple-element.28) | copy-start | bytes 49156
  96.9 55.5 %collective-permute-start.1 = (bf16[4096,512]{1,0:T(8,128)(2,1)}, bf16[4096,512]{1,0:T(8,128)(2,1)}, u32[]{:S(2)}, u32[]{:S(2)}) collective-permute-start(bf16[4096,512]{1,0:T(8,128)(2,1)} %shard_map.67), channel_id=1, source_target_pairs={{0,1},{1,0},{2,3},{3,2},{4,5},{5,4},{6,7},{7,6},{8,9},{9,8},{10,11... | collective-permute-start | bytes 12582920 | tf_op jit(solution)/shard_map/ppermute | solution.py:27
  100.2 23.7 %all-to-all-start.2 = ((bf16[64,16,512]{2,1,0:T(8,128)(2,1)}), bf16[64,16,512]{2,1,0:T(8,128)(2,1)S(1)}, u32[]{:S(2)}, u32[]{:S(2)}) async-start(bf16[64,16,512]{2,1,0:T(8,128)(2,1)} %bitcast.15), calls=%async_computation.2 | async-start | bytes 2097152 | tf_op jit(solution)/shard_map/all_to_all | solution.py:31
  125.5 21.7 %all-to-all-start.3 = ((bf16[64,16,512]{2,1,0:T(8,128)(2,1)}), bf16[64,16,512]{2,1,0:T(8,128)(2,1)S(1)}, u32[]{:S(2)}, u32[]{:S(2)}) async-start(bf16[64,16,512]{2,1,0:T(8,128)(2,1)} %broadcast_in_dim.13), calls=%async_computation.3 | async-start | bytes 2097152 | tf_op jit(solution)/shard_map/all_to_all | solution.py:36
  147.5 4.1 %collective-permute-start.2 = (f32[98,512]{1,0:T(8,128)S(1)}, f32[98,512]{1,0:T(8,128)S(1)}, u32[]{:S(2)}, u32[]{:S(2)}) collective-permute-start(f32[98,512]{1,0:T(8,128)S(1)} %fusion), channel_id=1, source_target_pairs={{0,1},{1,0},{2,3},{3,2},{4,5},{5,4},{6,7},{7,6},{8,9},{9,8},{10,11... | collective-permute-start | bytes 602120 | tf_op jit(solution)/shard_map/ppermute | solution.py:27

commit v8 on v7

--- a/solution.py
+++ b/solution.py
@@ -21,6 +21,10 @@
 
 f32 = jnp.float32
 bf16 = jnp.bfloat16
+
+
+def in_hbm(x):
+    return pltpu.with_memory_space_constraint(x, pltpu.HBM)
 
 
 def swapped(x):
@@ -278,8 +282,8 @@
             pl.BlockSpec((1, samples), fixed),
         ],
         out_shape=[
-            jax.ShapeDtypeStruct((samples, count), bf16),
-            jax.ShapeDtypeStruct((samples, depth), f32),
+            pltpu.HBM((samples, count), bf16),
+            pltpu.HBM((samples, depth), f32),
             jax.ShapeDtypeStruct((chips, 1, samples + 128), f32),
             jax.ShapeDtypeStruct((1, samples), f32),
         ],
@@ -289,13 +293,14 @@
             pltpu.VMEM((samples, 128), f32),
             pltpu.VMEM((samples, depth), f32),
         ],
+        compiler_params=pltpu.CompilerParams(vmem_limit_bytes=40 * 1024 * 1024),
         cost_estimate=pl.CostEstimate(
             flops=2 * count * depth * samples,
             bytes_accessed=4 * count * depth,
             transcendentals=count * samples,
         ),
         name="exponentials",
-    )(ids, x, goal, low)
+    )(ids, x, in_hbm(goal), in_hbm(low))
 
 
 def pull_kernel(early, rows, exp_ref, low_ref, start_ref, out_ref, exps, lows, exp_sems, low_sems, start_sem):
@@ -402,7 +407,7 @@
             flops=8 * samples * depth, bytes_accessed=14 * samples * depth, transcendentals=0
         ),
         name="settle",
-    )(ids, target_cos, report, pltpu.with_memory_space_constraint(pull, pltpu.HBM), goal, emb)
+    )(ids, target_cos, report, in_hbm(pull), goal, emb)
 
 
 def push_kernel(base, final, ids_ref, patch_ref, emb_ref, exp_ref, *refs):

time: 165 us -> 164 us (level)
  no operation moved by 1% of the time
where the time goes in v8:
time: 164 us; the launch traced here: 163 us
  Pallas kernels  77.3 us (47%)
  waiting for transfers between devices  43 us (26%)
  starting transfers between devices  35 us (21%)
  other arithmetic  4.51 us (3%)
  local copies, waits for them, and re-layouts  1.88 us (1%)
    all_to_all x3, waiting for transfers between devices, to_chips(): return lax.all_to_all(x, CHIP, split_axis=0, concat_axis=0, tiled=True)  26.8 us
    pallas_call x1, Pallas kernels, exponentials(): pl.pallas_call(functools.partial(exp_kernel, early, lanes), grid=(count /...  24.2 us
    all_to_all x3, starting transfers between devices, to_chips(): return lax.all_to_all(x, CHIP, split_axis=0, concat_axis=0, tiled=True)  22.1 us
    pallas_call x2, Pallas kernels, pushed(): pl.pallas_call(functools.partial(push_kernel, base, final), grid=(count /...  21.4 us
    all_to_all x1, waiting for transfers between devices, from_chips(): return lax.all_to_all(copies, CHIP, split_axis=0, concat_axis=0, tiled=True)  15.5 us
    pallas_call x1, Pallas kernels, center_directions(): pl.pallas_call(functools.partial(centers_kernel, batch, rows), in_specs=[...  14.4 us
    ppermute x3, starting transfers between devices, swapped(): return lax.ppermute(x, CORE, [(0, 1), (1, 0)])  7.84 us
    pallas_call x1, Pallas kernels, embedded_rows(): pl.pallas_call(functools.partial(embed_kernel, cuts), in_specs=[SMEM, VME...  7.65 us
  transfers between devices with their start and end apart: 7, of which 5 were waited for; matrix products, arithmetic and copies ran while one was open for 4% of the time, Pallas kernels for 17%

profile of v8, /device:TPU:1, one launch (start us, length us, event | category | flops | bytes accessed | tf_op | source)
XLA Modules:
  0.0 163.1 jit_solution(8047639366565265900)
XLA Ops:
  0.6 1.5 collective-permute-start
  2.1 7.7 %embed.1 = (bf16[16,512]{1,0:T(8,128)(2,1)}, bf16[64,16,768]{2,1,0:T(8,128)(2,1)}) custom-call(s32[1]{0:T(128)} %bitcast.core_ref, bf16[16,12544]{1,0:T(8,128)(2,1)} %f_ref.1, bf16[12544,512]{1,0:T(8,128)(2,1)} %w_ref.1), custom_call_target="tpu_custom_call" | custom-call | flops 205520896 | bytes 12845056 | tf_op jit(solution)/shard_map/embed/pallas_call | solution.py:94
  9.8 0.0 copy-start.3
  9.8 11.3 %all-to-all-start = ((bf16[64,16,768]{2,1,0:T(8,128)(2,1)}), bf16[64,16,768]{2,1,0:T(8,128)(2,1)S(1)}, u32[]{:S(2)}, u32[]{:S(2)}) async-start(bf16[64,16,768]{2,1,0:T(8,128)(2,1)} %get-tuple-element.17), calls=%async_computation | async-start | bytes 3145728 | tf_op jit(solution)/shard_map/all_to_all | solution.py:35
  21.0 0.0 copy-done.3
  21.1 0.1 reshape.131
  21.2 0.5 broadcast.134
  21.7 0.8 fusion.18
  22.5 0.1 sub.32
  22.6 0.6 fusion.14.busy_ref
  23.2 0.6 and_select_fusion.1.ids_ref
  23.8 0.0 copy-start.1
  23.8 0.0 collective-permute-done.other_ref
  23.8 14.4 %targets.1 = (bf16[8192,512]{1,0:T(8,128)(2,1)}, bf16[1024,512]{1,0:T(8,128)(2,1)}) custom-call(s32[1,1024]{1,0:T(1,128)} %and_select_fusion.1.ids_ref, s32[64]{0:T(128)} %fusion.14.busy_ref, bf16[4096,512]{1,0:T(8,128)(2,1)} %refs_0_.1, bf16[4096,512]{1,0:T(8,128)(2,1)} %collective-permute-done.other_ref), custom_call_target="tpu_custom_call" | custom-call | flops 4294967296 | bytes 16777216 | tf_op jit(solution)/shard_map/targets/pallas_call | solution.py:166
  38.2 6.0 %all-to-all-done = bf16[64,16,768]{2,1,0:T(8,128)(2,1)S(1)} async-done(((bf16[64,16,768]{2,1,0:T(8,128)(2,1)}), bf16[64,16,768]{2,1,0:T(8,128)(2,1)S(1)}, u32[]{:S(2)}, u32[]{:S(2)}) %all-to-all-start) | async-done | bytes 1572896 | tf_op jit(solution)/shard_map/all_to_all | solution.py:35
  44.2 0.0 copy-done.1
  44.2 24.2 %exponentials.1 = (bf16[1024,8192]{1,0:T(8,128)(2,1)}, f32[1024,512]{1,0:T(8,128)}, f32[64,1,1152]{2,1,0:T(1,128)}, f32[1,1024]{1,0:T(1,128)S(1)}) custom-call(s32[1,1024]{1,0:T(1,128)S(1)} %copy-done.1, bf16[1024,768]{1,0:T(8,128)(2,1)S(1)} %bitcast.9, bf16[1024,512]{1,0:T(8,128)(2,1)} %get-tuple-element.18.goal_ref, ...), custom_call_target="tpu_custom_call" | custom-call | flops 8589934592 | bytes 16777216 | tf_op jit(solution)/shard_map/exponentials/pallas_call | solution.py:269
  68.4 5.1 %all-to-all-start.1 = ((f32[64,1,1152]{2,1,0:T(1,128)}), f32[64,1,1152]{2,1,0:T(1,128)S(1)}, u32[]{:S(2)}, u32[]{:S(2)}) async-start(f32[64,1,1152]{2,1,0:T(1,128)} %get-tuple-element.21), calls=%async_computation.1 | async-start | bytes 589824 | tf_op jit(solution)/shard_map/all_to_all | solution.py:35
  73.5 0.0 copy-start
  73.5 6.4 %pull.1.pull_ref = f32[1024,512]{1,0:T(8,128)} custom-call(bf16[1024,8192]{1,0:T(8,128)(2,1)} %get-tuple-element.22.exp_ref, bf16[8192,512]{1,0:T(8,128)(2,1)} %get-tuple-element.19.low_ref, f32[1024,512]{1,0:T(8,128)} %get-tuple-element.23.start_ref), custom_call_target="tpu_custom_call" | custom-call | flops 2147483648 | bytes 6291456 | tf_op jit(solution)/shard_map/pull/pallas_call | solution.py:335
  79.9 3.2 %all-to-all-done.1.report_ref = f32[64,1,1152]{2,1,0:T(1,128)S(1)} async-done(((f32[64,1,1152]{2,1,0:T(1,128)}), f32[64,1,1152]{2,1,0:T(1,128)S(1)}, u32[]{:S(2)}, u32[]{:S(2)}) %all-to-all-start.1) | async-done | bytes 294944 | tf_op jit(solution)/shard_map/all_to_all | solution.py:35
  83.1 0.0 copy-done
  83.1 3.3 %settle.1 = (bf16[1024,512]{1,0:T(8,128)(2,1)}, bf16[1024,512]{1,0:T(8,128)(2,1)}, f32[1,1024]{1,0:T(1,128)}, f32[1,1152]{1,0:T(1,128)}) custom-call(s32[1,1024]{1,0:T(1,128)S(1)} %copy-done.1, f32[1,1024]{1,0:T(1,128)S(1)} %get-tuple-element.20.cos_ref, f32[64,1,1152]{2,1,0:T(1,128)S(1)} %all-to-all-done.1.report_ref, f32[1024,512]{1,0:T(8,128)} %pull.1.pull_ref, ...), custom_call_target="tpu_custom_call" | custom-call | flops 4194304 | bytes 7340032 | tf_op jit(solution)/shard_map/settle/pallas_call | solution.py:387
  86.4 9.3 %shard_map.67 = bf16[4096,512]{1,0:T(8,128)(2,1)} custom-call(s32[1,1024]{1,0:T(1,128)} %and_select_fusion.1.ids_ref, f32[1,1024]{1,0:T(1,128)} %get-tuple-element.25.patch_ref, bf16[1024,512]{1,0:T(8,128)(2,1)} %get-tuple-element.26.emb_ref, bf16[1024,8192]{1,0:T(8,128)(2,1)} %get-tuple-element.22.exp_ref), custom_call_target="tpu_custom_call" | custom-call | flops 4294967296 | bytes 8388608 | tf_op jit(solution)/shard_map/pallas_call | solution.py:448
  95.6 0.0 copy-start.2
  95.6 3.3 %collective-permute-start.1 = (bf16[4096,512]{1,0:T(8,128)(2,1)}, bf16[4096,512]{1,0:T(8,128)(2,1)}, u32[]{:S(2)}, u32[]{:S(2)}) collective-permute-start(bf16[4096,512]{1,0:T(8,128)(2,1)} %shard_map.67), channel_id=1, source_target_pairs={{0,1},{1,0},{2,3},{3,2},{4,5},{5,4},{6,7},{7,6},{8,9},{9,8},{10,11... | collective-permute-start | bytes 12582920 | tf_op jit(solution)/shard_map/ppermute | solution.py:31
  99.0 5.8 %all-to-all-start.2 = ((bf16[64,16,512]{2,1,0:T(8,128)(2,1)}), bf16[64,16,512]{2,1,0:T(8,128)(2,1)S(1)}, u32[]{:S(2)}, u32[]{:S(2)}) async-start(bf16[64,16,512]{2,1,0:T(8,128)(2,1)} %bitcast.15), calls=%async_computation.2 | async-start | bytes 2097152 | tf_op jit(solution)/shard_map/all_to_all | solution.py:35
  104.8 0.0 copy-done.2
  104.8 0.1 fusion.10
  104.9 17.7 %all-to-all-done.2 = bf16[64,16,512]{2,1,0:T(8,128)(2,1)S(1)} async-done(((bf16[64,16,512]{2,1,0:T(8,128)(2,1)}), bf16[64,16,512]{2,1,0:T(8,128)(2,1)S(1)}, u32[]{:S(2)}, u32[]{:S(2)}) %all-to-all-start.2) | async-done | bytes 1048608 | tf_op jit(solution)/shard_map/all_to_all | solution.py:35
  122.5 0.2 convert_reduce_fusion
  122.7 0.2 fusion.6
  122.9 0.1 fusion.9
  123.0 1.1 broadcast_in_dim.13
  124.1 5.0 %all-to-all-start.3 = ((bf16[64,16,512]{2,1,0:T(8,128)(2,1)}), bf16[64,16,512]{2,1,0:T(8,128)(2,1)S(1)}, u32[]{:S(2)}, u32[]{:S(2)}) async-start(bf16[64,16,512]{2,1,0:T(8,128)(2,1)} %broadcast_in_dim.13), calls=%async_computation.3 | async-start | bytes 2097152 | tf_op jit(solution)/shard_map/all_to_all | solution.py:40
  129.1 1.2 subtract_bitcast_fusion
  130.4 15.5 %all-to-all-done.3 = bf16[64,16,512]{2,1,0:T(8,128)(2,1)S(1)} async-done(((bf16[64,16,512]{2,1,0:T(8,128)(2,1)}), bf16[64,16,512]{2,1,0:T(8,128)(2,1)S(1)}, u32[]{:S(2)}, u32[]{:S(2)}) %all-to-all-start.3) | async-done | bytes 1048608 | tf_op jit(solution)/shard_map/all_to_all | solution.py:40
  145.8 0.3 fusion
  146.1 3.1 %collective-permute-start.2 = (f32[98,512]{1,0:T(8,128)S(1)}, f32[98,512]{1,0:T(8,128)S(1)}, u32[]{:S(2)}, u32[]{:S(2)}) collective-permute-start(f32[98,512]{1,0:T(8,128)S(1)} %fusion), channel_id=1, source_target_pairs={{0,1},{1,0},{2,3},{3,2},{4,5},{5,4},{6,7},{7,6},{8,9},{9,8},{10,11... | collective-permute-start | bytes 602120 | tf_op jit(solution)/shard_map/ppermute | solution.py:31
  149.2 0.3 fusion.2
  149.5 0.8 collective-permute-done.2
  150.3 0.7 add.77
  151.0 0.0 collective-permute-done.1.refs_1_
  151.0 12.1 %shard_map.68 = bf16[4096,512]{1,0:T(8,128)(2,1)} custom-call(s32[1,1024]{1,0:T(1,128)} %and_select_fusion.1.ids_ref, f32[1,1024]{1,0:T(1,128)} %get-tuple-element.25.patch_ref, bf16[1024,512]{1,0:T(8,128)(2,1)} %get-tuple-element.26.emb_ref, bf16[1024,8192]{1,0:T(8,128)(2,1)} %get-tuple-element.22.exp_ref, bf16[4096,512]{1,0:T(8,128)(2,1)} %refs_0_.1, ...), custom_call_target="tpu_custom_call" | custom-call | flops 4294967296 | bytes 8388608 | tf_op jit(solution)/shard_map/pallas_call | solution.py:448
  (1 shorter events, 0.0 us)
Async XLA Ops:
  0.6 23.2 %collective-permute-start = (bf16[4096,512]{1,0:T(8,128)(2,1)}, bf16[4096,512]{1,0:T(8,128)(2,1)}, u32[]{:S(2)}, u32[]{:S(2)}) collective-permute-start(bf16[4096,512]{1,0:T(8,128)(2,1)} %refs_0_.1), channel_id=1, source_target_pairs={{0,1},{1,0},{2,3},{3,2},{4,5},{5,4},{6,7},{7,6},{8,9},{9,8},{10,11... | collective-permute-start | bytes 12582920 | tf_op jit(solution)/shard_map/ppermute | solution.py:31
  9.8 11.3 %copy-start.3 = (s32[2048]{0:T(1024)S(1)}, s32[2048]{0:T(1024)}, u32[]{:S(2)}) copy-start(s32[2048]{0:T(1024)} %param.7) | copy-start | bytes 24580
  9.8 34.4 %all-to-all-start = ((bf16[64,16,768]{2,1,0:T(8,128)(2,1)}), bf16[64,16,768]{2,1,0:T(8,128)(2,1)S(1)}, u32[]{:S(2)}, u32[]{:S(2)}) async-start(bf16[64,16,768]{2,1,0:T(8,128)(2,1)} %get-tuple-element.17), calls=%async_computation | async-start | bytes 3145728 | tf_op jit(solution)/shard_map/all_to_all | solution.py:35
  23.8 20.3 %copy-start.1 = (s32[1,1024]{1,0:T(1,128)S(1)}, s32[1,1024]{1,0:T(1,128)}, u32[]{:S(2)}) copy-start(s32[1,1024]{1,0:T(1,128)} %and_select_fusion.1.ids_ref) | copy-start | bytes 12292
  68.4 14.7 %all-to-all-start.1 = ((f32[64,1,1152]{2,1,0:T(1,128)}), f32[64,1,1152]{2,1,0:T(1,128)S(1)}, u32[]{:S(2)}, u32[]{:S(2)}) async-start(f32[64,1,1152]{2,1,0:T(1,128)} %get-tuple-element.21), calls=%async_computation.1 | async-start | bytes 589824 | tf_op jit(solution)/shard_map/all_to_all | solution.py:35
  73.5 9.6 %copy-start = (bf16[1024,512]{1,0:T(8,128)(2,1)S(1)}, bf16[1024,512]{1,0:T(8,128)(2,1)}, u32[]{:S(2)}) copy-start(bf16[1024,512]{1,0:T(8,128)(2,1)} %get-tuple-element.18.goal_ref) | copy-start | bytes 3145732
  95.6 9.1 %copy-start.2 = (bf16[16,512]{1,0:T(8,128)(2,1)S(1)}, bf16[16,512]{1,0:T(8,128)(2,1)}, u32[]{:S(2)}) copy-start(bf16[16,512]{1,0:T(8,128)(2,1)} %get-tuple-element.28) | copy-start | bytes 49156
  95.6 55.4 %collective-permute-start.1 = (bf16[4096,512]{1,0:T(8,128)(2,1)}, bf16[4096,512]{1,0:T(8,128)(2,1)}, u32[]{:S(2)}, u32[]{:S(2)}) collective-permute-start(bf16[4096,512]{1,0:T(8,128)(2,1)} %shard_map.67), channel_id=1, source_target_pairs={{0,1},{1,0},{2,3},{3,2},{4,5},{5,4},{6,7},{7,6},{8,9},{9,8},{10,11... | collective-permute-start | bytes 12582920 | tf_op jit(solution)/shard_map/ppermute | solution.py:31
  99.0 23.6 %all-to-all-start.2 = ((bf16[64,16,512]{2,1,0:T(8,128)(2,1)}), bf16[64,16,512]{2,1,0:T(8,128)(2,1)S(1)}, u32[]{:S(2)}, u32[]{:S(2)}) async-start(bf16[64,16,512]{2,1,0:T(8,128)(2,1)} %bitcast.15), calls=%async_computation.2 | async-start | bytes 2097152 | tf_op jit(solution)/shard_map/all_to_all | solution.py:35
  124.1 21.7 %all-to-all-start.3 = ((bf16[64,16,512]{2,1,0:T(8,128)(2,1)}), bf16[64,16,512]{2,1,0:T(8,128)(2,1)S(1)}, u32[]{:S(2)}, u32[]{:S(2)}) async-start(bf16[64,16,512]{2,1,0:T(8,128)(2,1)} %broadcast_in_dim.13), calls=%async_computation.3 | async-start | bytes 2097152 | tf_op jit(solution)/shard_map/all_to_all | solution.py:40
  146.1 4.1 %collective-permute-start.2 = (f32[98,512]{1,0:T(8,128)S(1)}, f32[98,512]{1,0:T(8,128)S(1)}, u32[]{:S(2)}, u32[]{:S(2)}) collective-permute-start(f32[98,512]{1,0:T(8,128)S(1)} %fusion), channel_id=1, source_target_pairs={{0,1},{1,0},{2,3},{3,2},{4,5},{5,4},{6,7},{7,6},{8,9},{9,8},{10,11... | collective-permute-start | bytes 602120 | tf_op jit(solution)/shard_map/ppermute | solution.py:31

commit v9 on v8

--- a/solution.py
+++ b/solution.py
@@ -33,11 +33,6 @@
 
 def to_chips(x):
     return lax.all_to_all(x, CHIP, split_axis=0, concat_axis=0, tiled=True)
-
-
-def from_chips(x):
-    copies = jnp.broadcast_to(x, (lax.axis_size(CHIP), *x.shape))
-    return lax.all_to_all(copies, CHIP, split_axis=0, concat_axis=0, tiled=True)
 
 
 def inverse_norm(values, axis):
@@ -464,6 +459,33 @@
     )(ids, patch, emb, exps, *extra)
 
 
+def own_kernel(parcel_ref, emb_ref, copies_ref):
+    chips = parcel_ref.shape[0]
+    total = parcel_ref[0].astype(f32)
+    for chip in range(1, chips):
+        total = total + parcel_ref[chip].astype(f32)
+    emb = emb_ref[...].astype(f32)
+    inv = inverse_norm(emb, 1)
+    unit = emb * inv
+    grad = ((total - unit * jnp.sum(total * unit, axis=1, keepdims=True)) * inv).astype(bf16)
+    for chip in range(chips):
+        copies_ref[chip] = grad
+
+
+def own_gradients(parcel, embedded):
+    return pl.pallas_call(
+        own_kernel,
+        in_specs=[VMEM, VMEM],
+        out_specs=VMEM,
+        out_shape=pltpu.HBM(parcel.shape, bf16),
+        compiler_params=pltpu.CompilerParams(vmem_limit_bytes=24 * 1024 * 1024),
+        cost_estimate=pl.CostEstimate(
+            flops=parcel.size, bytes_accessed=4 * parcel.size, transcendentals=0
+        ),
+        name="own",
+    )(parcel, embedded)
+
+
 def step(features, fc_weight, centers, labels):
     own, wide = features.shape
     class_rows, depth = centers.shape
@@ -496,14 +518,8 @@
     other_push = swapped(other_push)
     grad_centers = pushed(ids, patch, scaled, exps, 0, centers, other_push)
 
-    own_float = embedded.astype(f32)
-    inv_emb = inverse_norm(own_float, 1)
-    emb_dir = own_float * inv_emb
-    grad_dir = jnp.sum(parcel.astype(f32), axis=0)
-    grad_emb = (
-        (grad_dir - emb_dir * jnp.sum(grad_dir * emb_dir, axis=1, keepdims=True)) * inv_emb
-    ).astype(bf16)
-    grads = from_chips(grad_emb).reshape(samples, depth)
+    copies = own_gradients(parcel, embedded)
+    grads = to_chips(copies).reshape(samples, depth)
 
     fcols = wide // (2 * chips)
     columns, their_columns = x[:, depth : depth + 128], x[:, depth + 128 :]

time: 164 us -> 163 us (level)
  blocking collectives: 0 us -> 23.4 us
  waiting for transfers between devices: 43 us -> 25.4 us
  starting transfers between devices: 35 us -> 29.2 us
    all_to_all x0 -> x1, blocking collectives: none -> 23.4 us  [to_chips(): return lax.all_to_all(x, CHIP, split_axis=0, concat_axis=0, tiled=True)]
    all_to_all x1 -> x0, waiting for transfers between devices: 15.5 us -> none  [from_chips(): return lax.all_to_all(copies, CHIP, split_axis=0, concat_axis=0, tiled=True)]
    all_to_all x1 -> x0, starting transfers between devices: 4.99 us -> none  [from_chips(): return lax.all_to_all(copies, CHIP, split_axis=0, concat_axis=0, tiled=True)]
    all_to_all x3, waiting for transfers between devices: 26.8 us -> 24.6 us  [to_chips(): return lax.all_to_all(x, CHIP, split_axis=0, concat_axis=0, tiled=True)]
  transfers between devices with their start and end apart: 7 -> 6, of which waited for: 5 -> 4; matrix products, arithmetic and copies ran while one was open for 4% -> 3% of each run, Pallas kernels for 17% -> 18%
where the time goes in v9:
time: 163 us
  Pallas kernels  78.7 us (48%)
  starting transfers between devices  29.2 us (18%)
  waiting for transfers between devices  25.4 us (16%)
  blocking collectives  23.4 us (14%)
  other arithmetic  3.92 us (2%)
    all_to_all x3, waiting for transfers between devices, to_chips(): return lax.all_to_all(x, CHIP, split_axis=0, concat_axis=0, tiled=True)  24.6 us
    pallas_call x1, Pallas kernels, exponentials(): pl.pallas_call(functools.partial(exp_kernel, early, lanes), grid=(count /...  24.2 us
    all_to_all x1, blocking collectives, to_chips(): return lax.all_to_all(x, CHIP, split_axis=0, concat_axis=0, tiled=True)  23.4 us
    pallas_call x2, Pallas kernels, pushed(): pl.pallas_call(functools.partial(push_kernel, base, final), grid=(count /...  21.5 us
    all_to_all x3, starting transfers between devices, to_chips(): return lax.all_to_all(x, CHIP, split_axis=0, concat_axis=0, tiled=True)  21.4 us
    pallas_call x1, Pallas kernels, center_directions(): pl.pallas_call(functools.partial(centers_kernel, batch, rows), in_specs=[...  14.4 us
    ppermute x3, starting transfers between devices, swapped(): return lax.ppermute(x, CORE, [(0, 1), (1, 0)])  7.82 us
    pallas_call x1, Pallas kernels, embedded_rows(): pl.pallas_call(functools.partial(embed_kernel, cuts), in_specs=[SMEM, VME...  7.67 us
  transfers between devices with their start and end apart: 6, of which 4 were waited for; matrix products, arithmetic and copies ran while one was open for 3% of the time, Pallas kernels for 18%

profile of v9, /device:TPU:1, one launch (start us, length us, event | category | flops | bytes accessed | tf_op | source)
XLA Modules:
  0.0 162.8 jit_solution(4084193764908536437)
XLA Ops:
  0.6 1.5 collective-permute-start
  2.1 0.0 copy-start.4
  2.1 7.7 %embed.1 = (bf16[16,512]{1,0:T(8,128)(2,1)}, bf16[64,16,768]{2,1,0:T(8,128)(2,1)}) custom-call(s32[1]{0:T(128)} %bitcast.core_ref, bf16[16,12544]{1,0:T(8,128)(2,1)} %f_ref.1, bf16[12544,512]{1,0:T(8,128)(2,1)} %w_ref.1), custom_call_target="tpu_custom_call" | custom-call | flops 205520896 | bytes 12845056 | tf_op jit(solution)/shard_map/embed/pallas_call | solution.py:89
  9.8 11.3 %all-to-all-start = ((bf16[64,16,768]{2,1,0:T(8,128)(2,1)}), bf16[64,16,768]{2,1,0:T(8,128)(2,1)S(1)}, u32[]{:S(2)}, u32[]{:S(2)}) async-start(bf16[64,16,768]{2,1,0:T(8,128)(2,1)} %get-tuple-element.17), calls=%async_computation | async-start | bytes 3145728 | tf_op jit(solution)/shard_map/all_to_all | solution.py:35
  21.0 0.0 copy-done.4
  21.1 0.1 reshape.124
  21.2 0.5 broadcast.123
  21.7 0.8 fusion.11
  22.5 0.1 sub.29
  22.6 0.6 fusion.7.busy_ref
  23.2 0.6 and_select_fusion.1.ids_ref
  23.8 0.0 copy-start.1
  23.8 0.0 collective-permute-done.other_ref
  23.8 14.4 %targets.1 = (bf16[8192,512]{1,0:T(8,128)(2,1)}, bf16[1024,512]{1,0:T(8,128)(2,1)}) custom-call(s32[1,1024]{1,0:T(1,128)} %and_select_fusion.1.ids_ref, s32[64]{0:T(128)} %fusion.7.busy_ref, bf16[4096,512]{1,0:T(8,128)(2,1)} %refs_0_.1, bf16[4096,512]{1,0:T(8,128)(2,1)} %collective-permute-done.other_ref), custom_call_target="tpu_custom_call" | custom-call | flops 4294967296 | bytes 16777216 | tf_op jit(solution)/shard_map/targets/pallas_call | solution.py:161
  38.2 6.0 %all-to-all-done = bf16[64,16,768]{2,1,0:T(8,128)(2,1)S(1)} async-done(((bf16[64,16,768]{2,1,0:T(8,128)(2,1)}), bf16[64,16,768]{2,1,0:T(8,128)(2,1)S(1)}, u32[]{:S(2)}, u32[]{:S(2)}) %all-to-all-start) | async-done | bytes 1572896 | tf_op jit(solution)/shard_map/all_to_all | solution.py:35
  44.2 0.0 copy-done.1
  44.2 24.2 %exponentials.1 = (bf16[1024,8192]{1,0:T(8,128)(2,1)}, f32[1024,512]{1,0:T(8,128)}, f32[64,1,1152]{2,1,0:T(1,128)}, f32[1,1024]{1,0:T(1,128)S(1)}) custom-call(s32[1,1024]{1,0:T(1,128)S(1)} %copy-done.1, bf16[1024,768]{1,0:T(8,128)(2,1)S(1)} %bitcast.9, bf16[1024,512]{1,0:T(8,128)(2,1)} %get-tuple-element.18.goal_ref, ...), custom_call_target="tpu_custom_call" | custom-call | flops 8589934592 | bytes 16777216 | tf_op jit(solution)/shard_map/exponentials/pallas_call | solution.py:264
  68.4 5.1 %all-to-all-start.1 = ((f32[64,1,1152]{2,1,0:T(1,128)}), f32[64,1,1152]{2,1,0:T(1,128)S(1)}, u32[]{:S(2)}, u32[]{:S(2)}) async-start(f32[64,1,1152]{2,1,0:T(1,128)} %get-tuple-element.21), calls=%async_computation.1 | async-start | bytes 589824 | tf_op jit(solution)/shard_map/all_to_all | solution.py:35
  73.5 0.0 copy-start
  73.5 6.4 %pull.1.pull_ref = f32[1024,512]{1,0:T(8,128)} custom-call(bf16[1024,8192]{1,0:T(8,128)(2,1)} %get-tuple-element.22.exp_ref, bf16[8192,512]{1,0:T(8,128)(2,1)} %get-tuple-element.19.low_ref, f32[1024,512]{1,0:T(8,128)} %get-tuple-element.23.start_ref), custom_call_target="tpu_custom_call" | custom-call | flops 2147483648 | bytes 6291456 | tf_op jit(solution)/shard_map/pull/pallas_call | solution.py:330
  79.9 3.2 %all-to-all-done.1.report_ref = f32[64,1,1152]{2,1,0:T(1,128)S(1)} async-done(((f32[64,1,1152]{2,1,0:T(1,128)}), f32[64,1,1152]{2,1,0:T(1,128)S(1)}, u32[]{:S(2)}, u32[]{:S(2)}) %all-to-all-start.1) | async-done | bytes 294944 | tf_op jit(solution)/shard_map/all_to_all | solution.py:35
  83.1 0.0 copy-done
  83.1 3.3 %settle.1 = (bf16[1024,512]{1,0:T(8,128)(2,1)}, bf16[1024,512]{1,0:T(8,128)(2,1)}, f32[1,1024]{1,0:T(1,128)}, f32[1,1152]{1,0:T(1,128)}) custom-call(s32[1,1024]{1,0:T(1,128)S(1)} %copy-done.1, f32[1,1024]{1,0:T(1,128)S(1)} %get-tuple-element.20.cos_ref, f32[64,1,1152]{2,1,0:T(1,128)S(1)} %all-to-all-done.1.report_ref, f32[1024,512]{1,0:T(8,128)} %pull.1.pull_ref, ...), custom_call_target="tpu_custom_call" | custom-call | flops 4194304 | bytes 7340032 | tf_op jit(solution)/shard_map/settle/pallas_call | solution.py:382
  86.3 0.0 copy-start.3
  86.3 0.0 copy-start.2
  86.3 9.4 %shard_map.67 = bf16[4096,512]{1,0:T(8,128)(2,1)} custom-call(s32[1,1024]{1,0:T(1,128)} %and_select_fusion.1.ids_ref, f32[1,1024]{1,0:T(1,128)} %get-tuple-element.25.patch_ref, bf16[1024,512]{1,0:T(8,128)(2,1)} %get-tuple-element.26.emb_ref, bf16[1024,8192]{1,0:T(8,128)(2,1)} %get-tuple-element.22.exp_ref), custom_call_target="tpu_custom_call" | custom-call | flops 4294967296 | bytes 8388608 | tf_op jit(solution)/shard_map/pallas_call | solution.py:443
  95.7 3.3 %collective-permute-start.1 = (bf16[4096,512]{1,0:T(8,128)(2,1)}, bf16[4096,512]{1,0:T(8,128)(2,1)}, u32[]{:S(2)}, u32[]{:S(2)}) collective-permute-start(bf16[4096,512]{1,0:T(8,128)(2,1)} %shard_map.67), channel_id=1, source_target_pairs={{0,1},{1,0},{2,3},{3,2},{4,5},{5,4},{6,7},{7,6},{8,9},{9,8},{10,11... | collective-permute-start | bytes 12582920 | tf_op jit(solution)/shard_map/ppermute | solution.py:31
  99.0 0.0 copy-done.3
  99.0 23.4 %all_to_all.20.parcel_ref = bf16[64,16,512]{2,1,0:T(8,128)(2,1)S(1)} all-to-all(bf16[64,16,512]{2,1,0:T(8,128)(2,1)S(1)} %bitcast.15), channel_id=1, replica_groups=mesh['cls_0'=4,'cls_1'=4,'cls_2'=4,'cls_3'=2] {'cls_0','cls_1','cls_2'}, dimensions={0} | all-to-all | bytes 2097152 | tf_op jit(solution)/shard_map/all_to_all | solution.py:35
  122.5 0.0 copy-done.2
  122.5 1.3 own.1
  123.7 5.0 %all-to-all-start.3 = ((bf16[64,16,512]{2,1,0:T(8,128)(2,1)}), bf16[64,16,512]{2,1,0:T(8,128)(2,1)S(1)}, u32[]{:S(2)}, u32[]{:S(2)}) async-start(bf16[64,16,512]{2,1,0:T(8,128)(2,1)} %own.1), calls=%async_computation.3 | async-start | bytes 2097152 | tf_op jit(solution)/shard_map/all_to_all | solution.py:35
  128.8 1.2 subtract_bitcast_fusion
  130.0 15.5 %all-to-all-done.3 = bf16[64,16,512]{2,1,0:T(8,128)(2,1)S(1)} async-done(((bf16[64,16,512]{2,1,0:T(8,128)(2,1)}), bf16[64,16,512]{2,1,0:T(8,128)(2,1)S(1)}, u32[]{:S(2)}, u32[]{:S(2)}) %all-to-all-start.3) | async-done | bytes 1048608 | tf_op jit(solution)/shard_map/all_to_all | solution.py:35
  145.5 0.3 fusion
  145.8 3.0 %collective-permute-start.2 = (f32[98,512]{1,0:T(8,128)S(1)}, f32[98,512]{1,0:T(8,128)S(1)}, u32[]{:S(2)}, u32[]{:S(2)}) collective-permute-start(f32[98,512]{1,0:T(8,128)S(1)} %fusion), channel_id=1, source_target_pairs={{0,1},{1,0},{2,3},{3,2},{4,5},{5,4},{6,7},{7,6},{8,9},{9,8},{10,11... | collective-permute-start | bytes 602120 | tf_op jit(solution)/shard_map/ppermute | solution.py:31
  148.9 0.3 fusion.2
  149.2 0.8 collective-permute-done.2
  150.0 0.7 add.68
  150.7 0.0 collective-permute-done.1.refs_1_
  150.7 12.1 %shard_map.68 = bf16[4096,512]{1,0:T(8,128)(2,1)} custom-call(s32[1,1024]{1,0:T(1,128)} %and_select_fusion.1.ids_ref, f32[1,1024]{1,0:T(1,128)} %get-tuple-element.25.patch_ref, bf16[1024,512]{1,0:T(8,128)(2,1)} %get-tuple-element.26.emb_ref, bf16[1024,8192]{1,0:T(8,128)(2,1)} %get-tuple-element.22.exp_ref, bf16[4096,512]{1,0:T(8,128)(2,1)} %refs_0_.1, ...), custom_call_target="tpu_custom_call" | custom-call | flops 4294967296 | bytes 8388608 | tf_op jit(solution)/shard_map/pallas_call | solution.py:443
Async XLA Ops:
  0.6 23.2 %collective-permute-start = (bf16[4096,512]{1,0:T(8,128)(2,1)}, bf16[4096,512]{1,0:T(8,128)(2,1)}, u32[]{:S(2)}, u32[]{:S(2)}) collective-permute-start(bf16[4096,512]{1,0:T(8,128)(2,1)} %refs_0_.1), channel_id=1, source_target_pairs={{0,1},{1,0},{2,3},{3,2},{4,5},{5,4},{6,7},{7,6},{8,9},{9,8},{10,11... | collective-permute-start | bytes 12582920 | tf_op jit(solution)/shard_map/ppermute | solution.py:31
  2.1 19.0 %copy-start.4 = (s32[2048]{0:T(1024)S(1)}, s32[2048]{0:T(1024)}, u32[]{:S(2)}) copy-start(s32[2048]{0:T(1024)} %param.7) | copy-start | bytes 24580
  9.8 34.4 %all-to-all-start = ((bf16[64,16,768]{2,1,0:T(8,128)(2,1)}), bf16[64,16,768]{2,1,0:T(8,128)(2,1)S(1)}, u32[]{:S(2)}, u32[]{:S(2)}) async-start(bf16[64,16,768]{2,1,0:T(8,128)(2,1)} %get-tuple-element.17), calls=%async_computation | async-start | bytes 3145728 | tf_op jit(solution)/shard_map/all_to_all | solution.py:35
  23.8 20.3 %copy-start.1 = (s32[1,1024]{1,0:T(1,128)S(1)}, s32[1,1024]{1,0:T(1,128)}, u32[]{:S(2)}) copy-start(s32[1,1024]{1,0:T(1,128)} %and_select_fusion.1.ids_ref) | copy-start | bytes 12292
  68.4 14.7 %all-to-all-start.1 = ((f32[64,1,1152]{2,1,0:T(1,128)}), f32[64,1,1152]{2,1,0:T(1,128)S(1)}, u32[]{:S(2)}, u32[]{:S(2)}) async-start(f32[64,1,1152]{2,1,0:T(1,128)} %get-tuple-element.21), calls=%async_computation.1 | async-start | bytes 589824 | tf_op jit(solution)/shard_map/all_to_all | solution.py:35
  73.5 9.6 %copy-start = (bf16[1024,512]{1,0:T(8,128)(2,1)S(1)}, bf16[1024,512]{1,0:T(8,128)(2,1)}, u32[]{:S(2)}) copy-start(bf16[1024,512]{1,0:T(8,128)(2,1)} %get-tuple-element.18.goal_ref) | copy-start | bytes 3145732
  86.3 12.7 %copy-start.3 = (bf16[1024,512]{1,0:T(8,128)(2,1)S(1)}, bf16[1024,512]{1,0:T(8,128)(2,1)}, u32[]{:S(2)}) copy-start(bf16[1024,512]{1,0:T(8,128)(2,1)} %get-tuple-element.27) | copy-start | bytes 3145732
  86.3 36.1 %copy-start.2 = (bf16[16,512]{1,0:T(8,128)(2,1)S(1)}, bf16[16,512]{1,0:T(8,128)(2,1)}, u32[]{:S(2)}) copy-start(bf16[16,512]{1,0:T(8,128)(2,1)} %get-tuple-element.28.emb_ref) | copy-start | bytes 49156
  95.7 55.0 %collective-permute-start.1 = (bf16[4096,512]{1,0:T(8,128)(2,1)}, bf16[4096,512]{1,0:T(8,128)(2,1)}, u32[]{:S(2)}, u32[]{:S(2)}) collective-permute-start(bf16[4096,512]{1,0:T(8,128)(2,1)} %shard_map.67), channel_id=1, source_target_pairs={{0,1},{1,0},{2,3},{3,2},{4,5},{5,4},{6,7},{7,6},{8,9},{9,8},{10,11... | collective-permute-start | bytes 12582920 | tf_op jit(solution)/shard_map/ppermute | solution.py:31
  123.7 21.7 %all-to-all-start.3 = ((bf16[64,16,512]{2,1,0:T(8,128)(2,1)}), bf16[64,16,512]{2,1,0:T(8,128)(2,1)S(1)}, u32[]{:S(2)}, u32[]{:S(2)}) async-start(bf16[64,16,512]{2,1,0:T(8,128)(2,1)} %own.1), calls=%async_computation.3 | async-start | bytes 2097152 | tf_op jit(solution)/shard_map/all_to_all | solution.py:35
  145.8 4.1 %collective-permute-start.2 = (f32[98,512]{1,0:T(8,128)S(1)}, f32[98,512]{1,0:T(8,128)S(1)}, u32[]{:S(2)}, u32[]{:S(2)}) collective-permute-start(f32[98,512]{1,0:T(8,128)S(1)} %fusion), channel_id=1, source_target_pairs={{0,1},{1,0},{2,3},{3,2},{4,5},{5,4},{6,7},{7,6},{8,9},{9,8},{10,11... | collective-permute-start | bytes 602120 | tf_op jit(solution)/shard_map/ppermute | solution.py:31
